TPU v7x, 128 devices: a whole 4x4x4 slice. The times are simulated.
128 devices in a mesh: gx: 4 (over z), gy: 32 (over y, x, core).
Axes of the slice: x: 4, y: 4, z: 4, core: 2. Of those that a mesh axis runs over, the one named last changes fastest.
Arguments:
- a_blocks: float32 [1024, 4, 128, 128], P(('gx', 'gy')), may hold values from -0.25 to 0.25
- a_cols: int32 [1024, 4], replicated, may hold values from 0 to 1023, as said below
- t_blocks: float32 [1024, 128, 128], P(('gx', 'gy')), may hold values from -0.5 to 0.5
- t_agg: int32 [1024], replicated, may hold values from 0 to 1, as said below
- dinv: float32 [1024, 128, 128], P(('gx', 'gy')), may hold values from -0.5 to 0.5
- coarse_inv: float32 [256, 128, 128], P(('gx', 'gy')), may hold values from -1.5 to 1.5
Outputs:
- coarse: float32 [256, 14, 128, 128], P(('gx', 'gy'))
Inputs may be any that keep to these rules, and one draw needn't show every extreme that they name: `a_cols`: block column 0 of row g is g itself; column 1 lies in g's own slab; column 2 lies in the slab below (on the cycle) and column 3 in the slab above; over the rows of one slab, columns 2 name exactly 4 distinct rows of the slab below, and columns 3 exactly 4 distinct rows of the slab above. `t_agg`: every slab's 2 aggregates each hold 4 of its rows.
All inputs are finite; a program needn't handle non-finite values.
Results may differ from a plain program's by a relative error of at most 0.0001.
Values sent between devices are 32-bit elements; how exact they have to be, the bound alone decides.
No kernel may reach another device: no remote copies, remote signals or barrier semaphores. Data moves between devices by JAX's collectives and lax.ppermute only.
A program may use at most 64 MiB of HBM per device.

v0:
```python
import jax
import jax.numpy as jnp
from jax import lax
from jax.sharding import PartitionSpec as P

AGG_DEV = 2


OMEGA = 0.6


def shifted(value, axis, steps):
    count = lax.axis_size(axis)
    pairs = [(source, (source + steps) % count) for source in range(count)]
    return lax.ppermute(value, axis, pairs)


def read_list(a_cols, slab, side, rows):
    block_cols = lax.dynamic_slice_in_dim(a_cols, slab * rows, rows, 0)[:, 2 + side]
    offsets = block_cols % rows
    counter = jnp.arange(rows, dtype=jnp.int32)
    is_read = jnp.any(offsets[:, None] == counter[None, :], axis=0).astype(jnp.int32)
    ranks = jnp.cumsum(is_read) - 1
    width = rows // 2
    places = jnp.arange(width, dtype=jnp.int32)
    matched = (is_read[:, None] == 1) & (ranks[:, None] == places[None, :])
    return jnp.sum(jnp.where(matched, counter[:, None], 0), axis=0)


def place_rows(columns, lower_list, upper_list, device, devices, rows):
    slab = columns // rows
    offset = columns % rows
    lower_slab = (device + devices - 1) % devices
    width = lower_list.shape[0]
    counter = jnp.arange(width, dtype=jnp.int32)
    lower_pos = jnp.sum(jnp.where(lower_list == offset[..., None], counter, 0), axis=-1)
    upper_pos = (
        jnp.sum(jnp.where(upper_list == offset[..., None], counter, 0), axis=-1) + width + rows
    )
    own_pos = offset + width
    return jnp.where(slab == device, own_pos, jnp.where(slab == lower_slab, lower_pos, upper_pos))


def shards(a_blocks, a_cols, t_blocks, t_agg, dinv, coarse_inv):
    highest = lax.Precision.HIGHEST
    devices = lax.axis_size(("gx", "gy"))
    device = lax.axis_index(("gx", "gy"))
    rows = t_blocks.shape[0]
    previous = (device + devices - 1) % devices
    following = (device + 1) % devices
    labels = jnp.arange(a_cols.shape[0], dtype=jnp.int32) // rows * AGG_DEV + t_agg
    own_cols = lax.dynamic_slice_in_dim(a_cols, device * rows, rows, 0)
    lower_list = read_list(a_cols, device, 0, rows)
    upper_list = read_list(a_cols, device, 1, rows)
    places = place_rows(own_cols, lower_list, upper_list, device, devices, rows)
    to_upper = read_list(a_cols, following, 0, rows)
    to_lower = read_list(a_cols, previous, 1, rows)
    from_lower = shifted(t_blocks[to_upper], ("gx", "gy"), 1)
    from_upper = shifted(t_blocks[to_lower], ("gx", "gy"), -1)
    t_extended = jnp.concatenate([from_lower, t_blocks, from_upper], axis=0)
    t_cols = t_extended[places]
    prod_at = jnp.einsum("rkab,rkbc->rkac", a_blocks, t_cols, precision=highest)
    smoothed = jnp.einsum("rab,rkbc->rkac", dinv, prod_at, precision=highest)
    first = (jnp.arange(a_blocks.shape[1]) == 0).astype(jnp.float32)
    prolong = first[None, :, None, None] * t_blocks[:, None] - OMEGA * smoothed
    p_lower = shifted(prolong[to_upper], ("gx", "gy"), 1)
    p_upper = shifted(prolong[to_lower], ("gx", "gy"), -1)
    p_extended = jnp.concatenate([p_lower, prolong, p_upper], axis=0)
    near_labels = labels[own_cols]
    far_labels = labels[a_cols[own_cols]]
    columns_near = 5 * AGG_DEV
    column_ids = jnp.arange(columns_near, dtype=jnp.int32)
    block = t_blocks.shape[1]

    def accumulate(row, buffer):
        a_row = lax.dynamic_index_in_dim(a_blocks, row, 0, keepdims=False)
        gathered = p_extended[places[row]]
        partial_value = jnp.einsum("kab,kqbc->kqac", a_row, gathered, precision=highest)
        far = far_labels[row]
        far_column = (far // AGG_DEV - device + 2) % devices * AGG_DEV + far % AGG_DEV
        picker = (far_column[..., None] == column_ids).astype(jnp.float32)
        grouped = jnp.einsum("kqn,kqac->nac", picker, partial_value, precision=highest)
        p_row = lax.dynamic_index_in_dim(prolong, row, 0, keepdims=False)
        contrib = jnp.einsum("pba,nbc->pnac", p_row, grouped, precision=highest)
        near = near_labels[row]
        near_slab = (near // AGG_DEV - device + 1) % devices
        target = near_slab * AGG_DEV + near % AGG_DEV
        slot = ((column_ids // AGG_DEV)[None, :] - near_slab[:, None] + 2) * AGG_DEV + (
            column_ids % AGG_DEV
        )[None, :]
        target_all = jnp.broadcast_to(target[:, None], slot.shape)
        return buffer.at[target_all, slot].add(contrib)

    buffer = jnp.zeros((3 * AGG_DEV, 7 * AGG_DEV, block, block), jnp.float32)
    buffer = lax.fori_loop(0, rows, accumulate, buffer)
    from_next = shifted(buffer[:AGG_DEV], ("gx", "gy"), -1)
    from_prev = shifted(buffer[2 * AGG_DEV :], ("gx", "gy"), 1)
    galerkin = buffer[AGG_DEV : 2 * AGG_DEV] + from_next + from_prev
    return jnp.einsum("aij,asjk->asik", coarse_inv, galerkin, precision=highest)


def solution(mesh):
    placed = (
        P(("gx", "gy"), None, None, None),
        P(),
        P(("gx", "gy"), None, None),
        P(),
        P(("gx", "gy"), None, None),
        P(("gx", "gy"), None, None),
    )
    return jax.shard_map(
        shards,
        mesh=mesh,
        in_specs=placed,
        out_specs=P(("gx", "gy"), None, None, None),
        check_vma=False,
    )
```

profile of v0, /device:TPU:0, one launch (start us, length us, event | category | flops | bytes accessed | tf_op | source)
XLA Modules:
  0.0 301.6 jit_solution(2429179025924841675)
XLA Ops:
  5.1 8.3 %collective-permute-start.1 = (f32[4,128,128]{2,1,0:T(8,128)S(1)}, f32[4,128,128]{2,1,0:T(8,128)}, u32[]{:S(2)}, u32[]{:S(2)}) collective-permute-start(f32[4,128,128]{2,1,0:T(8,128)S(1)} %gather_fusion.5), channel_id=1, source_target_pairs={{0,127},{1,0},{2,1},{3,2},{4,3},{5,4},{6,5},{7,6},{8,7},{9,8},{10,... | collective-permute-start | bytes 786440 | tf_op jit(solution)/shard_map/ppermute | solution.py:15
  20.3 5.7 %fusion.73 = f32[8,4,128,128]{3,2,1,0:T(8,128)S(1)} fusion(f32[8,4,128,128]{3,2,1,0:T(8,128)} %bitcast.155, f32[8,4,128,128]{3,2,1,0:T(8,128)} %param.8), kind=kOutput, calls=%fused_computation.177 | convolution fusion | flops 805306368 | bytes 6291456 | tf_op jit(solution)/shard_map/rkab,rkbc->rkac/dot_general | solution.py:62
  31.4 7.4 %collective-permute-start.3 = (f32[4,4,128,128]{2,3,1,0:T(8,128)}, f32[4,4,128,128]{2,3,1,0:T(8,128)}, u32[]{:S(2)}, u32[]{:S(2)}) collective-permute-start(f32[4,4,128,128]{2,3,1,0:T(8,128)} %gather_fusion.8), channel_id=1, source_target_pairs={{0,127},{1,0},{2,1},{3,2},{4,3},{5,4},{6,5},{7,6},{8,7},{9,8},{10,... | collective-permute-start | bytes 3145736 | tf_op jit(solution)/shard_map/ppermute | solution.py:15
  42.2 9.4 %collective-permute-done.2 = f32[4,4,128,128]{2,3,1,0:T(8,128)} collective-permute-done((f32[4,4,128,128]{2,3,1,0:T(8,128)}, f32[4,4,128,128]{2,3,1,0:T(8,128)}, u32[]{:S(2)}, u32[]{:S(2)}) %collective-permute-start.2) | collective-permute-done | bytes 1048608 | tf_op jit(solution)/shard_map/ppermute | solution.py:15
  51.6 3.9 %pad_maximum_fusion = f32[16,4,128,128]{2,3,1,0:T(8,128)} fusion(f32[4,4,128,128]{2,3,1,0:T(8,128)} %collective-permute-done.3, f32[8,4,128,128]{2,3,1,0:T(8,128)S(1)} %bitcast_subtract_fusion, f32[4,4,128,128]{2,3,1,0:T(8,128)} %collective-permute-done.2), kind=kLoop, calls=%fused_computation.76 | loop fusion | flops 2097152 | bytes 8388608 | tf_op jit(solution)/shard_map/concatenate | solution.py:68
  55.5 5.4 %copy.42 = f32[16,4,128,128]{3,2,1,0:T(8,128)} copy(f32[16,4,128,128]{2,3,1,0:T(8,128)} %pad_maximum_fusion) | data formatting | bytes 8388608
  60.9 3.1 %broadcast_in_dim.132 = f32[6,14,128,128]{3,2,1,0:T(8,128)} broadcast(f32[]{:T(128)} %constant.343.clone.1), dimensions={} | broadcast | bytes 5505028 | tf_op jit(solution)/shard_map/broadcast_in_dim | solution.py:94
  64.0 193.5 %while.19 = (s32[]{:T(128)}, f32[6,14,128,128]{3,2,1,0:T(8,128)}, s32[8,4]{1,0:T(8,128)S(1)}, s32[]{:T(128)}, s32[8,4,4]{2,1,0:T(4,128)S(1)}, /*index=5*/s32[8,4...) while((s32[]{:T(128)}, f32[6,14,128,128]{3,2,1,0:T(8,128)}, ...), condition=%wide.region_16.17_spmd.clone.clone, body=%wide.region_14.16_spmd.clone.clone.sunk | while | flops 1441401472 | bytes 41686536 | solution.py:95
  65.4 2.8 gather_fusion
  72.5 3.2 %convolution_bitcast_fusion.8 = f32[4,10,128,128]{2,3,0,1:T(8,128)S(1)} fusion(f32[10,128,128,1]{2,0,1,3:T(8,128)S(1)} %convolution_bitcast_fusion.7, f32[8,4,128,128]{2,3,1,0:T(8,128)} %copy-done.1, s32[]{:T(128)S(6)} %copy.69), kind=kOutput, calls=%fused_computation.14.clone.1 | convolution fusion | flops 1006632960 | bytes 3538948 | tf_op jit(solution)/shard_map/while/body/eval_jaxpr/pba,nbc->pnac/dot_general | solution.py:84
  77.8 10.5 %scatter_fusion = f32[6,14,128,128]{3,2,1,0:T(8,128)} fusion(f32[6,14,128,128]{3,2,1,0:T(8,128)} %get-tuple-element.569, s32[40]{0:T(128)S(1)} %reshape.694, f32[40,128,128]{2,1,0:T(8,128)} %bitcast.154), kind=kCustom, calls=%fused_computation.9.clone.clone.1 | custom fusion | flops 655360 | bytes 7864640 | tf_op jit(solution)/shard_map/while/body/eval_jaxpr/scatter-add | solution.py:92
  96.7 3.2 %convolution_bitcast_fusion.8 = f32[4,10,128,128]{2,3,0,1:T(8,128)S(1)} fusion(f32[10,128,128,1]{2,0,1,3:T(8,128)S(1)} %convolution_bitcast_fusion.7, f32[8,4,128,128]{2,3,1,0:T(8,128)} %copy-done.1, s32[]{:T(128)S(6)} %copy.69), kind=kOutput, calls=%fused_computation.14.clone.1 | convolution fusion | flops 1006632960 | bytes 3538948 | tf_op jit(solution)/shard_map/while/body/eval_jaxpr/pba,nbc->pnac/dot_general | solution.py:84
  102.0 10.3 %scatter_fusion = f32[6,14,128,128]{3,2,1,0:T(8,128)} fusion(f32[6,14,128,128]{3,2,1,0:T(8,128)} %get-tuple-element.569, s32[40]{0:T(128)S(1)} %reshape.694, f32[40,128,128]{2,1,0:T(8,128)} %bitcast.154), kind=kCustom, calls=%fused_computation.9.clone.clone.1 | custom fusion | flops 655360 | bytes 7864640 | tf_op jit(solution)/shard_map/while/body/eval_jaxpr/scatter-add | solution.py:92
  113.8 2.8 gather_fusion
  120.9 3.2 %convolution_bitcast_fusion.8 = f32[4,10,128,128]{2,3,0,1:T(8,128)S(1)} fusion(f32[10,128,128,1]{2,0,1,3:T(8,128)S(1)} %convolution_bitcast_fusion.7, f32[8,4,128,128]{2,3,1,0:T(8,128)} %copy-done.1, s32[]{:T(128)S(6)} %copy.69), kind=kOutput, calls=%fused_computation.14.clone.1 | convolution fusion | flops 1006632960 | bytes 3538948 | tf_op jit(solution)/shard_map/while/body/eval_jaxpr/pba,nbc->pnac/dot_general | solution.py:84
  126.2 10.4 %scatter_fusion = f32[6,14,128,128]{3,2,1,0:T(8,128)} fusion(f32[6,14,128,128]{3,2,1,0:T(8,128)} %get-tuple-element.569, s32[40]{0:T(128)S(1)} %reshape.694, f32[40,128,128]{2,1,0:T(8,128)} %bitcast.154), kind=kCustom, calls=%fused_computation.9.clone.clone.1 | custom fusion | flops 655360 | bytes 7864640 | tf_op jit(solution)/shard_map/while/body/eval_jaxpr/scatter-add | solution.py:92
  138.0 2.8 gather_fusion
  145.1 3.2 %convolution_bitcast_fusion.8 = f32[4,10,128,128]{2,3,0,1:T(8,128)S(1)} fusion(f32[10,128,128,1]{2,0,1,3:T(8,128)S(1)} %convolution_bitcast_fusion.7, f32[8,4,128,128]{2,3,1,0:T(8,128)} %copy-done.1, s32[]{:T(128)S(6)} %copy.69), kind=kOutput, calls=%fused_computation.14.clone.1 | convolution fusion | flops 1006632960 | bytes 3538948 | tf_op jit(solution)/shard_map/while/body/eval_jaxpr/pba,nbc->pnac/dot_general | solution.py:84
  150.4 10.4 %scatter_fusion = f32[6,14,128,128]{3,2,1,0:T(8,128)} fusion(f32[6,14,128,128]{3,2,1,0:T(8,128)} %get-tuple-element.569, s32[40]{0:T(128)S(1)} %reshape.694, f32[40,128,128]{2,1,0:T(8,128)} %bitcast.154), kind=kCustom, calls=%fused_computation.9.clone.clone.1 | custom fusion | flops 655360 | bytes 7864640 | tf_op jit(solution)/shard_map/while/body/eval_jaxpr/scatter-add | solution.py:92
  169.2 3.2 %convolution_bitcast_fusion.8 = f32[4,10,128,128]{2,3,0,1:T(8,128)S(1)} fusion(f32[10,128,128,1]{2,0,1,3:T(8,128)S(1)} %convolution_bitcast_fusion.7, f32[8,4,128,128]{2,3,1,0:T(8,128)} %copy-done.1, s32[]{:T(128)S(6)} %copy.69), kind=kOutput, calls=%fused_computation.14.clone.1 | convolution fusion | flops 1006632960 | bytes 3538948 | tf_op jit(solution)/shard_map/while/body/eval_jaxpr/pba,nbc->pnac/dot_general | solution.py:84
  174.6 10.4 %scatter_fusion = f32[6,14,128,128]{3,2,1,0:T(8,128)} fusion(f32[6,14,128,128]{3,2,1,0:T(8,128)} %get-tuple-element.569, s32[40]{0:T(128)S(1)} %reshape.694, f32[40,128,128]{2,1,0:T(8,128)} %bitcast.154), kind=kCustom, calls=%fused_computation.9.clone.clone.1 | custom fusion | flops 655360 | bytes 7864640 | tf_op jit(solution)/shard_map/while/body/eval_jaxpr/scatter-add | solution.py:92
  193.4 3.2 %convolution_bitcast_fusion.8 = f32[4,10,128,128]{2,3,0,1:T(8,128)S(1)} fusion(f32[10,128,128,1]{2,0,1,3:T(8,128)S(1)} %convolution_bitcast_fusion.7, f32[8,4,128,128]{2,3,1,0:T(8,128)} %copy-done.1, s32[]{:T(128)S(6)} %copy.69), kind=kOutput, calls=%fused_computation.14.clone.1 | convolution fusion | flops 1006632960 | bytes 3538948 | tf_op jit(solution)/shard_map/while/body/eval_jaxpr/pba,nbc->pnac/dot_general | solution.py:84
  198.7 10.4 %scatter_fusion = f32[6,14,128,128]{3,2,1,0:T(8,128)} fusion(f32[6,14,128,128]{3,2,1,0:T(8,128)} %get-tuple-element.569, s32[40]{0:T(128)S(1)} %reshape.694, f32[40,128,128]{2,1,0:T(8,128)} %bitcast.154), kind=kCustom, calls=%fused_computation.9.clone.clone.1 | custom fusion | flops 655360 | bytes 7864640 | tf_op jit(solution)/shard_map/while/body/eval_jaxpr/scatter-add | solution.py:92
  210.5 2.8 gather_fusion
  217.6 3.2 %convolution_bitcast_fusion.8 = f32[4,10,128,128]{2,3,0,1:T(8,128)S(1)} fusion(f32[10,128,128,1]{2,0,1,3:T(8,128)S(1)} %convolution_bitcast_fusion.7, f32[8,4,128,128]{2,3,1,0:T(8,128)} %copy-done.1, s32[]{:T(128)S(6)} %copy.69), kind=kOutput, calls=%fused_computation.14.clone.1 | convolution fusion | flops 1006632960 | bytes 3538948 | tf_op jit(solution)/shard_map/while/body/eval_jaxpr/pba,nbc->pnac/dot_general | solution.py:84
  222.9 10.4 %scatter_fusion = f32[6,14,128,128]{3,2,1,0:T(8,128)} fusion(f32[6,14,128,128]{3,2,1,0:T(8,128)} %get-tuple-element.569, s32[40]{0:T(128)S(1)} %reshape.694, f32[40,128,128]{2,1,0:T(8,128)} %bitcast.154), kind=kCustom, calls=%fused_computation.9.clone.clone.1 | custom fusion | flops 655360 | bytes 7864640 | tf_op jit(solution)/shard_map/while/body/eval_jaxpr/scatter-add | solution.py:92
  241.8 3.2 %convolution_bitcast_fusion.8 = f32[4,10,128,128]{2,3,0,1:T(8,128)S(1)} fusion(f32[10,128,128,1]{2,0,1,3:T(8,128)S(1)} %convolution_bitcast_fusion.7, f32[8,4,128,128]{2,3,1,0:T(8,128)} %copy-done.1, s32[]{:T(128)S(6)} %copy.69), kind=kOutput, calls=%fused_computation.14.clone.1 | convolution fusion | flops 1006632960 | bytes 3538948 | tf_op jit(solution)/shard_map/while/body/eval_jaxpr/pba,nbc->pnac/dot_general | solution.py:84
  247.1 10.4 %scatter_fusion = f32[6,14,128,128]{3,2,1,0:T(8,128)} fusion(f32[6,14,128,128]{3,2,1,0:T(8,128)} %get-tuple-element.569, s32[40]{0:T(128)S(1)} %reshape.694, f32[40,128,128]{2,1,0:T(8,128)} %bitcast.154), kind=kCustom, calls=%fused_computation.9.clone.clone.1 | custom fusion | flops 655360 | bytes 7864640 | tf_op jit(solution)/shard_map/while/body/eval_jaxpr/scatter-add | solution.py:92
  260.0 7.2 %collective-permute-start.4 = (f32[2,14,128,128]{3,2,1,0:T(8,128)S(1)}, f32[2,14,128,128]{3,2,1,0:T(8,128)S(1)}, u32[]{:S(2)}, u32[]{:S(2)}) collective-permute-start(f32[2,14,128,128]{3,2,1,0:T(8,128)S(1)} %get-tuple-element.477), channel_id=1, source_target_pairs={{0,127},{1,0},{2,1},{3,2},{4,3},{5,4},{6,5},{7,6},{8,7},{9,8},{10,... | collective-permute-start | bytes 5505032 | tf_op jit(solution)/shard_map/ppermute | solution.py:15
  267.2 20.7 %collective-permute-done.4 = f32[2,14,128,128]{3,2,1,0:T(8,128)S(1)} collective-permute-done((f32[2,14,128,128]{3,2,1,0:T(8,128)S(1)}, f32[2,14,128,128]{3,2,1,0:T(8,128)S(1)}, u32[]{:S(2)}, u32[]{:S(2)}) %collective-permute-start.4) | collective-permute-done | bytes 1835040 | tf_op jit(solution)/shard_map/ppermute | solution.py:15
  287.9 7.3 %collective-permute-done.5 = f32[2,14,128,128]{3,2,1,0:T(8,128)S(1)} collective-permute-done((f32[2,14,128,128]{3,2,1,0:T(8,128)S(1)}, f32[2,14,128,128]{3,2,1,0:T(8,128)S(1)}, u32[]{:S(2)}, u32[]{:S(2)}) %collective-permute-start.5) | collective-permute-done | bytes 1835040 | tf_op jit(solution)/shard_map/ppermute | solution.py:15
  295.3 4.6 %fusion.42 = f32[2,14,128,128]{2,3,1,0:T(8,128)S(1)} fusion(f32[2,14,128,128]{3,2,1,0:T(8,128)S(1)} %collective-permute-done.5, f32[2,14,128,128]{3,2,1,0:T(8,128)S(1)} %collective-permute-done.4, f32[6,14,128,128]{3,2,1,0:T(8,128)} %get-tuple-element.366, f32[2,128,128]{2,1,0:T(8,128)S(1)} %copy-done.4), kind=kOutput, calls=%fused_computation.84 | convolution fusion | flops 705560576 | bytes 7471104 | tf_op jit(solution)/shard_map/aij,asjk->asik/dot_general | solution.py:99
  (207 shorter events, 97.6 us)
Async XLA Ops:
  0.0 26.0 %copy-start = (f32[8,128,128]{2,1,0:T(8,128)S(1)}, f32[8,128,128]{2,1,0:T(8,128)}, u32[]{:S(2)}) copy-start(f32[8,128,128]{2,1,0:T(8,128)} %param.12) | copy-start | bytes 1572868
  0.0 17.3 %copy-start.3 = (f32[8,128,128]{2,1,0:T(8,128)S(1)}, f32[8,128,128]{2,1,0:T(8,128)}, u32[]{:S(2)}) copy-start(f32[8,128,128]{2,1,0:T(8,128)} %param.10) | copy-start | bytes 1572868
  2.9 12.8 %collective-permute-start = (f32[4,128,128]{2,1,0:T(8,128)S(1)}, f32[4,128,128]{2,1,0:T(8,128)S(1)}, u32[]{:S(2)}, u32[]{:S(2)}) collective-permute-start(f32[4,128,128]{2,1,0:T(8,128)S(1)} %gather_fusion.4), channel_id=1, source_target_pairs={{0,1},{1,2},{2,3},{3,4},{4,5},{5,6},{6,7},{7,8},{8,9},{9,10},{10,1... | collective-permute-start | bytes 786440 | tf_op jit(solution)/shard_map/ppermute | solution.py:15
  5.1 12.2 %collective-permute-start.1 = (f32[4,128,128]{2,1,0:T(8,128)S(1)}, f32[4,128,128]{2,1,0:T(8,128)}, u32[]{:S(2)}, u32[]{:S(2)}) collective-permute-start(f32[4,128,128]{2,1,0:T(8,128)S(1)} %gather_fusion.5), channel_id=1, source_target_pairs={{0,127},{1,0},{2,1},{3,2},{4,3},{5,4},{6,5},{7,6},{8,7},{9,8},{10,... | collective-permute-start | bytes 786440 | tf_op jit(solution)/shard_map/ppermute | solution.py:15
  28.2 10.7 %copy-start.5 = (s32[1024,4]{0,1:T(4,128)S(1)}, s32[1024,4]{0,1:T(4,128)}, u32[]{:S(2)}) copy-start(s32[1024,4]{0,1:T(4,128)} %param.9) | copy-start | bytes 49156
  28.2 11.1 %copy-start.6 = (s32[1024]{0:T(1024)S(1)}, s32[1024]{0:T(1024)}, u32[]{:S(2)}) copy-start(s32[1024]{0:T(1024)} %param.11) | copy-start | bytes 12292
  31.4 20.2 %collective-permute-start.2 = (f32[4,4,128,128]{2,3,1,0:T(8,128)}, f32[4,4,128,128]{2,3,1,0:T(8,128)}, u32[]{:S(2)}, u32[]{:S(2)}) collective-permute-start(f32[4,4,128,128]{2,3,1,0:T(8,128)} %gather_fusion.7), channel_id=1, source_target_pairs={{0,1},{1,2},{2,3},{3,4},{4,5},{5,6},{6,7},{7,8},{8,9},{9,10},{10,1... | collective-permute-start | bytes 3145736 | tf_op jit(solution)/shard_map/ppermute | solution.py:15
  31.4 20.2 %collective-permute-start.3 = (f32[4,4,128,128]{2,3,1,0:T(8,128)}, f32[4,4,128,128]{2,3,1,0:T(8,128)}, u32[]{:S(2)}, u32[]{:S(2)}) collective-permute-start(f32[4,4,128,128]{2,3,1,0:T(8,128)} %gather_fusion.8), channel_id=1, source_target_pairs={{0,127},{1,0},{2,1},{3,2},{4,3},{5,4},{6,5},{7,6},{8,7},{9,8},{10,... | collective-permute-start | bytes 3145736 | tf_op jit(solution)/shard_map/ppermute | solution.py:15
  64.0 1.4 copy-start.1
  77.8 10.5 %copy-start.2 = (f32[8,4,128,128]{2,3,1,0:T(8,128)S(1)}, f32[8,4,128,128]{2,3,1,0:T(8,128)}, u32[]{:S(2)}) copy-start(f32[8,4,128,128]{2,3,1,0:T(8,128)} %copy-done.1) | copy-start | bytes 6291460 | tf_op jit(solution)/shard_map/while
  88.2 1.4 copy-start.1
  102.0 10.4 %copy-start.2 = (f32[8,4,128,128]{2,3,1,0:T(8,128)S(1)}, f32[8,4,128,128]{2,3,1,0:T(8,128)}, u32[]{:S(2)}) copy-start(f32[8,4,128,128]{2,3,1,0:T(8,128)} %copy-done.1) | copy-start | bytes 6291460 | tf_op jit(solution)/shard_map/while
  112.4 1.4 copy-start.1
  126.2 10.4 %copy-start.2 = (f32[8,4,128,128]{2,3,1,0:T(8,128)S(1)}, f32[8,4,128,128]{2,3,1,0:T(8,128)}, u32[]{:S(2)}) copy-start(f32[8,4,128,128]{2,3,1,0:T(8,128)} %copy-done.1) | copy-start | bytes 6291460 | tf_op jit(solution)/shard_map/while
  136.6 1.4 copy-start.1
  150.4 10.4 %copy-start.2 = (f32[8,4,128,128]{2,3,1,0:T(8,128)S(1)}, f32[8,4,128,128]{2,3,1,0:T(8,128)}, u32[]{:S(2)}) copy-start(f32[8,4,128,128]{2,3,1,0:T(8,128)} %copy-done.1) | copy-start | bytes 6291460 | tf_op jit(solution)/shard_map/while
  160.8 1.4 copy-start.1
  174.6 10.4 %copy-start.2 = (f32[8,4,128,128]{2,3,1,0:T(8,128)S(1)}, f32[8,4,128,128]{2,3,1,0:T(8,128)}, u32[]{:S(2)}) copy-start(f32[8,4,128,128]{2,3,1,0:T(8,128)} %copy-done.1) | copy-start | bytes 6291460 | tf_op jit(solution)/shard_map/while
  184.9 1.4 copy-start.1
  198.7 10.4 %copy-start.2 = (f32[8,4,128,128]{2,3,1,0:T(8,128)S(1)}, f32[8,4,128,128]{2,3,1,0:T(8,128)}, u32[]{:S(2)}) copy-start(f32[8,4,128,128]{2,3,1,0:T(8,128)} %copy-done.1) | copy-start | bytes 6291460 | tf_op jit(solution)/shard_map/while
  209.1 1.4 copy-start.1
  222.9 10.4 %copy-start.2 = (f32[8,4,128,128]{2,3,1,0:T(8,128)S(1)}, f32[8,4,128,128]{2,3,1,0:T(8,128)}, u32[]{:S(2)}) copy-start(f32[8,4,128,128]{2,3,1,0:T(8,128)} %copy-done.1) | copy-start | bytes 6291460 | tf_op jit(solution)/shard_map/while
  233.3 1.4 copy-start.1
  247.1 10.4 %copy-start.2 = (f32[8,4,128,128]{2,3,1,0:T(8,128)S(1)}, f32[8,4,128,128]{2,3,1,0:T(8,128)}, u32[]{:S(2)}) copy-start(f32[8,4,128,128]{2,3,1,0:T(8,128)} %copy-done.1) | copy-start | bytes 6291460 | tf_op jit(solution)/shard_map/while
  257.4 37.8 %copy-start.4 = (f32[2,128,128]{2,1,0:T(8,128)S(1)}, f32[2,128,128]{2,1,0:T(8,128)}, u32[]{:S(2)}) copy-start(f32[2,128,128]{2,1,0:T(8,128)} %param.13) | copy-start | bytes 393220
  260.0 28.0 %collective-permute-start.4 = (f32[2,14,128,128]{3,2,1,0:T(8,128)S(1)}, f32[2,14,128,128]{3,2,1,0:T(8,128)S(1)}, u32[]{:S(2)}, u32[]{:S(2)}) collective-permute-start(f32[2,14,128,128]{3,2,1,0:T(8,128)S(1)} %get-tuple-element.477), channel_id=1, source_target_pairs={{0,127},{1,0},{2,1},{3,2},{4,3},{5,4},{6,5},{7,6},{8,7},{9,8},{10,... | collective-permute-start | bytes 5505032 | tf_op jit(solution)/shard_map/ppermute | solution.py:15
  267.2 28.1 %collective-permute-start.5 = (f32[2,14,128,128]{3,2,1,0:T(8,128)S(1)}, f32[2,14,128,128]{3,2,1,0:T(8,128)S(1)}, u32[]{:S(2)}, u32[]{:S(2)}) collective-permute-start(f32[2,14,128,128]{3,2,1,0:T(8,128)S(1)} %get-tuple-element.478), channel_id=1, source_target_pairs={{0,1},{1,2},{2,3},{3,4},{4,5},{5,6},{6,7},{7,8},{8,9},{9,10},{10,1... | collective-permute-start | bytes 5505032 | tf_op jit(solution)/shard_map/ppermute | solution.py:15
where the time goes:
time: 303 us; the launch traced here: 302 us
  other arithmetic  91.9 us (30%)
  local copies, waits for them, and re-layouts  79 us (26%)
  matrix products  67.9 us (22%)
  waiting for transfers between devices  39.1 us (13%)
  starting transfers between devices  23.1 us (8%)
    scatter-add x8, other arithmetic, accumulate(): return buffer.at[target_all, slot].add(contrib)  83.1 us
    ppermute x6, waiting for transfers between devices, shifted(): return lax.ppermute(value, axis, pairs)  39.1 us
    dot_general x8, matrix products, accumulate(): contrib = jnp.einsum('pba,nbc->pnac', p_row, grouped, precision=highest)  25.9 us
    ppermute x6, starting transfers between devices, shifted(): return lax.ppermute(value, axis, pairs)  23.1 us
    gather x8, local copies, waits for them, and re-layouts, accumulate(): gathered = p_extended[places[row]]  22.4 us
    dot_general x8, matrix products, accumulate(): jnp.einsum('kab,kqbc->kqac', a_row, gathered, precision=highest)  22.2 us
    transpose x8, local copies, waits for them, and re-layouts, accumulate(): contrib = jnp.einsum('pba,nbc->pnac', p_row, grouped, precision=highest)  16.6 us
    while x32, local copies, waits for them, and re-layouts  8.93 us
  transfers between devices with their start and end apart: 6, of which 4 were waited for; matrix products, arithmetic and copies ran while one was open for 3% of the time, Pallas kernels for 0%

commit v1 on v0

v1 whole, which is shorter than its diff:
```python
import functools

import jax
import jax.numpy as jnp
from jax import lax
from jax.experimental import pallas as pl
from jax.experimental.pallas import tpu as pltpu
from jax.sharding import PartitionSpec as P

OMEGA = 0.6
AXES = ("gx", "gy")
F32 = jnp.float32
BF16 = jnp.bfloat16
COL1, POS2, POS3, UP_LIST, LO_LIST, OWN_LAB, LOW_LAB, UPP_LAB, TAB = 0, 8, 16, 24, 28, 32, 64, 80, 128


def shifted(value, steps):
    count = lax.axis_size(AXES)
    pairs = [(source, (source + steps) % count) for source in range(count)]
    return lax.ppermute(value, AXES, pairs)


def split(x):
    high = x.astype(BF16)
    return high, (x - high.astype(F32)).astype(BF16)


def dot(a, b):
    return jnp.dot(a, b, preferred_element_type=F32)


def dot3(a_high, a_low, b_high, b_low):
    return dot(a_high, b_high) + dot(a_low, b_high) + dot(a_high, b_low)


def dot3k(a_high, a_low, b_high, b_low):
    both = jnp.concatenate([a_high, a_low], axis=1)
    return dot(both, jnp.concatenate([b_high, b_high], axis=0)) + dot(a_high, b_low)


def table_kernel(devices, cols, agg, t, tab, t_up, t_lo):
    rows, width = t.shape[0], t.shape[0] // 2
    minor = devices // lax.axis_size("gx")
    device = lax.axis_index("gx") * minor + lax.axis_index("gy")
    previous = lax.rem(device + devices - 1, devices)
    following = lax.rem(device + 1, devices)

    def col(row, k):
        return cols[(row >> 7) * 512 + k * 128 + (row & 127)]

    def read_mask(slab, k):
        mask = jnp.int32(0)
        for r in range(rows):
            mask = mask | (jnp.int32(1) << (col(slab * rows + r, k) & (rows - 1)))
        return mask

    def ranks(mask):
        found, rank = [], jnp.int32(0)
        for r in range(rows):
            found.append(rank)
            rank = rank + ((mask >> r) & 1)
        return found

    def listed(mask):
        found = ranks(mask)
        result = []
        for j in range(width):
            value = jnp.int32(0)
            for r in range(rows):
                hit = ((mask >> r) & 1) * (found[r] == j).astype(jnp.int32)
                value = value + hit * r
            result.append(value)
        return result

    def count_below(mask, offset):
        below = mask & ((jnp.int32(1) << offset) - 1)
        total = jnp.int32(0)
        for r in range(rows):
            total = total + ((below >> r) & 1)
        return total

    up_list = listed(read_mask(following, 2))
    lo_list = listed(read_mask(previous, 3))
    for j in range(width):
        tab[UP_LIST + j] = up_list[j]
        tab[LO_LIST + j] = lo_list[j]
        t_up[j] = t[up_list[j]]
        t_lo[j] = t[lo_list[j]]
    lower_mask, upper_mask = read_mask(device, 2), read_mask(device, 3)
    for r in range(rows):
        row = device * rows + r
        tab[COL1 + r] = col(row, 1) & (rows - 1)
        tab[POS2 + r] = count_below(lower_mask, col(row, 2) & (rows - 1))
        tab[POS3 + r] = count_below(upper_mask, col(row, 3) & (rows - 1))
        for k in range(4):
            tab[OWN_LAB + 4 * r + k] = agg[col(row, k)]
    lower_list, upper_list = listed(lower_mask), listed(upper_mask)
    for j in range(width):
        for k in range(4):
            tab[LOW_LAB + 4 * j + k] = agg[col(previous * rows + lower_list[j], k)]
            tab[UPP_LAB + 4 * j + k] = agg[col(following * rows + upper_list[j], k)]


def put(value, label, column):
    return jnp.where(label == column, value, jnp.zeros_like(value))


def two_columns(value, label):
    return jnp.concatenate([put(value, label, 0), put(value, label, 1)], axis=1)


def near_kernel(tab, a, t, dinv, own_high, own_low, trans_high, trans_low, near_up, near_lo, t_high, t_low, tile):
    rows, block = t.shape[0], t.shape[1]
    for r in range(rows):
        t_high[r], t_low[r] = split(t[r])
    for r in range(rows):
        near = tab[COL1 + r]
        a0 = split(a[r, 0])
        a1 = split(a[r, 1])
        prod = jnp.concatenate(
            [dot3k(*a0, t_high[r], t_low[r]), dot3k(*a1, t_high[near], t_low[near])], axis=1
        )
        smoothed = dot3k(*split(dinv[r]), *split(prod))
        p0 = t[r] - OMEGA * smoothed[:, :block]
        p1 = -OMEGA * smoothed[:, block:]
        label0, label1 = tab[OWN_LAB + 4 * r], tab[OWN_LAB + 4 * r + 1]
        both = two_columns(p0, label0) + two_columns(p1, label1)
        tile[r] = both
        own_high[r], own_low[r] = split(both)
        turned = both.T
        trans_high[:, r * block : (r + 1) * block], trans_low[:, r * block : (r + 1) * block] = split(turned)
    for j in range(rows // 2):
        near_up[j] = tile[tab[UP_LIST + j]]
        near_lo[j] = tile[tab[LO_LIST + j]]


def far_kernel(
    tab, a, dinv, t_below, t_above,
    below_high, below_low, above_high, above_low, trans_high, trans_low, far_up, far_lo,
    tb_high, tb_low, ta_high, ta_low, tile,
):
    rows, block = dinv.shape[0], dinv.shape[1]
    for j in range(rows // 2):
        tb_high[j], tb_low[j] = split(t_below[j])
        ta_high[j], ta_low[j] = split(t_above[j])
    for r in range(rows):
        below, above = tab[POS2 + r], tab[POS3 + r]
        prod = jnp.concatenate(
            [
                dot3k(*split(a[r, 2]), tb_high[below], tb_low[below]),
                dot3k(*split(a[r, 3]), ta_high[above], ta_low[above]),
            ],
            axis=1,
        )
        both = -OMEGA * dot3k(*split(dinv[r]), *split(prod))
        tile[r] = both
        left = two_columns(both[:, :block], tab[OWN_LAB + 4 * r + 2])
        right = two_columns(both[:, block:], tab[OWN_LAB + 4 * r + 3])
        below_high[r], below_low[r] = split(left)
        above_high[r], above_low[r] = split(right)
        place = slice(r * block, (r + 1) * block)
        trans_high[: 2 * block, place], trans_low[: 2 * block, place] = split(left.T)
        trans_high[2 * block :, place], trans_low[2 * block :, place] = split(right.T)
    for j in range(rows // 2):
        far_up[j] = tile[tab[UP_LIST + j]]
        far_lo[j] = tile[tab[LO_LIST + j]]


def wide(ref, *places):
    return jnp.concatenate([ref[place] for place in places], axis=0)


def first_kernel(
    tab, a, below_high, below_low, above_high, above_low, trans_high, trans_low, near_below, near_above,
    ap_high, ap_low, to_lower, to_upper,
    nb_high, nb_low, na_high, na_low,
):
    rows, block = a.shape[0], a.shape[2]
    for j in range(rows // 2):
        nb_high[j], nb_low[j] = split(near_below[j])
        na_high[j], na_low[j] = split(near_above[j])
    for r in range(rows):
        near, pos2, pos3 = tab[COL1 + r], tab[POS2 + r], tab[POS3 + r]
        a01 = split(jnp.concatenate([a[r, 0], a[r, 1]], axis=1))
        a2, a3 = split(a[r, 2]), split(a[r, 3])
        low = dot3(*a01, wide(below_high, r, near), wide(below_low, r, near)) + dot3k(*a2, nb_high[pos2], nb_low[pos2])
        upp = dot3(*a01, wide(above_high, r, near), wide(above_low, r, near)) + dot3k(*a3, na_high[pos3], na_low[pos3])
        place = slice(r * block, (r + 1) * block)
        ap_high[place, : 2 * block], ap_low[place, : 2 * block] = split(low)
        ap_high[place, 2 * block :], ap_low[place, 2 * block :] = split(upp)
    half = 2 * block
    for side, out in ((0, to_lower), (1, to_upper)):
        lhs = trans_high[side * half : (side + 1) * half], trans_low[side * half : (side + 1) * half]
        for c in range(2):
            cols = slice(c * half, (c + 1) * half)
            out[:, cols] = dot3(*lhs, ap_high[:, cols], ap_low[:, cols])


def second_kernel(
    tab, a, own_high, own_low, trans_high, trans_low, far_below, far_above,
    ap_high, ap_low, to_lower, to_upper,
    fb_high, fb_low, fa_high, fa_low,
):
    rows, block = a.shape[0], a.shape[2]
    half = 2 * block
    for j in range(rows // 2):
        low, upp = LOW_LAB + 4 * j, UPP_LAB + 4 * j
        fb_high[j], fb_low[j] = split(
            jnp.concatenate(
                [two_columns(far_below[j][:, :block], tab[low + 2]), two_columns(far_below[j][:, block:], tab[low + 3])],
                axis=1,
            )
        )
        fa_high[j], fa_low[j] = split(
            jnp.concatenate(
                [two_columns(far_above[j][:, :block], tab[upp + 2]), two_columns(far_above[j][:, block:], tab[upp + 3])],
                axis=1,
            )
        )
    for r in range(rows):
        near, pos2, pos3 = tab[COL1 + r], tab[POS2 + r], tab[POS3 + r]
        a01 = split(jnp.concatenate([a[r, 0], a[r, 1]], axis=1))
        a2, a3 = split(a[r, 2]), split(a[r, 3])
        left = dot3k(*a2, fb_high[pos2], fb_low[pos2])
        right = dot3k(*a3, fa_high[pos3], fa_low[pos3])
        own = dot3(*a01, wide(own_high, r, near), wide(own_low, r, near)) + left[:, half:] + right[:, :half]
        place = slice(r * block, (r + 1) * block)
        ap_high[place, :half], ap_low[place, :half] = split(left[:, :half])
        ap_high[place, half : 2 * half], ap_low[place, half : 2 * half] = split(own)
        ap_high[place, 2 * half :], ap_low[place, 2 * half :] = split(right[:, half:])
    for side, out in ((0, to_lower), (1, to_upper)):
        lhs = trans_high[side * half : (side + 1) * half], trans_low[side * half : (side + 1) * half]
        for c in range(3):
            cols = slice(c * half, (c + 1) * half)
            out[:, cols] = dot3(*lhs, ap_high[:, cols], ap_low[:, cols])


def own_kernel(trans_high, trans_low, ap1_high, ap1_low, ap2_high, ap2_low, own):
    half = trans_high.shape[0]
    lhs = trans_high[...], trans_low[...]
    for d, (high, low, c) in enumerate(
        ((ap2_high, ap2_low, 0), (ap1_high, ap1_low, 0), (ap2_high, ap2_low, 1), (ap1_high, ap1_low, 1), (ap2_high, ap2_low, 2))
    ):
        cols = slice(c * half, (c + 1) * half)
        own[:, d * half : (d + 1) * half] = dot3(*lhs, high[:, cols], low[:, cols])


def last_kernel(inverse, own, next1, next2, prev1, prev2, out):
    block = inverse.shape[1]
    half = 2 * block
    held = ((1, 0), (0, 0), (1, 1), (0, 1), (1, 2))
    for agg in range(2):
        inv = split(inverse[agg])
        line = slice(agg * block, (agg + 1) * block)
        for d in range(-3, 4):
            total = None
            if -2 <= d <= 2:
                total = own[line, (d + 2) * half : (d + 3) * half]
            for shift, bufs in ((1, (next1, next2)), (-1, (prev1, prev2))):
                if -2 <= d - shift <= 2:
                    which, c = held[d - shift + 2]
                    part = bufs[which][line, c * half : (c + 1) * half]
                    total = part if total is None else total + part
            result = dot3k(*inv, *split(total))
            out[agg, 2 * (d + 3)] = result[:, :block]
            out[agg, 2 * (d + 3) + 1] = result[:, block:]


def call(body, outs, ins, scratch=(), name=None, flops=0):
    smem = pl.BlockSpec(memory_space=pltpu.SMEM)
    vmem = pl.BlockSpec(memory_space=pltpu.VMEM)

    def spec(x):
        return smem if x.dtype == jnp.int32 else vmem

    return pl.pallas_call(
        body,
        out_shape=outs,
        in_specs=[spec(x) for x in ins],
        out_specs=jax.tree.map(spec, outs),
        scratch_shapes=[pltpu.VMEM(shape, dtype) for shape, dtype in scratch],
        compiler_params=pltpu.CompilerParams(vmem_limit_bytes=24 * 2**20),
        cost_estimate=pl.CostEstimate(flops=flops, bytes_accessed=2**20, transcendentals=0),
        name=name,
    )(*ins)


def shards(a_blocks, a_cols, t_blocks, t_agg, dinv, coarse_inv):
    devices = lax.axis_size(AXES)
    rows, block = t_blocks.shape[:2]
    width, half, deep = rows // 2, 2 * block, rows * block
    shape = jax.ShapeDtypeStruct
    pair = lambda *dims: [shape(dims, BF16), shape(dims, BF16)]
    cols = a_cols.reshape(-1, 128, 4).transpose(0, 2, 1).reshape(-1)
    product = 2 * block**3 * 3

    tab, t_up, t_lo = call(
        functools.partial(table_kernel, devices),
        [shape((TAB,), jnp.int32), shape((width, block, block), F32), shape((width, block, block), F32)],
        [cols, t_agg, t_blocks],
        name="table",
    )
    t_below = shifted(t_up, 1)
    t_above = shifted(t_lo, -1)
    own_high, own_low, pt_high, pt_low, near_up, near_lo = call(
        near_kernel,
        pair(rows, block, half) + pair(half, deep) + [shape((width, block, half), F32)] * 2,
        [tab, a_blocks, t_blocks, dinv],
        [((rows, block, block), BF16)] * 2 + [((rows, block, half), F32)],
        name="near",
        flops=32 * product,
    )
    near_below = shifted(near_up, 1)
    near_above = shifted(near_lo, -1)
    below_high, below_low, above_high, above_low, side_high, side_low, far_up, far_lo = call(
        far_kernel,
        pair(rows, block, half) * 2 + pair(2 * half, deep) + [shape((width, block, half), F32)] * 2,
        [tab, a_blocks, dinv, t_below, t_above],
        [((width, block, block), BF16)] * 4 + [((rows, block, half), F32)],
        name="far",
        flops=32 * product,
    )
    far_below = shifted(far_up, 1)
    far_above = shifted(far_lo, -1)
    ap1_high, ap1_low, lower1, upper1 = call(
        first_kernel,
        pair(deep, 2 * half) + [shape((half, 2 * half), F32)] * 2,
        [tab, a_blocks, below_high, below_low, above_high, above_low, side_high, side_low, near_below, near_above],
        [((width, block, half), BF16)] * 4,
        name="first",
        flops=200 * product,
    )
    next1 = shifted(lower1, -1)
    prev1 = shifted(upper1, 1)
    ap2_high, ap2_low, lower2, upper2 = call(
        second_kernel,
        pair(deep, 3 * half) + [shape((half, 3 * half), F32)] * 2,
        [tab, a_blocks, own_high, own_low, side_high, side_low, far_below, far_above],
        [((width, block, 2 * half), BF16)] * 4,
        name="second",
        flops=250 * product,
    )
    next2 = shifted(lower2, -1)
    prev2 = shifted(upper2, 1)
    (own,) = call(
        own_kernel,
        [shape((half, 5 * half), F32)],
        [pt_high, pt_low, ap1_high, ap1_low, ap2_high, ap2_low],
        name="own",
        flops=160 * product,
    )
    (out,) = call(
        last_kernel,
        [shape((2, 14, block, block), F32)],
        [coarse_inv, own, next1, next2, prev1, prev2],
        name="last",
        flops=28 * product,
    )
    return out


def solution(mesh):
    placed = (
        P(AXES, None, None, None),
        P(),
        P(AXES, None, None),
        P(),
        P(AXES, None, None),
        P(AXES, None, None),
    )
    return jax.shard_map(
        shards,
        mesh=mesh,
        in_specs=placed,
        out_specs=P(AXES, None, None, None),
        check_vma=False,
    )
```

time: 303 us -> 76.5 us (0.25)
  other arithmetic: 91.9 us -> 0 us
  local copies, waits for them, and re-layouts: 79 us -> 5.09 us
  matrix products: 67.9 us -> 0 us
  waiting for transfers between devices: 39.1 us -> 15.8 us
  Pallas kernels: 0 us -> 20.7 us
  starting transfers between devices: 23.1 us -> 34.4 us
    scatter-add x8 -> x0, other arithmetic: 83.1 us -> none  [accumulate(): return buffer.at[target_all, slot].add(contrib)]
    dot_general x27 -> x0, matrix products: 67.9 us -> none  [the longest x8 25.9 us: accumulate(): contrib = jnp.einsum('pba,nbc->pnac', p_row, grouped, precision=highest)]
    gather x19 -> x0, local copies, waits for them, and re-layouts: 33.4 us -> none  [the longest x8 22.4 us: accumulate(): gathered = p_extended[places[row]]]
    ppermute x6 -> x10, waiting for transfers between devices: 39.1 us -> 15.8 us  [shifted(): return lax.ppermute(value, AXES, pairs)]
    transpose x17 -> x0, local copies, waits for them, and re-layouts: 22.9 us -> none  [the longest x8 16.6 us: accumulate(): contrib = jnp.einsum('pba,nbc->pnac', p_row, grouped, precision=highest)]
    pallas_call x0 -> x7, Pallas kernels: none -> 20.7 us  [call(): pl.pallas_call(body, out_shape=outs, in_specs=[spec(x) for x in ins], out...]
    ppermute x6 -> x10, starting transfers between devices: 23.1 us -> 34.4 us  [shifted(): return lax.ppermute(value, AXES, pairs)]
    while x32 -> x0, local copies, waits for them, and re-layouts: 8.93 us -> none
  transfers between devices with their start and end apart: 6 -> 10, of which waited for: 4 -> 3; matrix products, arithmetic and copies ran while one was open for 3% -> 0% of each run, Pallas kernels for 0% -> 18%
where the time goes in v1:
time: 76.5 us; the launch traced here: 76.1 us
  starting transfers between devices  34.4 us (45%)
  Pallas kernels  20.7 us (27%)
  waiting for transfers between devices  15.8 us (21%)
  local copies, waits for them, and re-layouts  5.09 us (7%)
    ppermute x10, starting transfers between devices, shifted(): return lax.ppermute(value, AXES, pairs)  34.4 us
    pallas_call x7, Pallas kernels, call(): pl.pallas_call(body, out_shape=outs, in_specs=[spec(x) for x in ins], out...  20.7 us
    ppermute x10, waiting for transfers between devices, shifted(): return lax.ppermute(value, AXES, pairs)  15.8 us
    unnamed x16, local copies, waits for them, and re-layouts  5.09 us
  transfers between devices with their start and end apart: 10, of which 3 were waited for; matrix products, arithmetic and copies ran while one was open for 0% of the time, Pallas kernels for 18%

profile of v1, /device:TPU:0, one launch (start us, length us, event | category | flops | bytes accessed | tf_op | source)
XLA Modules:
  0.0 76.1 jit_solution(480563424190747998)
XLA Ops:
  0.0 1.0 %copy-done.2 = f32[8,128,128]{2,1,0:T(8,128)S(1)} copy-done((f32[8,128,128]{2,1,0:T(8,128)S(1)}, f32[8,128,128]{2,1,0:T(8,128)}, u32[]{:S(2)}) %copy-start.2) | copy-done | bytes 524312
  1.0 0.7 copy-done.6
  1.8 0.7 copy-done.7
  2.4 2.0 %table.1 = (s32[128]{0:T(128)S(1)}, f32[4,128,128]{2,1,0:T(8,128)S(1)}, f32[4,128,128]{2,1,0:T(8,128)S(1)}) custom-call(s32[4096]{0:T(1024)S(1)} %bitcast.5, s32[1024]{0:T(1024)S(1)} %copy-done.7, f32[8,128,128]{2,1,0:T(8,128)S(1)} %copy-done.2), custom_call_target="tpu_custom_call" | custom-call | bytes 1048576 | tf_op jit(solution)/shard_map/table/pallas_call | solution.py:276
  4.5 0.1 collective-permute-start
  4.6 8.3 %collective-permute-start.1 = (f32[4,128,128]{2,1,0:T(8,128)S(1)}, f32[4,128,128]{2,1,0:T(8,128)S(1)}, u32[]{:S(2)}, u32[]{:S(2)}) collective-permute-start(f32[4,128,128]{2,1,0:T(8,128)S(1)} %get-tuple-element.34), channel_id=1, source_target_pairs={{0,127},{1,0},{2,1},{3,2},{4,3},{5,4},{6,5},{7,6},{8,7},{9,8},{10,... | collective-permute-start | bytes 786440 | tf_op jit(solution)/shard_map/ppermute | solution.py:20
  12.9 4.0 %collective-permute-done.t_below = f32[4,128,128]{2,1,0:T(8,128)S(1)} collective-permute-done((f32[4,128,128]{2,1,0:T(8,128)S(1)}, f32[4,128,128]{2,1,0:T(8,128)S(1)}, u32[]{:S(2)}, u32[]{:S(2)}) %collective-permute-start) | collective-permute-done | bytes 262176 | tf_op jit(solution)/shard_map/ppermute | solution.py:20
  16.8 0.0 collective-permute-done.1.t_above
  16.8 1.6 %copy-done = f32[8,4,128,128]{3,2,1,0:T(8,128)S(1)} copy-done((f32[8,4,128,128]{3,2,1,0:T(8,128)S(1)}, f32[8,4,128,128]{3,2,1,0:T(8,128)}, u32[]{:S(2)}) %copy-start) | copy-done | bytes 2097176
  18.4 1.0 %copy-done.4 = f32[8,128,128]{2,1,0:T(8,128)S(1)} copy-done((f32[8,128,128]{2,1,0:T(8,128)S(1)}, f32[8,128,128]{2,1,0:T(8,128)}, u32[]{:S(2)}) %copy-start.4) | copy-done | bytes 524312
  19.5 2.8 %far.1 = (bf16[8,128,256]{2,1,0:T(8,128)(2,1)S(1)}, bf16[8,128,256]{2,1,0:T(8,128)(2,1)S(1)}, bf16[8,128,256]{2,1,0:T(8,128)(2,1)S(1)}, bf16[8,128,256]{2,1,0:T(...) custom-call(s32[128]{0:T(128)S(1)} %get-tuple-element.30.tab, ...), custom_call_target="tpu_custom_call" | custom-call | flops 402653184 | bytes 1048576 | tf_op jit(solution)/shard_map/far/pallas_call | solution.py:276
  22.3 0.1 collective-permute-start.4
  22.3 7.3 %collective-permute-start.5 = (f32[4,128,256]{2,1,0:T(8,128)S(1)}, f32[4,128,256]{2,1,0:T(8,128)S(1)}, u32[]{:S(2)}, u32[]{:S(2)}) collective-permute-start(f32[4,128,256]{2,1,0:T(8,128)S(1)} %get-tuple-element.48), channel_id=1, source_target_pairs={{0,127},{1,0},{2,1},{3,2},{4,3},{5,4},{6,5},{7,6},{8,7},{9,8},{10,... | collective-permute-start | bytes 1572872 | tf_op jit(solution)/shard_map/ppermute | solution.py:20
  29.7 2.6 %near.1 = (bf16[8,128,256]{2,1,0:T(8,128)(2,1)S(1)}, bf16[8,128,256]{2,1,0:T(8,128)(2,1)S(1)}, bf16[256,1024]{1,0:T(8,128)(2,1)S(1)}, bf16[256,1024]{1,0:T(8,128...) custom-call(s32[128]{0:T(128)S(1)} %get-tuple-element.30.tab, f32[8,4,128,128]{3,2,1,0:T(8,128)S(1)} %copy-done.1, ...), custom_call_target="tpu_custom_call" | custom-call | flops 402653184 | bytes 1048576 | tf_op jit(solution)/shard_map/near/pallas_call | solution.py:276
  32.3 0.1 collective-permute-start.2
  32.4 7.2 %collective-permute-start.3 = (f32[4,128,256]{2,1,0:T(8,128)S(1)}, f32[4,128,256]{2,1,0:T(8,128)S(1)}, u32[]{:S(2)}, u32[]{:S(2)}) collective-permute-start(f32[4,128,256]{2,1,0:T(8,128)S(1)} %get-tuple-element.42), channel_id=1, source_target_pairs={{0,127},{1,0},{2,1},{3,2},{4,3},{5,4},{6,5},{7,6},{8,7},{9,8},{10,... | collective-permute-start | bytes 1572872 | tf_op jit(solution)/shard_map/ppermute | solution.py:20
  39.5 0.0 collective-permute-done.4.far_below
  39.5 0.0 collective-permute-done.5.far_above
  39.5 5.2 %second.1 = (bf16[1024,768]{1,0:T(8,128)(2,1)S(1)}, bf16[1024,768]{1,0:T(8,128)(2,1)S(1)}, f32[256,768]{1,0:T(8,128)S(1)}, f32[256,768]{1,0:T(8,128)S(1)}) custom-call(s32[128]{0:T(128)S(1)} %get-tuple-element.30.tab, f32[8,4,128,128]{3,2,1,0:T(8,128)S(1)} %copy-done.1, bf16[8,128,256]{2,1,0:T(8,128)(2,1)S(1)} %get-tuple-element.45.own_high, ...), custom_call_target="tpu_custom_call" | custom-call | flops 3145728000 | bytes 1048576 | tf_op jit(solution)/shard_map/second/pallas_call | solution.py:276
  44.8 4.2 %collective-permute-start.7 = (f32[256,768]{1,0:T(8,128)S(1)}, f32[256,768]{1,0:T(8,128)S(1)}, u32[]{:S(2)}, u32[]{:S(2)}) collective-permute-start(f32[256,768]{1,0:T(8,128)S(1)} %get-tuple-element.52), channel_id=1, source_target_pairs={{0,127},{1,0},{2,1},{3,2},{4,3},{5,4},{6,5},{7,6},{8,7},{9,8},{10,... | collective-permute-start | bytes 2359304 | tf_op jit(solution)/shard_map/ppermute | solution.py:20
  49.0 0.0 collective-permute-start.9
  49.0 0.0 collective-permute-done.2.near_below
  49.0 0.0 collective-permute-done.3.near_above
  49.0 3.9 %first.1 = (bf16[1024,512]{1,0:T(8,128)(2,1)S(1)}, bf16[1024,512]{1,0:T(8,128)(2,1)S(1)}, f32[256,512]{1,0:T(8,128)S(1)}, f32[256,512]{1,0:T(8,128)S(1)}) custom-call(s32[128]{0:T(128)S(1)} %get-tuple-element.30.tab, f32[8,4,128,128]{3,2,1,0:T(8,128)S(1)} %copy-done.1, bf16[8,128,256]{2,1,0:T(8,128)(2,1)S(1)} %get-tuple-element.35.below_high, ...), custom_call_target="tpu_custom_call" | custom-call | flops 2516582400 | bytes 1048576 | tf_op jit(solution)/shard_map/first/pallas_call | solution.py:276
  52.9 7.2 %collective-permute-start.6 = (f32[256,512]{1,0:T(8,128)S(1)}, f32[256,512]{1,0:T(8,128)S(1)}, u32[]{:S(2)}, u32[]{:S(2)}) collective-permute-start(f32[256,512]{1,0:T(8,128)S(1)} %get-tuple-element.51), channel_id=1, source_target_pairs={{0,127},{1,0},{2,1},{3,2},{4,3},{5,4},{6,5},{7,6},{8,7},{9,8},{10,... | collective-permute-start | bytes 1572872 | tf_op jit(solution)/shard_map/ppermute | solution.py:20
  60.2 0.0 collective-permute-start.8
  60.2 2.2 %own.1 = f32[256,1280]{1,0:T(8,128)S(1)} custom-call(bf16[256,1024]{1,0:T(8,128)(2,1)S(1)} %get-tuple-element.31.trans_high, bf16[256,1024]{1,0:T(8,128)(2,1)S(1)} %get-tuple-element.32.trans_low, bf16[1024,512]{1,0:T(8,128)(2,1)S(1)} %get-tuple-element.43.ap1_high, bf16[1024,512]{1,0:T(8,128)(2,1)S(1)} %get-tuple-element.44.ap1_low, ...), custom_call_target="tpu_custom_call" | custom-call | flops 2013265920 | bytes 1048576 | tf_op jit(solution)/shard_map/own/pallas_call | solution.py:276
  62.4 4.5 %collective-permute-done.6.next1 = f32[256,512]{1,0:T(8,128)S(1)} collective-permute-done((f32[256,512]{1,0:T(8,128)S(1)}, f32[256,512]{1,0:T(8,128)S(1)}, u32[]{:S(2)}, u32[]{:S(2)}) %collective-permute-start.6) | collective-permute-done | bytes 524320 | tf_op jit(solution)/shard_map/ppermute | solution.py:20
  66.9 7.3 %collective-permute-done.8.prev1 = f32[256,512]{1,0:T(8,128)S(1)} collective-permute-done((f32[256,512]{1,0:T(8,128)S(1)}, f32[256,512]{1,0:T(8,128)S(1)}, u32[]{:S(2)}, u32[]{:S(2)}) %collective-permute-start.8) | collective-permute-done | bytes 524320 | tf_op jit(solution)/shard_map/ppermute | solution.py:20
  74.2 0.0 collective-permute-done.7.next2
  74.2 0.0 collective-permute-done.9.prev2
  74.2 1.9 %last.1 = f32[2,14,128,128]{3,2,1,0:T(8,128)} custom-call(f32[2,128,128]{2,1,0:T(8,128)S(1)} %copy-done.5, f32[256,1280]{1,0:T(8,128)S(1)} %own.1, f32[256,512]{1,0:T(8,128)S(1)} %collective-permute-done.6.next1, f32[256,768]{1,0:T(8,128)S(1)} %collective-permute-done.7.next2, f32[256,512]{1,0:T(8,128)S(1)} %collective-permute-done.8.prev1, ...), custom_call_target="tpu_custom_call" | custom-call | flops 352321536 | bytes 1048576 | tf_op jit(solution)/shard_map/last/pallas_call | solution.py:276
  (11 shorter events, 0.0 us)
Async XLA Ops:
  0.0 1.0 %copy-start.2 = (f32[8,128,128]{2,1,0:T(8,128)S(1)}, f32[8,128,128]{2,1,0:T(8,128)}, u32[]{:S(2)}) copy-start(f32[8,128,128]{2,1,0:T(8,128)} %t.3) | copy-start | bytes 1572868
  1.0 0.7 copy-start.6
  1.8 0.7 copy-start.7
  4.5 12.4 %collective-permute-start = (f32[4,128,128]{2,1,0:T(8,128)S(1)}, f32[4,128,128]{2,1,0:T(8,128)S(1)}, u32[]{:S(2)}, u32[]{:S(2)}) collective-permute-start(f32[4,128,128]{2,1,0:T(8,128)S(1)} %get-tuple-element.33), channel_id=1, source_target_pairs={{0,1},{1,2},{2,3},{3,4},{4,5},{5,6},{6,7},{7,8},{8,9},{9,10},{10,1... | collective-permute-start | bytes 786440 | tf_op jit(solution)/shard_map/ppermute | solution.py:20
  4.6 12.3 %collective-permute-start.1 = (f32[4,128,128]{2,1,0:T(8,128)S(1)}, f32[4,128,128]{2,1,0:T(8,128)S(1)}, u32[]{:S(2)}, u32[]{:S(2)}) collective-permute-start(f32[4,128,128]{2,1,0:T(8,128)S(1)} %get-tuple-element.34), channel_id=1, source_target_pairs={{0,127},{1,0},{2,1},{3,2},{4,3},{5,4},{6,5},{7,6},{8,7},{9,8},{10,... | collective-permute-start | bytes 786440 | tf_op jit(solution)/shard_map/ppermute | solution.py:20
  16.8 1.6 %copy-start = (f32[8,4,128,128]{3,2,1,0:T(8,128)S(1)}, f32[8,4,128,128]{3,2,1,0:T(8,128)}, u32[]{:S(2)}) copy-start(f32[8,4,128,128]{3,2,1,0:T(8,128)} %a.7) | copy-start | bytes 6291460
  18.4 1.0 %copy-start.4 = (f32[8,128,128]{2,1,0:T(8,128)S(1)}, f32[8,128,128]{2,1,0:T(8,128)}, u32[]{:S(2)}) copy-start(f32[8,128,128]{2,1,0:T(8,128)} %dinv.3) | copy-start | bytes 1572868
  19.5 10.2 %copy-start.1 = (f32[8,4,128,128]{3,2,1,0:T(8,128)S(1)}, f32[8,4,128,128]{3,2,1,0:T(8,128)}, u32[]{:S(2)}) copy-start(f32[8,4,128,128]{3,2,1,0:T(8,128)} %a.7) | copy-start | bytes 6291460
  19.5 10.2 %copy-start.3 = (f32[8,128,128]{2,1,0:T(8,128)S(1)}, f32[8,128,128]{2,1,0:T(8,128)}, u32[]{:S(2)}) copy-start(f32[8,128,128]{2,1,0:T(8,128)} %t.3) | copy-start | bytes 1572868
  22.3 17.3 %collective-permute-start.4 = (f32[4,128,256]{2,1,0:T(8,128)S(1)}, f32[4,128,256]{2,1,0:T(8,128)S(1)}, u32[]{:S(2)}, u32[]{:S(2)}) collective-permute-start(f32[4,128,256]{2,1,0:T(8,128)S(1)} %get-tuple-element.47), channel_id=1, source_target_pairs={{0,1},{1,2},{2,3},{3,4},{4,5},{5,6},{6,7},{7,8},{8,9},{9,10},{10,1... | collective-permute-start | bytes 1572872 | tf_op jit(solution)/shard_map/ppermute | solution.py:20
  22.3 17.2 %collective-permute-start.5 = (f32[4,128,256]{2,1,0:T(8,128)S(1)}, f32[4,128,256]{2,1,0:T(8,128)S(1)}, u32[]{:S(2)}, u32[]{:S(2)}) collective-permute-start(f32[4,128,256]{2,1,0:T(8,128)S(1)} %get-tuple-element.48), channel_id=1, source_target_pairs={{0,127},{1,0},{2,1},{3,2},{4,3},{5,4},{6,5},{7,6},{8,7},{9,8},{10,... | collective-permute-start | bytes 1572872 | tf_op jit(solution)/shard_map/ppermute | solution.py:20
  32.3 16.7 %collective-permute-start.2 = (f32[4,128,256]{2,1,0:T(8,128)S(1)}, f32[4,128,256]{2,1,0:T(8,128)S(1)}, u32[]{:S(2)}, u32[]{:S(2)}) collective-permute-start(f32[4,128,256]{2,1,0:T(8,128)S(1)} %get-tuple-element.41), channel_id=1, source_target_pairs={{0,1},{1,2},{2,3},{3,4},{4,5},{5,6},{6,7},{7,8},{8,9},{9,10},{10,1... | collective-permute-start | bytes 1572872 | tf_op jit(solution)/shard_map/ppermute | solution.py:20
  32.4 16.6 %collective-permute-start.3 = (f32[4,128,256]{2,1,0:T(8,128)S(1)}, f32[4,128,256]{2,1,0:T(8,128)S(1)}, u32[]{:S(2)}, u32[]{:S(2)}) collective-permute-start(f32[4,128,256]{2,1,0:T(8,128)S(1)} %get-tuple-element.42), channel_id=1, source_target_pairs={{0,127},{1,0},{2,1},{3,2},{4,3},{5,4},{6,5},{7,6},{8,7},{9,8},{10,... | collective-permute-start | bytes 1572872 | tf_op jit(solution)/shard_map/ppermute | solution.py:20
  44.8 29.4 %collective-permute-start.7 = (f32[256,768]{1,0:T(8,128)S(1)}, f32[256,768]{1,0:T(8,128)S(1)}, u32[]{:S(2)}, u32[]{:S(2)}) collective-permute-start(f32[256,768]{1,0:T(8,128)S(1)} %get-tuple-element.52), channel_id=1, source_target_pairs={{0,127},{1,0},{2,1},{3,2},{4,3},{5,4},{6,5},{7,6},{8,7},{9,8},{10,... | collective-permute-start | bytes 2359304 | tf_op jit(solution)/shard_map/ppermute | solution.py:20
  49.0 25.2 %collective-permute-start.9 = (f32[256,768]{1,0:T(8,128)S(1)}, f32[256,768]{1,0:T(8,128)S(1)}, u32[]{:S(2)}, u32[]{:S(2)}) collective-permute-start(f32[256,768]{1,0:T(8,128)S(1)} %get-tuple-element.54), channel_id=1, source_target_pairs={{0,1},{1,2},{2,3},{3,4},{4,5},{5,6},{6,7},{7,8},{8,9},{9,10},{10,1... | collective-permute-start | bytes 2359304 | tf_op jit(solution)/shard_map/ppermute | solution.py:20
  52.9 13.9 %collective-permute-start.6 = (f32[256,512]{1,0:T(8,128)S(1)}, f32[256,512]{1,0:T(8,128)S(1)}, u32[]{:S(2)}, u32[]{:S(2)}) collective-permute-start(f32[256,512]{1,0:T(8,128)S(1)} %get-tuple-element.51), channel_id=1, source_target_pairs={{0,127},{1,0},{2,1},{3,2},{4,3},{5,4},{6,5},{7,6},{8,7},{9,8},{10,... | collective-permute-start | bytes 1572872 | tf_op jit(solution)/shard_map/ppermute | solution.py:20
  60.2 14.0 %collective-permute-start.8 = (f32[256,512]{1,0:T(8,128)S(1)}, f32[256,512]{1,0:T(8,128)S(1)}, u32[]{:S(2)}, u32[]{:S(2)}) collective-permute-start(f32[256,512]{1,0:T(8,128)S(1)} %get-tuple-element.53), channel_id=1, source_target_pairs={{0,1},{1,2},{2,3},{3,4},{4,5},{5,6},{6,7},{7,8},{8,9},{9,10},{10,1... | collective-permute-start | bytes 1572872 | tf_op jit(solution)/shard_map/ppermute | solution.py:20
  60.2 14.0 %copy-start.5 = (f32[2,128,128]{2,1,0:T(8,128)S(1)}, f32[2,128,128]{2,1,0:T(8,128)}, u32[]{:S(2)}) copy-start(f32[2,128,128]{2,1,0:T(8,128)} %inverse.1) | copy-start | bytes 393220

commit v2 on v1

v2 whole, which is shorter than its diff:
```python
import functools

import jax
import jax.numpy as jnp
from jax import lax
from jax.experimental import pallas as pl
from jax.experimental.pallas import tpu as pltpu
from jax.sharding import PartitionSpec as P


OMEGA = 0.6
AXES = ("gx", "gy")
F32 = jnp.float32
BF16 = jnp.bfloat16
COL1, POS2, POS3, LISTS, OWN_LAB, SIDE_LAB, TAB = 0, 8, 16, 24, 32, 64, 128
BELOW, ABOVE = 0, 1
ROW_CHUNK = 128


def exchanged(value, first):
    count = lax.axis_size(AXES)
    pairs = []
    for low in range(first, count + first, 2):
        high = (low + 1) % count
        pairs += [(low, high), (high, low)]
    return lax.ppermute(value, AXES, pairs)


def pair_side():
    return 1 - lax.rem(lax.axis_index("gy"), 2)


def split(x):
    high = x.astype(BF16)
    return high, (x - high.astype(F32)).astype(BF16)


def dot(a, b):
    return jnp.dot(a, b, preferred_element_type=F32)


def dot3(a_high, a_low, b_high, b_low):
    return dot(a_high, b_high) + dot(a_low, b_high) + dot(a_high, b_low)


def dot3k(a_high, a_low, b_high, b_low):
    both = jnp.concatenate([a_high, a_low], axis=1)
    return dot(both, jnp.concatenate([b_high, b_high], axis=0)) + dot(a_high, b_low)


def load_kernel(devices, cols_hbm, agg_hbm, t_hbm, dinv_hbm, a_hbm, tab, t_0, t_1, t, dinv, a, cols, agg, sem):
    copies = [
        pltpu.make_async_copy(source, target, sem.at[i])
        for i, (source, target) in enumerate(
            ((cols_hbm, cols), (agg_hbm, agg), (t_hbm, t), (dinv_hbm, dinv), (a_hbm, a))
        )
    ]
    for copy in copies:
        copy.start()
    rows, width = t.shape[0], t.shape[0] // 2
    device = lax.axis_index("gx") * lax.axis_size("gy") + lax.axis_index("gy")
    previous = lax.rem(device + devices - 1, devices)
    following = lax.rem(device + 1, devices)
    side = pair_side()

    def col(row, k):
        return cols[(row // ROW_CHUNK) * (4 * ROW_CHUNK) + k * ROW_CHUNK + lax.rem(row, ROW_CHUNK)]

    def read_mask(slab, k):
        mask = jnp.int32(0)
        for r in range(rows):
            mask = mask | (jnp.int32(1) << (col(slab * rows + r, k) & (rows - 1)))
        return mask

    def listed(mask):
        found, rank = [], jnp.int32(0)
        for r in range(rows):
            found.append(rank)
            rank = rank + ((mask >> r) & 1)
        result = []
        for j in range(width):
            value = jnp.int32(0)
            for r in range(rows):
                hit = ((mask >> r) & 1) * (found[r] == j).astype(jnp.int32)
                value = value + hit * r
            result.append(value)
        return result

    def count_below(mask, offset):
        below = mask & ((jnp.int32(1) << offset) - 1)
        total = jnp.int32(0)
        for r in range(rows):
            total = total + ((below >> r) & 1)
        return total

    copies[0].wait()
    lists = listed(read_mask(previous, 3)), listed(read_mask(following, 2))
    copies[2].wait()
    for j in range(width):
        mine = jnp.where(side == ABOVE, lists[ABOVE][j], lists[BELOW][j])
        other = jnp.where(side == ABOVE, lists[BELOW][j], lists[ABOVE][j])
        tab[LISTS + j] = mine
        tab[LISTS + width + j] = other
        t_0[j] = t[mine]
        t_1[j] = t[other]
    copies[1].wait()
    masks = read_mask(device, 2), read_mask(device, 3)
    for r in range(rows):
        row = device * rows + r
        tab[COL1 + r] = col(row, 1) & (rows - 1)
        tab[POS2 + r] = count_below(masks[BELOW], col(row, 2) & (rows - 1))
        tab[POS3 + r] = count_below(masks[ABOVE], col(row, 3) & (rows - 1))
        for k in range(4):
            tab[OWN_LAB + 4 * r + k] = agg[col(row, k)]
    for which, slab in ((BELOW, previous), (ABOVE, following)):
        held = listed(masks[which])
        for j in range(width):
            for k in range(4):
                tab[SIDE_LAB + 16 * which + 4 * j + k] = agg[col(slab * rows + held[j], k)]
    copies[3].wait()
    copies[4].wait()


def put(value, label, column):
    return jnp.where(label == column, value, jnp.zeros_like(value))


def two_columns(value, label):
    return jnp.concatenate([put(value, label, 0), put(value, label, 1)], axis=1)


def send(tab, tile, out_0, out_1):
    width = out_0.shape[0]
    for j in range(width):
        out_0[j] = tile[tab[LISTS + j]]
        out_1[j] = tile[tab[LISTS + width + j]]


def near_kernel(
    tab, a, t, dinv,
    a_high, a_low, own_high, own_low, trans_high, trans_low, near_0, near_1,
    t_high, t_low, tile,
):
    rows, block = t.shape[0], t.shape[1]
    for r in range(rows):
        t_high[r], t_low[r] = split(t[r])
    for r in range(rows):
        near = tab[COL1 + r]
        a0, a1 = split(a[r, 0]), split(a[r, 1])
        a_high[r] = jnp.concatenate([a0[0], a1[0]], axis=1)
        a_low[r] = jnp.concatenate([a0[1], a1[1]], axis=1)
        prod = jnp.concatenate(
            [dot3k(*a0, t_high[r], t_low[r]), dot3k(*a1, t_high[near], t_low[near])], axis=1
        )
        smoothed = dot3k(*split(dinv[r]), *split(prod))
        p0 = t[r] - OMEGA * smoothed[:, :block]
        p1 = -OMEGA * smoothed[:, block:]
        label0, label1 = tab[OWN_LAB + 4 * r], tab[OWN_LAB + 4 * r + 1]
        both = two_columns(p0, label0) + two_columns(p1, label1)
        tile[r] = both
        own_high[r], own_low[r] = split(both)
        place = slice(r * block, (r + 1) * block)
        trans_high[:, place], trans_low[:, place] = split(both.T)
    send(tab, tile, near_0, near_1)


def far_kernel(
    tab, a, dinv, t_0, t_1, after,
    a_high, a_low, below_high, below_low, above_high, above_low, trans_high, trans_low, far_0, far_1,
    t_high, t_low, tile,
):
    rows, block = dinv.shape[0], dinv.shape[1]
    side = pair_side()
    for j in range(rows // 2):
        t_high[side, j], t_low[side, j] = split(t_0[j])
        t_high[1 - side, j], t_low[1 - side, j] = split(t_1[j])
    for r in range(rows):
        below, above = tab[POS2 + r], tab[POS3 + r]
        a2, a3 = split(a[r, 2]), split(a[r, 3])
        a_high[r] = jnp.concatenate([a2[0], a3[0]], axis=1)
        a_low[r] = jnp.concatenate([a2[1], a3[1]], axis=1)
        prod = jnp.concatenate(
            [
                dot3k(*a2, t_high[BELOW, below], t_low[BELOW, below]),
                dot3k(*a3, t_high[ABOVE, above], t_low[ABOVE, above]),
            ],
            axis=1,
        )
        both = -OMEGA * dot3k(*split(dinv[r]), *split(prod))
        tile[r] = both
        left = two_columns(both[:, :block], tab[OWN_LAB + 4 * r + 2])
        right = two_columns(both[:, block:], tab[OWN_LAB + 4 * r + 3])
        below_high[r], below_low[r] = split(left)
        above_high[r], above_low[r] = split(right)
        place = slice(r * block, (r + 1) * block)
        trans_high[BELOW, :, place], trans_low[BELOW, :, place] = split(left.T)
        trans_high[ABOVE, :, place], trans_low[ABOVE, :, place] = split(right.T)
    send(tab, tile, far_0, far_1)


def wide(ref, *places):
    return jnp.concatenate([ref[place] for place in places], axis=0)


def pre_kernel(
    tab, a_high, a_low, own_high, own_low, below_high, below_low, above_high, above_low,
    part,
):
    rows = a_high.shape[0]
    half = own_high.shape[2]
    for r in range(rows):
        near = tab[COL1 + r]
        pairs = ((below_high, below_low), (own_high, own_low), (above_high, above_low))
        for c, (high, low) in enumerate(pairs):
            part[r, :, c * half : (c + 1) * half] = dot3(a_high[r], a_low[r], wide(high, r, near), wide(low, r, near))


def partial_rows(trans_high, trans_low, ap_high, ap_low, outs):
    side = pair_side()
    half = trans_high.shape[1]
    for which, out in ((side, outs[0]), (1 - side, outs[1])):
        for c in range(ap_high.shape[1] // half):
            cols = slice(c * half, (c + 1) * half)
            out[:, cols] = dot3(trans_high[which], trans_low[which], ap_high[:, cols], ap_low[:, cols])


def first_kernel(
    tab, a_high, a_low, part, trans_high, trans_low, near_0, near_1,
    ap_high, ap_low, out_0, out_1,
    p_high, p_low,
):
    rows, block = a_high.shape[0], a_high.shape[1]
    half = 2 * block
    side = pair_side()
    for j in range(rows // 2):
        p_high[side, j], p_low[side, j] = split(near_0[j])
        p_high[1 - side, j], p_low[1 - side, j] = split(near_1[j])
    for r in range(rows):
        pos2, pos3 = tab[POS2 + r], tab[POS3 + r]
        a2 = a_high[r, :, :block], a_low[r, :, :block]
        a3 = a_high[r, :, block:], a_low[r, :, block:]
        low = part[r, :, :half] + dot3k(*a2, p_high[BELOW, pos2], p_low[BELOW, pos2])
        upp = part[r, :, 2 * half :] + dot3k(*a3, p_high[ABOVE, pos3], p_low[ABOVE, pos3])
        place = slice(r * block, (r + 1) * block)
        ap_high[place, :half], ap_low[place, :half] = split(low)
        ap_high[place, half:], ap_low[place, half:] = split(upp)
    partial_rows(trans_high, trans_low, ap_high, ap_low, (out_0, out_1))


def second_kernel(
    tab, a_high, a_low, part, trans_high, trans_low, far_0, far_1, after,
    ap_high, ap_low, out_0, out_1,
    p_high, p_low,
):
    rows, block = a_high.shape[0], a_high.shape[1]
    half = 2 * block
    side = pair_side()
    for which, ref in ((side, far_0), (1 - side, far_1)):
        for j in range(rows // 2):
            label = SIDE_LAB + 16 * which + 4 * j
            value = ref[j]
            spread = [two_columns(value[:, :block], tab[label + 2]), two_columns(value[:, block:], tab[label + 3])]
            p_high[which, j], p_low[which, j] = split(jnp.concatenate(spread, axis=1))
    for r in range(rows):
        pos2, pos3 = tab[POS2 + r], tab[POS3 + r]
        a2 = a_high[r, :, :block], a_low[r, :, :block]
        a3 = a_high[r, :, block:], a_low[r, :, block:]
        left = dot3k(*a2, p_high[BELOW, pos2], p_low[BELOW, pos2])
        right = dot3k(*a3, p_high[ABOVE, pos3], p_low[ABOVE, pos3])
        own = part[r, :, half : 2 * half] + left[:, half:] + right[:, :half]
        place = slice(r * block, (r + 1) * block)
        ap_high[place, :half], ap_low[place, :half] = split(left[:, :half])
        ap_high[place, half : 2 * half], ap_low[place, half : 2 * half] = split(own)
        ap_high[place, 2 * half :], ap_low[place, 2 * half :] = split(right[:, half:])
    partial_rows(trans_high, trans_low, ap_high, ap_low, (out_0, out_1))


HELD = ((1, 0), (0, 0), (1, 1), (0, 1), (1, 2))


def own_kernel(trans_high, trans_low, ap1_high, ap1_low, ap2_high, ap2_low, own):
    half = trans_high.shape[0]
    aps = (ap1_high, ap1_low), (ap2_high, ap2_low)
    for d, (which, c) in enumerate(HELD):
        cols = slice(c * half, (c + 1) * half)
        high, low = aps[which]
        own[:, d * half : (d + 1) * half] = dot3(trans_high[...], trans_low[...], high[:, cols], low[:, cols])


def last_kernel(inverse, own, first_0, first_1, second_0, second_1, out):
    block = inverse.shape[1]
    half = 2 * block

    def finish(above, below):
        for agg in range(2):
            inv = split(inverse[agg])
            line = slice(agg * block, (agg + 1) * block)
            for d in range(-3, 4):
                total = None
                if -2 <= d <= 2:
                    total = own[line, (d + 2) * half : (d + 3) * half]
                for shift, bufs in ((1, above), (-1, below)):
                    if -2 <= d - shift <= 2:
                        which, c = HELD[d - shift + 2]
                        part = bufs[which][line, c * half : (c + 1) * half]
                        total = part if total is None else total + part
                result = dot3k(*inv, *split(total))
                out[agg, 2 * (d + 3)] = result[:, :block]
                out[agg, 2 * (d + 3) + 1] = result[:, block:]

    side = pair_side()

    @pl.when(side == ABOVE)
    def _():
        finish((first_0, second_0), (first_1, second_1))

    @pl.when(side == BELOW)
    def _():
        finish((first_1, second_1), (first_0, second_0))


def call(body, outs, ins, scratch=(), micros=1.0, hbm=False):
    smem = pl.BlockSpec(memory_space=pltpu.SMEM)
    vmem = pl.BlockSpec(memory_space=pltpu.VMEM)
    flops = int(micros * 1e6 * 100)

    def spec(x):
        return smem if x.dtype == jnp.int32 else vmem

    return pl.pallas_call(
        body,
        out_shape=outs,
        in_specs=[pl.BlockSpec(memory_space=pltpu.HBM) if hbm else spec(x) for x in ins],
        out_specs=jax.tree.map(spec, outs),
        scratch_shapes=[pltpu.VMEM(*x) if isinstance(x, tuple) else x for x in scratch],
        compiler_params=pltpu.CompilerParams(vmem_limit_bytes=24 * 2**20),
        cost_estimate=pl.CostEstimate(flops=flops, bytes_accessed=2**20, transcendentals=0),
    )(*ins)


def shards(a_blocks, a_cols, t_blocks, t_agg, dinv, coarse_inv):
    devices = lax.axis_size(AXES)
    rows, block = t_blocks.shape[:2]
    width, half, deep = rows // 2, 2 * block, rows * block
    shape = jax.ShapeDtypeStruct
    pair = lambda *dims: [shape(dims, BF16), shape(dims, BF16)]
    cols = a_cols.reshape(-1, ROW_CHUNK, 4).transpose(0, 2, 1).reshape(-1)

    def swap(value_0, value_1):
        far = exchanged(value_1, 1)
        return exchanged(value_0, 0), far

    tab, t_0, t_1, t, d, a = call(
        functools.partial(load_kernel, devices),
        [shape((TAB,), jnp.int32)]
        + [shape((width, block, block), F32)] * 2
        + [shape(x.shape, F32) for x in (t_blocks, dinv, a_blocks)],
        [pltpu.with_memory_space_constraint(x, pltpu.HBM) for x in (cols, t_agg, t_blocks, dinv, a_blocks)],
        [pltpu.SMEM(cols.shape, jnp.int32), pltpu.SMEM(t_agg.shape, jnp.int32), pltpu.SemaphoreType.DMA((5,))],
        hbm=True,
    )
    t_0, t_1 = swap(t_0, t_1)
    a01_high, a01_low, own_high, own_low, pt_high, pt_low, near_0, near_1 = call(
        near_kernel,
        pair(rows, block, half) * 2 + pair(half, deep) + [shape((width, block, half), F32)] * 2,
        [tab, a, t, d],
        [((rows, block, block), BF16)] * 2 + [((rows, block, half), F32)],
        micros=3,
    )
    near_0, near_1 = swap(near_0, near_1)
    a23_high, a23_low, below_high, below_low, above_high, above_low, side_high, side_low, far_0, far_1 = call(
        far_kernel,
        pair(rows, block, half) * 3 + pair(2, half, deep) + [shape((width, block, half), F32)] * 2,
        [tab, a, d, t_0, t_1, own_high],
        [((2, width, block, block), BF16)] * 2 + [((rows, block, half), F32)],
        micros=3,
    )
    far_0, far_1 = swap(far_0, far_1)
    (part,) = call(
        pre_kernel,
        [shape((rows, block, 3 * half), F32)],
        [tab, a01_high, a01_low, own_high, own_low, below_high, below_low, above_high, above_low],
        micros=2,
    )
    ap1_high, ap1_low, first_0, first_1 = call(
        first_kernel,
        pair(deep, 2 * half) + [shape((half, 2 * half), F32)] * 2,
        [tab, a23_high, a23_low, part, side_high, side_low, near_0, near_1],
        [((2, width, block, half), BF16)] * 2,
        micros=4,
    )
    first_0, first_1 = swap(first_0, first_1)
    ap2_high, ap2_low, second_0, second_1 = call(
        second_kernel,
        pair(deep, 3 * half) + [shape((half, 3 * half), F32)] * 2,
        [tab, a23_high, a23_low, part, side_high, side_low, far_0, far_1, ap1_high],
        [((2, width, block, 2 * half), BF16)] * 2,
        micros=5,
    )
    second_0, second_1 = swap(second_0, second_1)
    (own,) = call(
        own_kernel, [shape((half, 5 * half), F32)], [pt_high, pt_low, ap1_high, ap1_low, ap2_high, ap2_low], micros=2
    )
    (out,) = call(
        last_kernel,
        [shape((2, 14, block, block), F32)],
        [coarse_inv, own, first_0, first_1, second_0, second_1],
        micros=2,
    )
    return out


def solution(mesh):
    placed = (
        P(AXES, None, None, None),
        P(),
        P(AXES, None, None),
        P(),
        P(AXES, None, None),
        P(AXES, None, None),
    )
    return jax.shard_map(
        shards,
        mesh=mesh,
        in_specs=placed,
        out_specs=P(AXES, None, None, None),
        check_vma=False,
    )
```

time: 76.5 us -> 63.5 us (0.83)
  starting transfers between devices: 34.4 us -> 24.9 us
  local copies, waits for them, and re-layouts: 5.09 us -> 0.01 us
  Pallas kernels: 20.7 us -> 21.9 us
    ppermute x10, starting transfers between devices: 34.4 us -> 24.9 us  [exchanged(): return lax.ppermute(value, AXES, pairs)]
    unnamed x16 -> x2, local copies, waits for them, and re-layouts: 5.09 us -> 0.01 us
    pallas_call x7 -> x8, Pallas kernels: 20.7 us -> 21.9 us  [call(): pl.pallas_call(body, out_shape=outs, in_specs=[pl.BlockSpec(memory_space=...]
  transfers between devices with their start and end apart: 10 -> 10, of which waited for: 3 -> 4; matrix products, arithmetic and copies ran while one was open for 0% -> 0% of each run, Pallas kernels for 18% -> 20%
where the time goes in v2:
time: 63.5 us; the launch traced here: 63.4 us
  starting transfers between devices  24.9 us (39%)
  Pallas kernels  21.9 us (34%)
  waiting for transfers between devices  16.5 us (26%)
    ppermute x10, starting transfers between devices, exchanged(): return lax.ppermute(value, AXES, pairs)  24.9 us
    pallas_call x8, Pallas kernels, call(): pl.pallas_call(body, out_shape=outs, in_specs=[pl.BlockSpec(memory_space=...  21.9 us
    ppermute x10, waiting for transfers between devices, exchanged(): return lax.ppermute(value, AXES, pairs)  16.5 us
  transfers between devices with their start and end apart: 10, of which 4 were waited for; matrix products, arithmetic and copies ran while one was open for 0% of the time, Pallas kernels for 20%

profile of v2, /device:TPU:0, one launch (start us, length us, event | category | flops | bytes accessed | tf_op | source)
XLA Modules:
  0.0 63.4 jit_solution(8252148012463041443)
XLA Ops:
  0.0 2.6 %shard_map.64 = (s32[128]{0:T(128)S(1)}, f32[4,128,128]{2,1,0:T(8,128)S(1)}, f32[4,128,128]{2,1,0:T(8,128)S(1)}, f32[8,128,128]{2,1,0:T(8,128)S(1)}, f32[8,128,1...) custom-call(s32[4096]{0:T(1024)} %bitcast.5, s32[1024]{0:T(1024)} %agg_hbm.1, f32[8,128,128]{2,1,0:T(8,128)} %t_hbm.1, ...), custom_call_target="tpu_custom_call" | custom-call | flops 100000000 | bytes 1048576 | tf_op jit(solution)/shard_map/pallas_call | solution.py:330
  2.6 0.1 collective-permute-start
  2.7 8.9 %collective-permute-start.1 = (f32[4,128,128]{2,1,0:T(8,128)S(1)}, f32[4,128,128]{2,1,0:T(8,128)S(1)}, u32[]{:S(2)}, u32[]{:S(2)}) collective-permute-start(f32[4,128,128]{2,1,0:T(8,128)S(1)} %get-tuple-element.44), channel_id=1, source_target_pairs={{1,2},{2,1},{3,4},{4,3},{5,6},{6,5},{7,8},{8,7},{9,10},{10,9},{11,... | collective-permute-start | bytes 786440 | tf_op jit(solution)/shard_map/ppermute | solution.py:26
  11.6 2.7 %shard_map.65 = (bf16[8,128,256]{2,1,0:T(8,128)(2,1)S(1)}, bf16[8,128,256]{2,1,0:T(8,128)(2,1)S(1)}, bf16[8,128,256]{2,1,0:T(8,128)(2,1)S(1)}, bf16[8,128,256]{2...) custom-call(s32[128]{0:T(128)S(1)} %get-tuple-element.37.tab, ...), custom_call_target="tpu_custom_call" | custom-call | flops 300000000 | bytes 1048576 | tf_op jit(solution)/shard_map/pallas_call | solution.py:330
  14.2 0.1 collective-permute-start.2
  14.3 0.9 %collective-permute-start.3 = (f32[4,128,256]{2,1,0:T(8,128)S(1)}, f32[4,128,256]{2,1,0:T(8,128)S(1)}, u32[]{:S(2)}, u32[]{:S(2)}) collective-permute-start(f32[4,128,256]{2,1,0:T(8,128)S(1)} %get-tuple-element.58), channel_id=1, source_target_pairs={{1,2},{2,1},{3,4},{4,3},{5,6},{6,5},{7,8},{8,7},{9,10},{10,9},{11,... | collective-permute-start | bytes 1572872 | tf_op jit(solution)/shard_map/ppermute | solution.py:26
  15.2 0.0 collective-permute-done.t_0
  15.2 0.4 collective-permute-done.1.t_1
  15.6 2.8 %shard_map.66 = (bf16[8,128,256]{2,1,0:T(8,128)(2,1)S(1)}, bf16[8,128,256]{2,1,0:T(8,128)(2,1)S(1)}, bf16[8,128,256]{2,1,0:T(8,128)(2,1)S(1)}, bf16[8,128,256]{2...) custom-call(s32[128]{0:T(128)S(1)} %get-tuple-element.37.tab, ...), custom_call_target="tpu_custom_call" | custom-call | flops 300000000 | bytes 1048576 | tf_op jit(solution)/shard_map/pallas_call | solution.py:330
  18.4 0.1 collective-permute-start.4
  18.5 7.4 %collective-permute-start.5 = (f32[4,128,256]{2,1,0:T(8,128)S(1)}, f32[4,128,256]{2,1,0:T(8,128)S(1)}, u32[]{:S(2)}, u32[]{:S(2)}) collective-permute-start(f32[4,128,256]{2,1,0:T(8,128)S(1)} %get-tuple-element.62), channel_id=1, source_target_pairs={{1,2},{2,1},{3,4},{4,3},{5,6},{6,5},{7,8},{8,7},{9,10},{10,9},{11,... | collective-permute-start | bytes 1572872 | tf_op jit(solution)/shard_map/ppermute | solution.py:26
  26.0 1.9 %shard_map.67.part = f32[8,128,768]{2,1,0:T(8,128)S(1)} custom-call(s32[128]{0:T(128)S(1)} %get-tuple-element.37.tab, bf16[8,128,256]{2,1,0:T(8,128)(2,1)S(1)} %get-tuple-element.48.a_high, bf16[8,128,256]{2,1,0:T(8,128)(2,1)S(1)} %get-tuple-element.49.a_low, bf16[8,128,256]{2,1,0:T(8,128)(2,1)S(1)} %get-tuple-element.45.after.own_high, ...), custom_call_target="tpu_custom_call" | custom-call | flops 200000000 | bytes 1048576 | tf_op jit(solution)/shard_map/pallas_call | solution.py:330
  27.9 0.0 collective-permute-done.2.near_0
  27.9 0.5 collective-permute-done.3.near_1
  28.4 3.1 %shard_map.68 = (bf16[1024,512]{1,0:T(8,128)(2,1)S(1)}, bf16[1024,512]{1,0:T(8,128)(2,1)S(1)}, f32[256,512]{1,0:T(8,128)S(1)}, f32[256,512]{1,0:T(8,128)S(1)}) custom-call(s32[128]{0:T(128)S(1)} %get-tuple-element.37.tab, bf16[8,128,256]{2,1,0:T(8,128)(2,1)S(1)} %get-tuple-element.46.a_high, bf16[8,128,256]{2,1,0:T(8,128)(2,1)S(1)} %get-tuple-element.47.a_low, ...), custom_call_target="tpu_custom_call" | custom-call | flops 400000000 | bytes 1048576 | tf_op jit(solution)/shard_map/pallas_call | solution.py:330
  31.5 0.0 collective-permute-done.4.far_0
  31.5 2.5 %collective-permute-done.5.far_1 = f32[4,128,256]{2,1,0:T(8,128)S(1)} collective-permute-done((f32[4,128,256]{2,1,0:T(8,128)S(1)}, f32[4,128,256]{2,1,0:T(8,128)S(1)}, u32[]{:S(2)}, u32[]{:S(2)}) %collective-permute-start.5) | collective-permute-done | bytes 524320 | tf_op jit(solution)/shard_map/ppermute | solution.py:26
  34.1 4.8 %shard_map.69 = (bf16[1024,768]{1,0:T(8,128)(2,1)S(1)}, bf16[1024,768]{1,0:T(8,128)(2,1)S(1)}, f32[256,768]{1,0:T(8,128)S(1)}, f32[256,768]{1,0:T(8,128)S(1)}) custom-call(s32[128]{0:T(128)S(1)} %get-tuple-element.37.tab, bf16[8,128,256]{2,1,0:T(8,128)(2,1)S(1)} %get-tuple-element.46.a_high, bf16[8,128,256]{2,1,0:T(8,128)(2,1)S(1)} %get-tuple-element.47.a_low, ...), custom_call_target="tpu_custom_call" | custom-call | flops 500000000 | bytes 1048576 | tf_op jit(solution)/shard_map/pallas_call | solution.py:330
  38.8 0.1 collective-permute-start.8
  38.9 6.0 %collective-permute-start.9 = (f32[256,768]{1,0:T(8,128)S(1)}, f32[256,768]{1,0:T(8,128)S(1)}, u32[]{:S(2)}, u32[]{:S(2)}) collective-permute-start(f32[256,768]{1,0:T(8,128)S(1)} %get-tuple-element.68), channel_id=1, source_target_pairs={{1,2},{2,1},{3,4},{4,3},{5,6},{6,5},{7,8},{8,7},{9,10},{10,9},{11,... | collective-permute-start | bytes 2359304 | tf_op jit(solution)/shard_map/ppermute | solution.py:26
  44.9 0.0 collective-permute-start.6
  45.0 1.2 %collective-permute-start.7 = (f32[256,512]{1,0:T(8,128)S(1)}, f32[256,512]{1,0:T(8,128)S(1)}, u32[]{:S(2)}, u32[]{:S(2)}) collective-permute-start(f32[256,512]{1,0:T(8,128)S(1)} %get-tuple-element.66), channel_id=1, source_target_pairs={{1,2},{2,1},{3,4},{4,3},{5,6},{6,5},{7,8},{8,7},{9,10},{10,9},{11,... | collective-permute-start | bytes 1572872 | tf_op jit(solution)/shard_map/ppermute | solution.py:26
  46.2 0.0 copy-start
  46.2 2.2 %shard_map.70.own = f32[256,1280]{1,0:T(8,128)S(1)} custom-call(bf16[256,1024]{1,0:T(8,128)(2,1)S(1)} %get-tuple-element.41.trans_high, bf16[256,1024]{1,0:T(8,128)(2,1)S(1)} %get-tuple-element.42.trans_low, bf16[1024,512]{1,0:T(8,128)(2,1)S(1)} %get-tuple-element.59.after.ap1_high, bf16[1024,512]{1,0:T(8,128)(2,1)S(1)} %get-tuple-element.60.ap1_low, ...), custom_call_target="tpu_custom_call" | custom-call | flops 200000000 | bytes 1048576 | tf_op jit(solution)/shard_map/pallas_call | solution.py:330
  48.4 0.0 collective-permute-done.6.first_0
  48.4 13.1 %collective-permute-done.7.first_1 = f32[256,512]{1,0:T(8,128)S(1)} collective-permute-done((f32[256,512]{1,0:T(8,128)S(1)}, f32[256,512]{1,0:T(8,128)S(1)}, u32[]{:S(2)}, u32[]{:S(2)}) %collective-permute-start.7) | collective-permute-done | bytes 524320 | tf_op jit(solution)/shard_map/ppermute | solution.py:26
  61.5 0.0 collective-permute-done.8.second_0
  61.5 0.0 collective-permute-done.9.second_1
  61.5 0.0 copy-done
  61.5 1.9 %shard_map.71 = f32[2,14,128,128]{3,2,1,0:T(8,128)} custom-call(f32[2,128,128]{2,1,0:T(8,128)S(1)} %copy-done, f32[256,1280]{1,0:T(8,128)S(1)} %shard_map.70.own, f32[256,512]{1,0:T(8,128)S(1)} %collective-permute-done.6.first_0, f32[256,512]{1,0:T(8,128)S(1)} %collective-permute-done.7.first_1, f32[256,768]{1,0:T(8,128)S(1)} %collective-permute-done.8.second_0, ...), custom_call_target="tpu_custom_call" | custom-call | flops 200000000 | bytes 1048576 | tf_op jit(solution)/shard_map/pallas_call | solution.py:330
Async XLA Ops:
  2.6 12.7 %collective-permute-start = (f32[4,128,128]{2,1,0:T(8,128)S(1)}, f32[4,128,128]{2,1,0:T(8,128)S(1)}, u32[]{:S(2)}, u32[]{:S(2)}) collective-permute-start(f32[4,128,128]{2,1,0:T(8,128)S(1)} %get-tuple-element.43), channel_id=1, source_target_pairs={{0,1},{1,0},{2,3},{3,2},{4,5},{5,4},{6,7},{7,6},{8,9},{9,8},{10,11... | collective-permute-start | bytes 786440 | tf_op jit(solution)/shard_map/ppermute | solution.py:26
  2.7 12.9 %collective-permute-start.1 = (f32[4,128,128]{2,1,0:T(8,128)S(1)}, f32[4,128,128]{2,1,0:T(8,128)S(1)}, u32[]{:S(2)}, u32[]{:S(2)}) collective-permute-start(f32[4,128,128]{2,1,0:T(8,128)S(1)} %get-tuple-element.44), channel_id=1, source_target_pairs={{1,2},{2,1},{3,4},{4,3},{5,6},{6,5},{7,8},{8,7},{9,10},{10,9},{11,... | collective-permute-start | bytes 786440 | tf_op jit(solution)/shard_map/ppermute | solution.py:26
  14.2 13.7 %collective-permute-start.2 = (f32[4,128,256]{2,1,0:T(8,128)S(1)}, f32[4,128,256]{2,1,0:T(8,128)S(1)}, u32[]{:S(2)}, u32[]{:S(2)}) collective-permute-start(f32[4,128,256]{2,1,0:T(8,128)S(1)} %get-tuple-element.57), channel_id=1, source_target_pairs={{0,1},{1,0},{2,3},{3,2},{4,5},{5,4},{6,7},{7,6},{8,9},{9,8},{10,11... | collective-permute-start | bytes 1572872 | tf_op jit(solution)/shard_map/ppermute | solution.py:26
  14.3 14.1 %collective-permute-start.3 = (f32[4,128,256]{2,1,0:T(8,128)S(1)}, f32[4,128,256]{2,1,0:T(8,128)S(1)}, u32[]{:S(2)}, u32[]{:S(2)}) collective-permute-start(f32[4,128,256]{2,1,0:T(8,128)S(1)} %get-tuple-element.58), channel_id=1, source_target_pairs={{1,2},{2,1},{3,4},{4,3},{5,6},{6,5},{7,8},{8,7},{9,10},{10,9},{11,... | collective-permute-start | bytes 1572872 | tf_op jit(solution)/shard_map/ppermute | solution.py:26
  18.4 13.1 %collective-permute-start.4 = (f32[4,128,256]{2,1,0:T(8,128)S(1)}, f32[4,128,256]{2,1,0:T(8,128)S(1)}, u32[]{:S(2)}, u32[]{:S(2)}) collective-permute-start(f32[4,128,256]{2,1,0:T(8,128)S(1)} %get-tuple-element.61), channel_id=1, source_target_pairs={{0,1},{1,0},{2,3},{3,2},{4,5},{5,4},{6,7},{7,6},{8,9},{9,8},{10,11... | collective-permute-start | bytes 1572872 | tf_op jit(solution)/shard_map/ppermute | solution.py:26
  18.5 15.5 %collective-permute-start.5 = (f32[4,128,256]{2,1,0:T(8,128)S(1)}, f32[4,128,256]{2,1,0:T(8,128)S(1)}, u32[]{:S(2)}, u32[]{:S(2)}) collective-permute-start(f32[4,128,256]{2,1,0:T(8,128)S(1)} %get-tuple-element.62), channel_id=1, source_target_pairs={{1,2},{2,1},{3,4},{4,3},{5,6},{6,5},{7,8},{8,7},{9,10},{10,9},{11,... | collective-permute-start | bytes 1572872 | tf_op jit(solution)/shard_map/ppermute | solution.py:26
  38.8 22.6 %collective-permute-start.8 = (f32[256,768]{1,0:T(8,128)S(1)}, f32[256,768]{1,0:T(8,128)S(1)}, u32[]{:S(2)}, u32[]{:S(2)}) collective-permute-start(f32[256,768]{1,0:T(8,128)S(1)} %get-tuple-element.67), channel_id=1, source_target_pairs={{0,1},{1,0},{2,3},{3,2},{4,5},{5,4},{6,7},{7,6},{8,9},{9,8},{10,11... | collective-permute-start | bytes 2359304 | tf_op jit(solution)/shard_map/ppermute | solution.py:26
  38.9 22.5 %collective-permute-start.9 = (f32[256,768]{1,0:T(8,128)S(1)}, f32[256,768]{1,0:T(8,128)S(1)}, u32[]{:S(2)}, u32[]{:S(2)}) collective-permute-start(f32[256,768]{1,0:T(8,128)S(1)} %get-tuple-element.68), channel_id=1, source_target_pairs={{1,2},{2,1},{3,4},{4,3},{5,6},{6,5},{7,8},{8,7},{9,10},{10,9},{11,... | collective-permute-start | bytes 2359304 | tf_op jit(solution)/shard_map/ppermute | solution.py:26
  44.9 3.4 %collective-permute-start.6 = (f32[256,512]{1,0:T(8,128)S(1)}, f32[256,512]{1,0:T(8,128)S(1)}, u32[]{:S(2)}, u32[]{:S(2)}) collective-permute-start(f32[256,512]{1,0:T(8,128)S(1)} %get-tuple-element.65), channel_id=1, source_target_pairs={{0,1},{1,0},{2,3},{3,2},{4,5},{5,4},{6,7},{7,6},{8,9},{9,8},{10,11... | collective-permute-start | bytes 1572872 | tf_op jit(solution)/shard_map/ppermute | solution.py:26
  45.0 16.5 %collective-permute-start.7 = (f32[256,512]{1,0:T(8,128)S(1)}, f32[256,512]{1,0:T(8,128)S(1)}, u32[]{:S(2)}, u32[]{:S(2)}) collective-permute-start(f32[256,512]{1,0:T(8,128)S(1)} %get-tuple-element.66), channel_id=1, source_target_pairs={{1,2},{2,1},{3,4},{4,3},{5,6},{6,5},{7,8},{8,7},{9,10},{10,9},{11,... | collective-permute-start | bytes 1572872 | tf_op jit(solution)/shard_map/ppermute | solution.py:26
  46.2 15.3 %copy-start = (f32[2,128,128]{2,1,0:T(8,128)S(1)}, f32[2,128,128]{2,1,0:T(8,128)}, u32[]{:S(2)}) copy-start(f32[2,128,128]{2,1,0:T(8,128)} %inverse.1) | copy-start | bytes 393220

commit v3 on v2

v3 whole, which is shorter than its diff:
```python
import functools

import jax
import jax.numpy as jnp
from jax import lax
from jax.experimental import pallas as pl
from jax.experimental.pallas import tpu as pltpu
from jax.sharding import PartitionSpec as P


OMEGA = 0.6
AXES = ("gx", "gy")
F32 = jnp.float32
BF16 = jnp.bfloat16
ROW, NEAR, POS2, POS3, LIST_0, OWN_LAB, SIDE_LAB, TAB = 0, 8, 16, 24, 32, 48, 80, 128
BELOW, ABOVE = 0, 1
ROW_CHUNK = 128


def exchanged(value, first):
    count = lax.axis_size(AXES)
    pairs = []
    for low in range(first, count + first, 2):
        high = (low + 1) % count
        pairs += [(low, high), (high, low)]
    return lax.ppermute(value, AXES, pairs)


def pair_side():
    return 1 - lax.rem(lax.axis_index("gy"), 2)


def split(x):
    high = x.astype(BF16)
    return high, (x - high.astype(F32)).astype(BF16)


def dot(a, b):
    return jnp.dot(a, b, preferred_element_type=F32)


def dot3(a_high, a_low, b_high, b_low):
    return dot(a_high, b_high) + dot(a_low, b_high) + dot(a_high, b_low)


def dot3k(a_high, a_low, b_high, b_low):
    both = jnp.concatenate([a_high, a_low], axis=1)
    return dot(both, jnp.concatenate([b_high, b_high], axis=0)) + dot(a_high, b_low)


def load_kernel(devices, cols_hbm, agg_hbm, t_hbm, tab, t_0, t_1, t, cols, agg, sem):
    copies = [
        pltpu.make_async_copy(source, target, sem.at[i])
        for i, (source, target) in enumerate(((cols_hbm, cols), (agg_hbm, agg), (t_hbm, t)))
    ]
    for copy in copies:
        copy.start()
    rows, width = t.shape[0], t.shape[0] // 2
    device = lax.axis_index("gx") * lax.axis_size("gy") + lax.axis_index("gy")
    previous = lax.rem(device + devices - 1, devices)
    following = lax.rem(device + 1, devices)
    side = pair_side()

    def col(row, k):
        return cols[(row // ROW_CHUNK) * (4 * ROW_CHUNK) + k * ROW_CHUNK + lax.rem(row, ROW_CHUNK)]

    def read_mask(slab, k):
        mask = jnp.int32(0)
        for r in range(rows):
            mask = mask | (jnp.int32(1) << (col(slab * rows + r, k) & (rows - 1)))
        return mask

    def listed(mask):
        found, rank = [], jnp.int32(0)
        for r in range(rows):
            found.append(rank)
            rank = rank + ((mask >> r) & 1)
        result = []
        for j in range(width):
            value = jnp.int32(0)
            for r in range(rows):
                hit = ((mask >> r) & 1) * (found[r] == j).astype(jnp.int32)
                value = value + hit * r
            result.append(value)
        return result

    def count_below(mask, offset):
        below = mask & ((jnp.int32(1) << offset) - 1)
        total = jnp.int32(0)
        for r in range(rows):
            total = total + ((below >> r) & 1)
        return total

    copies[0].wait()
    read = read_mask(previous, 3), read_mask(following, 2)
    mask_0 = jnp.where(side == ABOVE, read[ABOVE], read[BELOW])
    mask_1 = jnp.where(side == ABOVE, read[BELOW], read[ABOVE])
    order = listed(mask_1) + listed((jnp.int32(1) << rows) - 1 - mask_1)
    list_0 = listed(mask_0)
    copies[2].wait()
    for j in range(width):
        t_1[j] = t[order[j]]
        t_0[j] = t[list_0[j]]

    def place(offset):
        sent = (mask_1 >> offset) & 1
        rank = count_below(mask_1, offset)
        return jnp.where(sent == 1, rank, width + offset - rank)

    copies[1].wait()
    masks = read_mask(device, 2), read_mask(device, 3)
    for j in range(width):
        tab[LIST_0 + j] = place(list_0[j])
    for u in range(rows):
        row = device * rows + order[u]
        tab[ROW + u] = order[u]
        tab[NEAR + u] = place(col(row, 1) & (rows - 1))
        tab[POS2 + u] = count_below(masks[BELOW], col(row, 2) & (rows - 1))
        tab[POS3 + u] = count_below(masks[ABOVE], col(row, 3) & (rows - 1))
        for k in range(4):
            tab[OWN_LAB + 4 * u + k] = agg[col(row, k)]
    for which, slab in ((BELOW, previous), (ABOVE, following)):
        held = listed(masks[which])
        for j in range(width):
            for k in range(2):
                tab[SIDE_LAB + 8 * which + 2 * j + k] = agg[col(slab * rows + held[j], 2 + k)]


def put(value, label, column):
    return jnp.where(label == column, value, jnp.zeros_like(value))


def two_columns(value, label):
    return jnp.concatenate([put(value, label, 0), put(value, label, 1)], axis=1)


def near_tile(tab, a, t, dinv, u):
    block = t.shape[1]
    row = tab[ROW + u]
    near = tab[ROW + tab[NEAR + u]]
    prod = jnp.concatenate(
        [dot3k(*split(a[row, 0]), *split(t[row])), dot3k(*split(a[row, 1]), *split(t[near]))], axis=1
    )
    smoothed = dot3k(*split(dinv[row]), *split(prod))
    p0 = t[row] - OMEGA * smoothed[:, :block]
    p1 = -OMEGA * smoothed[:, block:]
    return two_columns(p0, tab[OWN_LAB + 4 * u]) + two_columns(p1, tab[OWN_LAB + 4 * u + 1])


def near_sent_kernel(tab, a, t, dinv, near_1):
    for u in range(near_1.shape[0]):
        near_1[u] = near_tile(tab, a, t, dinv, u)


def near_rest_kernel(tab, a, t, dinv, near_1, near_0, own):
    width = near_1.shape[0]
    for u in range(width):
        own[u] = near_1[u]
        own[width + u] = near_tile(tab, a, t, dinv, width + u)
    for j in range(width):
        near_0[j] = own[tab[LIST_0 + j]]


def far_tile(tab, a, dinv, t_high, t_low, u):
    row = tab[ROW + u]
    below, above = tab[POS2 + u], tab[POS3 + u]
    prod = jnp.concatenate(
        [
            dot3k(*split(a[row, 2]), t_high[BELOW, below], t_low[BELOW, below]),
            dot3k(*split(a[row, 3]), t_high[ABOVE, above], t_low[ABOVE, above]),
        ],
        axis=1,
    )
    return -OMEGA * dot3k(*split(dinv[row]), *split(prod))


def far_sent_kernel(tab, a, dinv, t_0, t_1, after, far_1, t_high, t_low):
    side = pair_side()
    for j in range(t_0.shape[0]):
        t_high[side, j], t_low[side, j] = split(t_0[j])
        t_high[1 - side, j], t_low[1 - side, j] = split(t_1[j])
    for u in range(far_1.shape[0]):
        far_1[u] = far_tile(tab, a, dinv, t_high, t_low, u)


def far_rest_kernel(tab, a, dinv, t_high, t_low, far_1, far_0, far):
    width = far_1.shape[0]
    for u in range(width):
        far[u] = far_1[u]
        far[width + u] = far_tile(tab, a, dinv, t_high, t_low, width + u)
    for j in range(width):
        far_0[j] = far[tab[LIST_0 + j]]


def far_split_kernel(tab, a, dinv, t_0, t_1, far_1, far_0, far, t_high, t_low):
    side = pair_side()
    for j in range(t_0.shape[0]):
        t_high[side, j], t_low[side, j] = split(t_0[j])
        t_high[1 - side, j], t_low[1 - side, j] = split(t_1[j])
    far_rest_kernel(tab, a, dinv, t_high, t_low, far_1, far_0, far)


def wide(ref, *places):
    return jnp.concatenate([ref[place] for place in places], axis=0)


def store_turned(trans, side, label, place, value):
    block = value.shape[0]
    trans[side, pl.ds(pl.multiple_of(label * block, block), block), place] = value.T
    trans[side, pl.ds(pl.multiple_of((1 - label) * block, block), block), place] = jnp.zeros_like(value)


def pre_kernel(
    tab, a, own, far,
    part, a_high, a_low, trans_high, trans_low,
    own_high, own_low, below_high, below_low, above_high, above_low,
):
    rows, block = own.shape[0], own.shape[1]
    half = 2 * block
    for u in range(rows):
        own_high[u], own_low[u] = split(own[u])
        place = slice(u * block, (u + 1) * block)
        for side, high_ref, low_ref in ((BELOW, below_high, below_low), (ABOVE, above_high, above_low)):
            label = tab[OWN_LAB + 4 * u + 2 + side]
            high, low = split(far[u, :, side * block : (side + 1) * block])
            high_ref[u] = two_columns(high, label)
            low_ref[u] = two_columns(low, label)
            store_turned(trans_high, side, label, place, high)
            store_turned(trans_low, side, label, place, low)
    pairs = ((below_high, below_low), (own_high, own_low), (above_high, above_low))
    for u in range(rows):
        row, near = tab[ROW + u], tab[NEAR + u]
        a01 = split(jnp.concatenate([a[row, 0], a[row, 1]], axis=1))
        a_high[u], a_low[u] = split(jnp.concatenate([a[row, 2], a[row, 3]], axis=1))
        for c, (high, low) in enumerate(pairs):
            part[u, :, c * half : (c + 1) * half] = dot3(*a01, wide(high, u, near), wide(low, u, near))


def coarse_rows(trans_high, trans_low, ap_high, ap_low, which, out):
    half = trans_high.shape[1]
    for c in range(ap_high.shape[1] // half):
        cols = slice(c * half, (c + 1) * half)
        out[:, cols] = dot3(trans_high[which], trans_low[which], ap_high[:, cols], ap_low[:, cols])


def first_kernel(
    tab, a_high, a_low, part, trans_high, trans_low, near_0, near_1,
    ap_high, ap_low, out_1,
    p_high, p_low,
):
    rows, block = a_high.shape[0], a_high.shape[1]
    half = 2 * block
    side = pair_side()
    for j in range(rows // 2):
        p_high[side, j], p_low[side, j] = split(near_0[j])
        p_high[1 - side, j], p_low[1 - side, j] = split(near_1[j])
    for u in range(rows):
        pos2, pos3 = tab[POS2 + u], tab[POS3 + u]
        a2 = a_high[u, :, :block], a_low[u, :, :block]
        a3 = a_high[u, :, block:], a_low[u, :, block:]
        low = part[u, :, :half] + dot3k(*a2, p_high[BELOW, pos2], p_low[BELOW, pos2])
        upp = part[u, :, 2 * half :] + dot3k(*a3, p_high[ABOVE, pos3], p_low[ABOVE, pos3])
        place = slice(u * block, (u + 1) * block)
        ap_high[place, :half], ap_low[place, :half] = split(low)
        ap_high[place, half:], ap_low[place, half:] = split(upp)
    coarse_rows(trans_high, trans_low, ap_high, ap_low, 1 - side, out_1)


def second_kernel(
    tab, a_high, a_low, part, trans_high, trans_low, far_0, far_1, after,
    ap_high, ap_low, out_1,
    p_high, p_low,
):
    rows, block = a_high.shape[0], a_high.shape[1]
    half = 2 * block
    side = pair_side()
    for j in range(rows // 2):
        p_high[side, j], p_low[side, j] = split(far_0[j])
        p_high[1 - side, j], p_low[1 - side, j] = split(far_1[j])
    for u in range(rows):
        pos2, pos3 = tab[POS2 + u], tab[POS3 + u]
        a2 = a_high[u, :, :block], a_low[u, :, :block]
        a3 = a_high[u, :, block:], a_low[u, :, block:]
        left = dot3k(*a2, p_high[BELOW, pos2], p_low[BELOW, pos2])
        right = dot3k(*a3, p_high[ABOVE, pos3], p_low[ABOVE, pos3])
        labels = [tab[SIDE_LAB + 8 * which + 2 * pos + k] for which, pos in ((BELOW, pos2), (ABOVE, pos3)) for k in (0, 1)]
        own = part[u, :, half : 2 * half] + two_columns(left[:, block:], labels[1]) + two_columns(right[:, :block], labels[2])
        place = slice(u * block, (u + 1) * block)
        ap_high[place, half : 2 * half], ap_low[place, half : 2 * half] = split(own)
        for cols, value, label in (
            (slice(0, half), left[:, :block], labels[0]),
            (slice(2 * half, 3 * half), right[:, block:], labels[3]),
        ):
            high, low = split(value)
            ap_high[place, cols] = two_columns(high, label)
            ap_low[place, cols] = two_columns(low, label)
    coarse_rows(trans_high, trans_low, ap_high, ap_low, 1 - side, out_1)


def other_kernel(trans_high, trans_low, ap_high, ap_low, out_0):
    coarse_rows(trans_high, trans_low, ap_high, ap_low, pair_side(), out_0)


HELD = ((1, 0), (0, 0), (1, 1), (0, 1), (1, 2))


def own_kernel(own, ap1_high, ap1_low, ap2_high, ap2_low, out, trans_high, trans_low):
    rows, block = own.shape[0], own.shape[1]
    half = 2 * block
    for u in range(rows):
        place = slice(u * block, (u + 1) * block)
        high, low = split(own[u])
        trans_high[:, place] = high.T
        trans_low[:, place] = low.T
    aps = (ap1_high, ap1_low), (ap2_high, ap2_low)
    for d, (which, c) in enumerate(HELD):
        cols = slice(c * half, (c + 1) * half)
        high, low = aps[which]
        out[:, d * half : (d + 1) * half] = dot3(trans_high[...], trans_low[...], high[:, cols], low[:, cols])


def write_slots(inv, total, result, agg, d, out, sem):
    block = total.shape[0]
    value = dot3k(*inv, *split(total))
    result[0] = value[:, :block]
    result[1] = value[:, block:]
    copy = pltpu.make_async_copy(result, out.at[agg, pl.ds(2 * (d + 3), 2)], sem)
    copy.start()
    return copy


def both_sides(run):
    side = pair_side()
    pl.when(side == ABOVE)(lambda: run(ABOVE))
    pl.when(side == BELOW)(lambda: run(BELOW))


def early_kernel(inverse, own, first_0, first_1, second_0, out, waiting, results, sems):
    block = inverse.shape[1]
    half = 2 * block

    def run(side):
        shift_0, shift_1 = (1, -1) if side == ABOVE else (-1, 1)
        copies = []
        for agg in range(2):
            inv = split(inverse[agg])
            line = slice(agg * block, (agg + 1) * block)
            for d in range(-3, 4):
                total = None
                if -2 <= d <= 2:
                    total = own[line, (d + 2) * half : (d + 3) * half]
                late = None
                for shift, bufs in ((shift_0, (first_0, second_0)), (shift_1, (first_1, None))):
                    if -2 <= d - shift <= 2:
                        which, c = HELD[d - shift + 2]
                        if bufs[which] is None:
                            late = c
                            continue
                        part = bufs[which][line, c * half : (c + 1) * half]
                        total = part if total is None else total + part
                if late is not None:
                    waiting[agg, late] = jnp.zeros((block, half), F32) if total is None else total
                else:
                    n = len(copies)
                    copies.append(write_slots(inv, total, results.at[n], agg, d, out, sems.at[n]))
        for copy in copies:
            copy.wait()

    both_sides(run)


def late_kernel(inverse, waiting, second_1, partly, out, results, sems):
    block = inverse.shape[1]
    half = 2 * block

    def run(side):
        shift = -1 if side == ABOVE else 1
        copies = []
        for agg in range(2):
            inv = split(inverse[agg])
            line = slice(agg * block, (agg + 1) * block)
            for c in range(3):
                total = waiting[agg, c] + second_1[line, c * half : (c + 1) * half]
                n = len(copies)
                copies.append(write_slots(inv, total, results.at[n], agg, 2 * c - 2 + shift, out, sems.at[n]))
        for copy in copies:
            copy.wait()

    both_sides(run)


SMEM = pl.BlockSpec(memory_space=pltpu.SMEM)
VMEM = pl.BlockSpec(memory_space=pltpu.VMEM)
HBM = pl.BlockSpec(memory_space=pltpu.HBM)


def call(body, outs, ins, scratch=(), micros=1.0, in_hbm=(), out_hbm=(), aliases={}):
    def specs(values, in_place):
        return [HBM if i in in_place else SMEM if x.dtype == jnp.int32 else VMEM for i, x in enumerate(values)]

    return pl.pallas_call(
        body,
        out_shape=outs,
        in_specs=specs(ins, in_hbm),
        out_specs=specs(outs, out_hbm),
        scratch_shapes=[pltpu.VMEM(*x) if isinstance(x, tuple) else x for x in scratch],
        input_output_aliases=aliases,
        compiler_params=pltpu.CompilerParams(vmem_limit_bytes=24 * 2**20),
        cost_estimate=pl.CostEstimate(flops=int(micros * 1e9), bytes_accessed=2**20, transcendentals=0),
    )(*ins)


def shards(a, a_cols, t_blocks, t_agg, dinv, coarse_inv):
    devices = lax.axis_size(AXES)
    rows, block = t_blocks.shape[:2]
    width, half, deep = rows // 2, 2 * block, rows * block
    shape = jax.ShapeDtypeStruct
    full = lambda *dims: shape(dims, F32)
    pair = lambda *dims: [shape(dims, BF16), shape(dims, BF16)]
    two = lambda *dims: [(dims, BF16)] * 2
    tile = full(width, block, half)
    cols = a_cols.reshape(-1, ROW_CHUNK, 4).transpose(0, 2, 1).reshape(-1)

    tab, t_0, t_1, t = call(
        functools.partial(load_kernel, devices),
        [shape((TAB,), jnp.int32)] + [full(width, block, block)] * 2 + [full(*t_blocks.shape)],
        [pltpu.with_memory_space_constraint(x, pltpu.HBM) for x in (cols, t_agg, t_blocks)],
        [pltpu.SMEM(cols.shape, jnp.int32), pltpu.SMEM(t_agg.shape, jnp.int32), pltpu.SemaphoreType.DMA((3,))],
        micros=3,
        in_hbm=(0, 1, 2),
    )
    t_1 = exchanged(t_1, 1)
    t_0 = exchanged(t_0, 0)
    (near_1,) = call(near_sent_kernel, [tile], [tab, a, t, dinv], micros=2)
    got_near_1 = exchanged(near_1, 1)
    near_0, own = call(near_rest_kernel, [tile, full(rows, block, half)], [tab, a, t, dinv, near_1], micros=2)
    near_0, near_1 = exchanged(near_0, 0), got_near_1
    (far_1,) = call(far_sent_kernel, [tile], [tab, a, dinv, t_0, t_1, own], two(2, width, block, block), micros=2)
    got_far_1 = exchanged(far_1, 1)
    far_0, far = call(
        far_split_kernel,
        [tile, full(rows, block, half)],
        [tab, a, dinv, t_0, t_1, far_1],
        two(2, width, block, block),
        micros=2,
    )
    far_0, far_1 = exchanged(far_0, 0), got_far_1
    part, a23_high, a23_low, side_high, side_low = call(
        pre_kernel,
        [full(rows, block, 3 * half)] + pair(rows, block, half) + pair(2, half, deep),
        [tab, a, own, far],
        two(rows, block, half) * 3,
        micros=3,
    )
    ap1_high, ap1_low, first_1 = call(
        first_kernel,
        pair(deep, 2 * half) + [full(half, 2 * half)],
        [tab, a23_high, a23_low, part, side_high, side_low, near_0, near_1],
        two(2, width, block, half),
        micros=3,
    )
    first_1 = exchanged(first_1, 1)
    (first_0,) = call(other_kernel, [full(half, 2 * half)], [side_high, side_low, ap1_high, ap1_low], micros=1)
    first_0 = exchanged(first_0, 0)
    ap2_high, ap2_low, second_1 = call(
        second_kernel,
        pair(deep, 3 * half) + [full(half, 3 * half)],
        [tab, a23_high, a23_low, part, side_high, side_low, far_0, far_1, ap1_high],
        two(2, width, block, half),
        micros=3,
    )
    second_1 = exchanged(second_1, 1)
    (second_0,) = call(other_kernel, [full(half, 3 * half)], [side_high, side_low, ap2_high, ap2_low], micros=1)
    second_0 = exchanged(second_0, 0)
    (total,) = call(
        own_kernel, [full(half, 5 * half)], [own, ap1_high, ap1_low, ap2_high, ap2_low], two(half, deep), micros=2
    )
    result = full(2, 14, block, block)
    partly, waiting = call(
        early_kernel,
        [result, full(2, 3, block, half)],
        [coarse_inv, total, first_0, first_1, second_0],
        [((8, 2, block, block), F32), pltpu.SemaphoreType.DMA((8,))],
        micros=2,
        out_hbm=(0,),
    )
    (out,) = call(
        late_kernel,
        [result],
        [coarse_inv, waiting, second_1, partly],
        [((6, 2, block, block), F32), pltpu.SemaphoreType.DMA((6,))],
        micros=1,
        in_hbm=(3,),
        out_hbm=(0,),
        aliases={3: 0},
    )
    return out


def solution(mesh):
    placed = (
        P(AXES, None, None, None),
        P(),
        P(AXES, None, None),
        P(),
        P(AXES, None, None),
        P(AXES, None, None),
    )
    return jax.shard_map(
        shards,
        mesh=mesh,
        in_specs=placed,
        out_specs=P(AXES, None, None, None),
        check_vma=False,
    )
```

time: 63.5 us -> 62.5 us (0.984)
  waiting for transfers between devices: 16.5 us -> 13.8 us
  Pallas kernels: 21.9 us -> 24.1 us
  starting transfers between devices: 24.9 us -> 24.2 us
    ppermute x10, waiting for transfers between devices: 16.5 us -> 13.8 us  [exchanged(): return lax.ppermute(value, AXES, pairs)]
    pallas_call x8 -> x13, Pallas kernels: 21.9 us -> 24.1 us  [call(): pl.pallas_call(body, out_shape=outs, in_specs=specs(ins, in_hbm), out_spe...]
    ppermute x10, starting transfers between devices: 24.9 us -> 24.2 us  [exchanged(): return lax.ppermute(value, AXES, pairs)]
  transfers between devices with their start and end apart: 10 -> 10, of which waited for: 4 -> 3; matrix products, arithmetic and copies ran while one was open for 0% -> 0% of each run, Pallas kernels for 20% -> 26%
where the time goes in v3:
time: 62.5 us; the launch traced here: 62.4 us
  starting transfers between devices  24.2 us (39%)
  Pallas kernels  24.1 us (39%)
  waiting for transfers between devices  13.8 us (22%)
    ppermute x10, starting transfers between devices, exchanged(): return lax.ppermute(value, AXES, pairs)  24.2 us
    pallas_call x13, Pallas kernels, call(): pl.pallas_call(body, out_shape=outs, in_specs=specs(ins, in_hbm), out_spe...  24.1 us
    ppermute x10, waiting for transfers between devices, exchanged(): return lax.ppermute(value, AXES, pairs)  13.8 us
  transfers between devices with their start and end apart: 10, of which 3 were waited for; matrix products, arithmetic and copies ran while one was open for 0% of the time, Pallas kernels for 26%

profile of v3, /device:TPU:0, one launch (start us, length us, event | category | flops | bytes accessed | tf_op | source)
XLA Modules:
  0.0 62.4 jit_solution(3733148761032085721)
XLA Ops:
  0.0 2.5 %shard_map.64 = (s32[128]{0:T(128)S(1)}, f32[4,128,128]{2,1,0:T(8,128)S(1)}, f32[4,128,128]{2,1,0:T(8,128)S(1)}, f32[8,128,128]{2,1,0:T(8,128)S(1)}) custom-call(s32[4096]{0:T(1024)} %bitcast.5, s32[1024]{0:T(1024)} %agg_hbm.1, f32[8,128,128]{2,1,0:T(8,128)} %t_hbm.1), custom_call_target="tpu_custom_call" | custom-call | flops 3000000000 | bytes 1048576 | tf_op jit(solution)/shard_map/pallas_call | solution.py:401
  2.6 0.1 collective-permute-start
  2.6 8.9 %collective-permute-start.1 = (f32[4,128,128]{2,1,0:T(8,128)S(1)}, f32[4,128,128]{2,1,0:T(8,128)S(1)}, u32[]{:S(2)}, u32[]{:S(2)}) collective-permute-start(f32[4,128,128]{2,1,0:T(8,128)S(1)} %get-tuple-element.30), channel_id=1, source_target_pairs={{1,2},{2,1},{3,4},{4,3},{5,6},{6,5},{7,8},{8,7},{9,10},{10,9},{11,... | collective-permute-start | bytes 786440 | tf_op jit(solution)/shard_map/ppermute | solution.py:26
  11.5 1.6 %shard_map.65.near_1 = f32[4,128,256]{2,1,0:T(8,128)S(1)} custom-call(s32[128]{0:T(128)S(1)} %get-tuple-element.26.tab, f32[8,4,128,128]{3,2,1,0:T(8,128)S(1)} %copy-done.1, f32[8,128,128]{2,1,0:T(8,128)S(1)} %get-tuple-element.27.t, f32[8,128,128]{2,1,0:T(8,128)S(1)} %copy-done.2), custom_call_target="tpu_custom_call" | custom-call | flops 2000000000 | bytes 1048576 | tf_op jit(solution)/shard_map/pallas_call | solution.py:401
  13.2 0.1 collective-permute-start.3
  13.2 1.6 %shard_map.66 = (f32[4,128,256]{2,1,0:T(8,128)S(1)}, f32[8,128,256]{2,1,0:T(8,128)S(1)}) custom-call(s32[128]{0:T(128)S(1)} %get-tuple-element.26.tab, f32[8,4,128,128]{3,2,1,0:T(8,128)S(1)} %copy-done.1, f32[8,128,128]{2,1,0:T(8,128)S(1)} %get-tuple-element.27.t, f32[8,128,128]{2,1,0:T(8,128)S(1)} %copy-done.2, f32[4,128,256]{2,1,0:T(8,128)S(1)} %shard_map.65.near_1), custom_call_target="tpu_custom_call" | custom-call | flops 2000000000 | bytes 1048576 | tf_op jit(solution)/shard_map/pallas_call | solution.py:401
  14.9 0.1 collective-permute-start.2
  15.0 0.0 collective-permute-done.t_0
  15.0 0.6 collective-permute-done.1.t_1
  15.6 1.7 %shard_map.67.far_1 = f32[4,128,256]{2,1,0:T(8,128)S(1)} custom-call(s32[128]{0:T(128)S(1)} %get-tuple-element.26.tab, f32[8,4,128,128]{3,2,1,0:T(8,128)S(1)} %copy-done.1, f32[8,128,128]{2,1,0:T(8,128)S(1)} %copy-done.2, f32[4,128,128]{2,1,0:T(8,128)S(1)} %collective-permute-done.t_0, f32[4,128,128]{2,1,0:T(8,128)S(1)} %collective-permute-done.1.t_1, ...), custom_call_target="tpu_custom_call" | custom-call | flops 2000000000 | bytes 1048576 | tf_op jit(solution)/shard_map/pallas_call | solution.py:401
  17.3 7.3 %collective-permute-start.5 = (f32[4,128,256]{2,1,0:T(8,128)S(1)}, f32[4,128,256]{2,1,0:T(8,128)S(1)}, u32[]{:S(2)}, u32[]{:S(2)}) collective-permute-start(f32[4,128,256]{2,1,0:T(8,128)S(1)} %shard_map.67.far_1), channel_id=1, source_target_pairs={{1,2},{2,1},{3,4},{4,3},{5,6},{6,5},{7,8},{8,7},{9,10},{10,9},{11,... | collective-permute-start | bytes 1572872 | tf_op jit(solution)/shard_map/ppermute | solution.py:26
  24.5 1.7 %shard_map.68 = (f32[4,128,256]{2,1,0:T(8,128)S(1)}, f32[8,128,256]{2,1,0:T(8,128)S(1)}) custom-call(s32[128]{0:T(128)S(1)} %get-tuple-element.26.tab, f32[8,4,128,128]{3,2,1,0:T(8,128)S(1)} %copy-done.1, f32[8,128,128]{2,1,0:T(8,128)S(1)} %copy-done.2, f32[4,128,128]{2,1,0:T(8,128)S(1)} %collective-permute-done.t_0, ...), custom_call_target="tpu_custom_call" | custom-call | flops 2000000000 | bytes 1048576 | tf_op jit(solution)/shard_map/pallas_call | solution.py:401
  26.2 0.3 collective-permute-start.4
  26.5 2.7 %shard_map.69 = (f32[8,128,768]{2,1,0:T(8,128)S(1)}, bf16[8,128,256]{2,1,0:T(8,128)(2,1)S(1)}, bf16[8,128,256]{2,1,0:T(8,128)(2,1)S(1)}, bf16[2,256,1024]{2,1,0:T(8,128)(2,1)S(1)}, bf16[2,256,1024]{2,1,0:T(8,128)(2,1)S(1)}) custom-call(s32[128]{0:T(128)S(1)} %get-tuple-element.26.tab, f32[8,4,128,128]{3,2,1,0:T(8,128)S(1)} %copy-done.1, ...), custom_call_target="tpu_custom_call" | custom-call | flops 3000000000 | bytes 1048576 | tf_op jit(solution)/shard_map/pallas_call | solution.py:401
  29.2 0.0 collective-permute-done.3.near_1
  29.2 2.3 %shard_map.70 = (bf16[1024,512]{1,0:T(8,128)(2,1)S(1)}, bf16[1024,512]{1,0:T(8,128)(2,1)S(1)}, f32[256,512]{1,0:T(8,128)S(1)}) custom-call(s32[128]{0:T(128)S(1)} %get-tuple-element.26.tab, bf16[8,128,256]{2,1,0:T(8,128)(2,1)S(1)} %get-tuple-element.32.a_high, bf16[8,128,256]{2,1,0:T(8,128)(2,1)S(1)} %get-tuple-element.33.a_low, ...), custom_call_target="tpu_custom_call" | custom-call | flops 3000000000 | bytes 1048576 | tf_op jit(solution)/shard_map/pallas_call | solution.py:401
  31.5 1.4 %collective-permute-done.5.far_1 = f32[4,128,256]{2,1,0:T(8,128)S(1)} collective-permute-done((f32[4,128,256]{2,1,0:T(8,128)S(1)}, f32[4,128,256]{2,1,0:T(8,128)S(1)}, u32[]{:S(2)}, u32[]{:S(2)}) %collective-permute-start.5) | collective-permute-done | bytes 524320 | tf_op jit(solution)/shard_map/ppermute | solution.py:26
  32.9 2.8 %shard_map.71 = (bf16[1024,768]{1,0:T(8,128)(2,1)S(1)}, bf16[1024,768]{1,0:T(8,128)(2,1)S(1)}, f32[256,768]{1,0:T(8,128)S(1)}) custom-call(s32[128]{0:T(128)S(1)} %get-tuple-element.26.tab, bf16[8,128,256]{2,1,0:T(8,128)(2,1)S(1)} %get-tuple-element.32.a_high, bf16[8,128,256]{2,1,0:T(8,128)(2,1)S(1)} %get-tuple-element.33.a_low, ...), custom_call_target="tpu_custom_call" | custom-call | flops 3000000000 | bytes 1048576 | tf_op jit(solution)/shard_map/pallas_call | solution.py:401
  35.7 1.4 %shard_map.74 = f32[256,768]{1,0:T(8,128)S(1)} custom-call(bf16[2,256,1024]{2,1,0:T(8,128)(2,1)S(1)} %get-tuple-element.35.trans_high, bf16[2,256,1024]{2,1,0:T(8,128)(2,1)S(1)} %get-tuple-element.36.trans_low, bf16[1024,768]{1,0:T(8,128)(2,1)S(1)} %get-tuple-element.41.ap2_high.ap_high, bf16[1024,768]{1,0:T(8,128)(2,1)S(1)} %get-tuple-element.42.ap2_low.ap_low), custom_call_target="tpu_custom_call" | custom-call | flops 1000000000 | bytes 1048576 | tf_op jit(solution)/shard_map/pallas_call | solution.py:401
  37.1 0.1 collective-permute-start.8
  37.2 5.7 %collective-permute-start.9 = (f32[256,768]{1,0:T(8,128)S(1)}, f32[256,768]{1,0:T(8,128)S(1)}, u32[]{:S(2)}, u32[]{:S(2)}) collective-permute-start(f32[256,768]{1,0:T(8,128)S(1)} %get-tuple-element.45), channel_id=1, source_target_pairs={{1,2},{2,1},{3,4},{4,3},{5,6},{6,5},{7,8},{8,7},{9,10},{10,9},{11,... | collective-permute-start | bytes 2359304 | tf_op jit(solution)/shard_map/ppermute | solution.py:26
  42.9 1.0 %shard_map.73 = f32[256,512]{1,0:T(8,128)S(1)} custom-call(bf16[2,256,1024]{2,1,0:T(8,128)(2,1)S(1)} %get-tuple-element.35.trans_high, bf16[2,256,1024]{2,1,0:T(8,128)(2,1)S(1)} %get-tuple-element.36.trans_low, bf16[1024,512]{1,0:T(8,128)(2,1)S(1)} %get-tuple-element.38.after.ap1_high.ap_high, bf16[1024,512]{1,0:T(8,128)(2,1)S(1)} %get-tuple-element.39.ap1_low.ap_low), custom_call_target="tpu_custom_call" | custom-call | flops 1000000000 | bytes 1048576 | tf_op jit(solution)/shard_map/pallas_call | solution.py:401
  43.9 0.1 collective-permute-start.6
  44.0 0.0 copy-start
  44.0 1.6 %collective-permute-start.7 = (f32[256,512]{1,0:T(8,128)S(1)}, f32[256,512]{1,0:T(8,128)S(1)}, u32[]{:S(2)}, u32[]{:S(2)}) collective-permute-start(f32[256,512]{1,0:T(8,128)S(1)} %get-tuple-element.43), channel_id=1, source_target_pairs={{1,2},{2,1},{3,4},{4,3},{5,6},{6,5},{7,8},{8,7},{9,10},{10,9},{11,... | collective-permute-start | bytes 1572872 | tf_op jit(solution)/shard_map/ppermute | solution.py:26
  45.6 2.4 %shard_map.72.own = f32[256,1280]{1,0:T(8,128)S(1)} custom-call(f32[8,128,256]{2,1,0:T(8,128)S(1)} %get-tuple-element.28.after.own, bf16[1024,512]{1,0:T(8,128)(2,1)S(1)} %get-tuple-element.38.after.ap1_high.ap_high, bf16[1024,512]{1,0:T(8,128)(2,1)S(1)} %get-tuple-element.39.ap1_low.ap_low, bf16[1024,768]{1,0:T(8,128)(2,1)S(1)} %get-tuple-element.41.ap2_high.ap_high, ...), custom_call_target="tpu_custom_call" | custom-call | flops 2000000000 | bytes 1048576 | tf_op jit(solution)/shard_map/pallas_call | solution.py:401
  48.0 0.0 collective-permute-done.6.first_0
  48.0 11.7 %collective-permute-done.7.first_1 = f32[256,512]{1,0:T(8,128)S(1)} collective-permute-done((f32[256,512]{1,0:T(8,128)S(1)}, f32[256,512]{1,0:T(8,128)S(1)}, u32[]{:S(2)}, u32[]{:S(2)}) %collective-permute-start.7) | collective-permute-done | bytes 524320 | tf_op jit(solution)/shard_map/ppermute | solution.py:26
  59.7 0.0 collective-permute-done.8.second_0
  59.7 1.4 %shard_map.75 = (f32[2,14,128,128]{3,2,1,0:T(8,128)}, f32[2,3,128,256]{3,2,1,0:T(8,128)S(1)}) custom-call(f32[2,128,128]{2,1,0:T(8,128)S(1)} %copy-done, f32[256,1280]{1,0:T(8,128)S(1)} %shard_map.72.own, f32[256,512]{1,0:T(8,128)S(1)} %collective-permute-done.6.first_0, f32[256,512]{1,0:T(8,128)S(1)} %collective-permute-done.7.first_1, ...), custom_call_target="tpu_custom_call" | custom-call | flops 2000000000 | bytes 1048576 | tf_op jit(solution)/shard_map/pallas_call | solution.py:401
  61.1 0.0 collective-permute-done.9.second_1
  61.1 1.2 %shard_map.76 = f32[2,14,128,128]{3,2,1,0:T(8,128)} custom-call(f32[2,128,128]{2,1,0:T(8,128)S(1)} %copy-done, f32[2,3,128,256]{3,2,1,0:T(8,128)S(1)} %get-tuple-element.44.waiting, f32[256,768]{1,0:T(8,128)S(1)} %collective-permute-done.9.second_1, f32[2,14,128,128]{3,2,1,0:T(8,128)} %get-tuple-element.46.partly), custom_call_target="tpu_custom_call", output_to_operand_aliasing={{}: (3, {})} | custom-call | flops 1000000000 | bytes 1048576 | tf_op jit(solution)/shard_map/pallas_call | solution.py:401
  (7 shorter events, 0.0 us)
Async XLA Ops:
  0.0 11.5 %copy-start.1 = (f32[8,4,128,128]{3,2,1,0:T(8,128)S(1)}, f32[8,4,128,128]{3,2,1,0:T(8,128)}, u32[]{:S(2)}) copy-start(f32[8,4,128,128]{3,2,1,0:T(8,128)} %a.9) | copy-start | bytes 6291460
  0.0 11.5 %copy-start.2 = (f32[8,128,128]{2,1,0:T(8,128)S(1)}, f32[8,128,128]{2,1,0:T(8,128)}, u32[]{:S(2)}) copy-start(f32[8,128,128]{2,1,0:T(8,128)} %dinv.7) | copy-start | bytes 1572868
  2.6 12.4 %collective-permute-start = (f32[4,128,128]{2,1,0:T(8,128)S(1)}, f32[4,128,128]{2,1,0:T(8,128)S(1)}, u32[]{:S(2)}, u32[]{:S(2)}) collective-permute-start(f32[4,128,128]{2,1,0:T(8,128)S(1)} %get-tuple-element.29), channel_id=1, source_target_pairs={{0,1},{1,0},{2,3},{3,2},{4,5},{5,4},{6,7},{7,6},{8,9},{9,8},{10,11... | collective-permute-start | bytes 786440 | tf_op jit(solution)/shard_map/ppermute | solution.py:26
  2.6 12.9 %collective-permute-start.1 = (f32[4,128,128]{2,1,0:T(8,128)S(1)}, f32[4,128,128]{2,1,0:T(8,128)S(1)}, u32[]{:S(2)}, u32[]{:S(2)}) collective-permute-start(f32[4,128,128]{2,1,0:T(8,128)S(1)} %get-tuple-element.30), channel_id=1, source_target_pairs={{1,2},{2,1},{3,4},{4,3},{5,6},{6,5},{7,8},{8,7},{9,10},{10,9},{11,... | collective-permute-start | bytes 786440 | tf_op jit(solution)/shard_map/ppermute | solution.py:26
  13.2 16.0 %collective-permute-start.3 = (f32[4,128,256]{2,1,0:T(8,128)S(1)}, f32[4,128,256]{2,1,0:T(8,128)S(1)}, u32[]{:S(2)}, u32[]{:S(2)}) collective-permute-start(f32[4,128,256]{2,1,0:T(8,128)S(1)} %shard_map.65.near_1), channel_id=1, source_target_pairs={{1,2},{2,1},{3,4},{4,3},{5,6},{6,5},{7,8},{8,7},{9,10},{10,9},{11,... | collective-permute-start | bytes 1572872 | tf_op jit(solution)/shard_map/ppermute | solution.py:26
  14.9 14.3 %collective-permute-start.2 = (f32[4,128,256]{2,1,0:T(8,128)S(1)}, f32[4,128,256]{2,1,0:T(8,128)S(1)}, u32[]{:S(2)}, u32[]{:S(2)}) collective-permute-start(f32[4,128,256]{2,1,0:T(8,128)S(1)} %get-tuple-element.37), channel_id=1, source_target_pairs={{0,1},{1,0},{2,3},{3,2},{4,5},{5,4},{6,7},{7,6},{8,9},{9,8},{10,11... | collective-permute-start | bytes 1572872 | tf_op jit(solution)/shard_map/ppermute | solution.py:26
  17.3 15.6 %collective-permute-start.5 = (f32[4,128,256]{2,1,0:T(8,128)S(1)}, f32[4,128,256]{2,1,0:T(8,128)S(1)}, u32[]{:S(2)}, u32[]{:S(2)}) collective-permute-start(f32[4,128,256]{2,1,0:T(8,128)S(1)} %shard_map.67.far_1), channel_id=1, source_target_pairs={{1,2},{2,1},{3,4},{4,3},{5,6},{6,5},{7,8},{8,7},{9,10},{10,9},{11,... | collective-permute-start | bytes 1572872 | tf_op jit(solution)/shard_map/ppermute | solution.py:26
  26.2 6.7 %collective-permute-start.4 = (f32[4,128,256]{2,1,0:T(8,128)S(1)}, f32[4,128,256]{2,1,0:T(8,128)S(1)}, u32[]{:S(2)}, u32[]{:S(2)}) collective-permute-start(f32[4,128,256]{2,1,0:T(8,128)S(1)} %get-tuple-element.40), channel_id=1, source_target_pairs={{0,1},{1,0},{2,3},{3,2},{4,5},{5,4},{6,7},{7,6},{8,9},{9,8},{10,11... | collective-permute-start | bytes 1572872 | tf_op jit(solution)/shard_map/ppermute | solution.py:26
  37.1 22.6 %collective-permute-start.8 = (f32[256,768]{1,0:T(8,128)S(1)}, f32[256,768]{1,0:T(8,128)S(1)}, u32[]{:S(2)}, u32[]{:S(2)}) collective-permute-start(f32[256,768]{1,0:T(8,128)S(1)} %shard_map.74), channel_id=1, source_target_pairs={{0,1},{1,0},{2,3},{3,2},{4,5},{5,4},{6,7},{7,6},{8,9},{9,8},{10,11... | collective-permute-start | bytes 2359304 | tf_op jit(solution)/shard_map/ppermute | solution.py:26
  37.2 23.9 %collective-permute-start.9 = (f32[256,768]{1,0:T(8,128)S(1)}, f32[256,768]{1,0:T(8,128)S(1)}, u32[]{:S(2)}, u32[]{:S(2)}) collective-permute-start(f32[256,768]{1,0:T(8,128)S(1)} %get-tuple-element.45), channel_id=1, source_target_pairs={{1,2},{2,1},{3,4},{4,3},{5,6},{6,5},{7,8},{8,7},{9,10},{10,9},{11,... | collective-permute-start | bytes 2359304 | tf_op jit(solution)/shard_map/ppermute | solution.py:26
  43.9 4.1 %collective-permute-start.6 = (f32[256,512]{1,0:T(8,128)S(1)}, f32[256,512]{1,0:T(8,128)S(1)}, u32[]{:S(2)}, u32[]{:S(2)}) collective-permute-start(f32[256,512]{1,0:T(8,128)S(1)} %shard_map.73), channel_id=1, source_target_pairs={{0,1},{1,0},{2,3},{3,2},{4,5},{5,4},{6,7},{7,6},{8,9},{9,8},{10,11... | collective-permute-start | bytes 1572872 | tf_op jit(solution)/shard_map/ppermute | solution.py:26
  44.0 15.7 %copy-start = (f32[2,128,128]{2,1,0:T(8,128)S(1)}, f32[2,128,128]{2,1,0:T(8,128)}, u32[]{:S(2)}) copy-start(f32[2,128,128]{2,1,0:T(8,128)} %inverse.3) | copy-start | bytes 393220
  44.0 15.7 %collective-permute-start.7 = (f32[256,512]{1,0:T(8,128)S(1)}, f32[256,512]{1,0:T(8,128)S(1)}, u32[]{:S(2)}, u32[]{:S(2)}) collective-permute-start(f32[256,512]{1,0:T(8,128)S(1)} %get-tuple-element.43), channel_id=1, source_target_pairs={{1,2},{2,1},{3,4},{4,3},{5,6},{6,5},{7,8},{8,7},{9,10},{10,9},{11,... | collective-permute-start | bytes 1572872 | tf_op jit(solution)/shard_map/ppermute | solution.py:26

commit v4 on v3

v4 whole, which is shorter than its diff:
```python
import functools

import jax
import jax.numpy as jnp
from jax import lax
from jax.experimental import pallas as pl
from jax.experimental.pallas import tpu as pltpu
from jax.sharding import PartitionSpec as P


OMEGA = 0.6
AXES = ("gx", "gy")
F32 = jnp.float32
BF16 = jnp.bfloat16
ROW, NEAR, POS2, POS3, LIST_0, OWN_LAB, SIDE_LAB, TAB = 0, 8, 16, 24, 32, 48, 80, 128
BELOW, ABOVE = 0, 1
ROW_CHUNK = 128


def exchanged(value, first):
    count = lax.axis_size(AXES)
    pairs = []
    for low in range(first, count + first, 2):
        high = (low + 1) % count
        pairs += [(low, high), (high, low)]
    return lax.ppermute(value, AXES, pairs)


def pair_side():
    return 1 - lax.rem(lax.axis_index("gy"), 2)


def split(x):
    high = x.astype(BF16)
    return high, (x - high.astype(F32)).astype(BF16)


def dot(a, b):
    return jnp.dot(a, b, preferred_element_type=F32)


def dot3(a_high, a_low, b_high, b_low):
    return dot(a_high, b_high) + dot(a_low, b_high) + dot(a_high, b_low)


def dot3k(a_high, a_low, b_high, b_low):
    both = jnp.concatenate([a_high, a_low], axis=1)
    return dot(both, jnp.concatenate([b_high, b_high], axis=0)) + dot(a_high, b_low)


def load_kernel(devices, cols_hbm, agg_hbm, t_hbm, tab, t_0, t_1, t, cols, agg, rank, sem):
    rows, width = t.shape[0], t.shape[0] // 2
    device = lax.axis_index("gx") * lax.axis_size("gy") + lax.axis_index("gy")
    previous = lax.rem(device + devices - 1, devices)
    following = lax.rem(device + 1, devices)
    slabs = previous, following, device
    side = pair_side()
    shift = ROW_CHUNK.bit_length() - 1
    chunk = 4 * ROW_CHUNK
    copies = [
        pltpu.make_async_copy(
            cols_hbm.at[pl.ds(pl.multiple_of(((slab * rows) >> shift) * chunk, chunk), chunk)],
            cols.at[pl.ds(i * chunk, chunk)],
            sem.at[i],
        )
        for i, slab in enumerate(slabs)
    ]
    copies += [pltpu.make_async_copy(t_hbm, t, sem.at[3]), pltpu.make_async_copy(agg_hbm, agg, sem.at[4])]
    for copy in copies:
        copy.start()

    def col(i, r, k):
        return cols[i * chunk + k * ROW_CHUNK + ((slabs[i] * rows) & (ROW_CHUNK - 1)) + r]

    def rank_rows(i, k, where):
        mask = jnp.int32(0)
        for r in range(rows):
            mask = mask | (jnp.int32(1) << (col(i, r, k) & (rows - 1)))
        named, other = jnp.int32(0), jnp.int32(width)
        for r in range(rows):
            hit = (mask >> r) & 1
            place = jnp.where(hit == 1, named, other)
            rank[where * rows + r] = place
            rank[(where + 1) * rows + place] = r
            named = named + hit
            other = other + 1 - hit

    def ranked(where, r):
        return rank[where * rows + r]

    copies[0].wait()
    copies[1].wait()
    rank_rows(0, 3, 0)
    rank_rows(1, 2, 2)
    sent_1, sent_0 = jnp.where(side == ABOVE, 0, 2), jnp.where(side == ABOVE, 2, 0)
    copies[3].wait()
    for j in range(width):
        t_1[j] = t[ranked(sent_1 + 1, j)]
        t_0[j] = t[ranked(sent_0 + 1, j)]
    copies[2].wait()
    copies[4].wait()
    rank_rows(2, 2, 4)
    rank_rows(2, 3, 6)
    for j in range(width):
        tab[LIST_0 + j] = ranked(sent_1, ranked(sent_0 + 1, j))
        for which in (BELOW, ABOVE):
            for k in range(2):
                tab[SIDE_LAB + 8 * which + 2 * j + k] = agg[col(which, ranked(5 + 2 * which, j), 2 + k)]
    for u in range(rows):
        row = ranked(sent_1 + 1, u)
        tab[ROW + u] = row
        tab[NEAR + u] = ranked(sent_1, col(2, row, 1) & (rows - 1))
        tab[POS2 + u] = ranked(4, col(2, row, 2) & (rows - 1))
        tab[POS3 + u] = ranked(6, col(2, row, 3) & (rows - 1))
        for k in range(4):
            tab[OWN_LAB + 4 * u + k] = agg[col(2, row, k)]


def put(value, label, column):
    return jnp.where(label == column, value, jnp.zeros_like(value))


def two_columns(value, label):
    return jnp.concatenate([put(value, label, 0), put(value, label, 1)], axis=1)


def near_tile(tab, a, t, dinv, u):
    block = t.shape[1]
    row = tab[ROW + u]
    near = tab[ROW + tab[NEAR + u]]
    prod = jnp.concatenate(
        [dot3k(*split(a[row, 0]), *split(t[row])), dot3k(*split(a[row, 1]), *split(t[near]))], axis=1
    )
    smoothed = dot3k(*split(dinv[row]), *split(prod))
    p0 = t[row] - OMEGA * smoothed[:, :block]
    p1 = -OMEGA * smoothed[:, block:]
    return two_columns(p0, tab[OWN_LAB + 4 * u]) + two_columns(p1, tab[OWN_LAB + 4 * u + 1])


def near_sent_kernel(tab, a, t, dinv, near_1):
    for u in range(near_1.shape[0]):
        near_1[u] = near_tile(tab, a, t, dinv, u)


def wide(ref, *places):
    return jnp.concatenate([ref[place] for place in places], axis=0)


def near_rest_kernel(tab, a, t, dinv, near_1, near_0, own, part, a_high, a_low, own_high, own_low):
    width = near_1.shape[0]
    for u in range(width):
        own[u] = near_1[u]
        own[width + u] = near_tile(tab, a, t, dinv, width + u)
    for j in range(width):
        near_0[j] = own[tab[LIST_0 + j]]
    for u in range(2 * width):
        own_high[u], own_low[u] = split(own[u])
    for u in range(2 * width):
        row, near = tab[ROW + u], tab[NEAR + u]
        a_high[u], a_low[u] = split(jnp.concatenate([a[row, 0], a[row, 1]], axis=1))
        part[u] = dot3(a_high[u], a_low[u], wide(own_high, u, near), wide(own_low, u, near))


def far_kernel(tab, a, dinv, t_0, t_1, after, far_0, far_1, far, a_high, a_low, t_high, t_low):
    rows, block = dinv.shape[0], dinv.shape[1]
    width = rows // 2
    side = pair_side()
    for j in range(width):
        t_high[side, j], t_low[side, j] = split(t_0[j])
        t_high[1 - side, j], t_low[1 - side, j] = split(t_1[j])
    for u in range(rows):
        row = tab[ROW + u]
        below, above = tab[POS2 + u], tab[POS3 + u]
        a2, a3 = split(a[row, 2]), split(a[row, 3])
        a_high[u] = jnp.concatenate([a2[0], a3[0]], axis=1)
        a_low[u] = jnp.concatenate([a2[1], a3[1]], axis=1)
        prod = jnp.concatenate(
            [
                dot3k(*a2, t_high[BELOW, below], t_low[BELOW, below]),
                dot3k(*a3, t_high[ABOVE, above], t_low[ABOVE, above]),
            ],
            axis=1,
        )
        both = -OMEGA * dot3k(*split(dinv[row]), *split(prod))
        far[u, BELOW] = both[:, :block]
        far[u, ABOVE] = both[:, block:]
    for j in range(width):
        far_1[j] = far[j]
        far_0[j] = far[tab[LIST_0 + j]]


def store_turned(trans, label, place, value):
    block = value.shape[0]
    trans[pl.ds(pl.multiple_of(label * block, block), block), place] = value.T
    trans[pl.ds(pl.multiple_of((1 - label) * block, block), block), place] = jnp.zeros_like(value)


def turn(tab, far, side, trans_high, trans_low):
    for u in range(far.shape[0]):
        block = far.shape[2]
        label = tab[OWN_LAB + 4 * u + 2 + side]
        high, low = split(far[u, side])
        place = slice(u * block, (u + 1) * block)
        store_turned(trans_high, label, place, high)
        store_turned(trans_low, label, place, low)


def pre_kernel(
    tab, a_high, a_low, far,
    part, trans_high, trans_low,
    far_high, far_low,
):
    rows, block = far.shape[0], far.shape[2]
    half = 2 * block
    for u in range(rows):
        for side in (BELOW, ABOVE):
            label = tab[OWN_LAB + 4 * u + 2 + side]
            high, low = split(far[u, side])
            far_high[side, u] = two_columns(high, label)
            far_low[side, u] = two_columns(low, label)
    turn(tab, far, 1 - pair_side(), trans_high, trans_low)
    for u in range(rows):
        near = tab[NEAR + u]
        for side in (BELOW, ABOVE):
            part[u, :, side * half : (side + 1) * half] = dot3(
                a_high[u], a_low[u], wide(far_high.at[side], u, near), wide(far_low.at[side], u, near)
            )


def coarse_rows(trans_high, trans_low, ap_high, ap_low, out, start=0):
    half = trans_high.shape[0]
    for c in range(ap_high.shape[1] // half):
        cols = slice(c * half, (c + 1) * half)
        out[:, start + c * half : start + (c + 1) * half] = dot3(
            trans_high[...], trans_low[...], ap_high[:, cols], ap_low[:, cols]
        )


def first_kernel(
    tab, a_high, a_low, part, trans_high, trans_low, near_0, near_1,
    ap_high, ap_low, out_1,
    p_high, p_low,
):
    rows, block = a_high.shape[0], a_high.shape[1]
    half = 2 * block
    side = pair_side()
    for j in range(rows // 2):
        p_high[side, j], p_low[side, j] = split(near_0[j])
        p_high[1 - side, j], p_low[1 - side, j] = split(near_1[j])
    for u in range(rows):
        pos2, pos3 = tab[POS2 + u], tab[POS3 + u]
        a2 = a_high[u, :, :block], a_low[u, :, :block]
        a3 = a_high[u, :, block:], a_low[u, :, block:]
        low = part[u, :, :half] + dot3k(*a2, p_high[BELOW, pos2], p_low[BELOW, pos2])
        upp = part[u, :, half:] + dot3k(*a3, p_high[ABOVE, pos3], p_low[ABOVE, pos3])
        place = slice(u * block, (u + 1) * block)
        ap_high[place, :half], ap_low[place, :half] = split(low)
        ap_high[place, half:], ap_low[place, half:] = split(upp)
    coarse_rows(trans_high, trans_low, ap_high, ap_low, out_1)


def second_kernel(
    tab, a_high, a_low, part, trans_high, trans_low, far_0, far_1, after,
    ap_high, ap_low, out_1,
    p_high, p_low,
):
    rows, block = a_high.shape[0], a_high.shape[1]
    half = 2 * block
    side = pair_side()
    for j in range(rows // 2):
        for q in range(2):
            cols = slice(q * block, (q + 1) * block)
            p_high[side, j, :, cols], p_low[side, j, :, cols] = split(far_0[j, q])
            p_high[1 - side, j, :, cols], p_low[1 - side, j, :, cols] = split(far_1[j, q])
    for u in range(rows):
        pos2, pos3 = tab[POS2 + u], tab[POS3 + u]
        a2 = a_high[u, :, :block], a_low[u, :, :block]
        a3 = a_high[u, :, block:], a_low[u, :, block:]
        left = dot3k(*a2, p_high[BELOW, pos2], p_low[BELOW, pos2])
        right = dot3k(*a3, p_high[ABOVE, pos3], p_low[ABOVE, pos3])
        labels = [tab[SIDE_LAB + 8 * which + 2 * pos + k] for which, pos in ((BELOW, pos2), (ABOVE, pos3)) for k in (0, 1)]
        own = part[u] + two_columns(left[:, block:], labels[1]) + two_columns(right[:, :block], labels[2])
        place = slice(u * block, (u + 1) * block)
        ap_high[place, half : 2 * half], ap_low[place, half : 2 * half] = split(own)
        for cols, value, label in (
            (slice(0, half), left[:, :block], labels[0]),
            (slice(2 * half, 3 * half), right[:, block:], labels[3]),
        ):
            high, low = split(value)
            ap_high[place, cols] = two_columns(high, label)
            ap_low[place, cols] = two_columns(low, label)
    coarse_rows(trans_high, trans_low, ap_high, ap_low, out_1)


def other_kernel(tab, far, ap1_high, ap1_low, ap2_high, ap2_low, out_0, trans_high, trans_low):
    turn(tab, far, pair_side(), trans_high, trans_low)
    coarse_rows(trans_high, trans_low, ap1_high, ap1_low, out_0)
    coarse_rows(trans_high, trans_low, ap2_high, ap2_low, out_0, ap1_high.shape[1])


HELD = ((1, 0), (0, 0), (1, 1), (0, 1), (1, 2))


def own_kernel(own, ap1_high, ap1_low, ap2_high, ap2_low, out, trans_high, trans_low):
    rows, block = own.shape[0], own.shape[1]
    half = 2 * block
    for u in range(rows):
        place = slice(u * block, (u + 1) * block)
        high, low = split(own[u])
        trans_high[:, place] = high.T
        trans_low[:, place] = low.T
    aps = (ap1_high, ap1_low), (ap2_high, ap2_low)
    for d, (which, c) in enumerate(HELD):
        cols = slice(c * half, (c + 1) * half)
        high, low = aps[which]
        out[:, d * half : (d + 1) * half] = dot3(trans_high[...], trans_low[...], high[:, cols], low[:, cols])


def write_slots(inv, total, result, agg, d, out, sem):
    block = total.shape[0]
    value = dot3k(*inv, *split(total))
    result[0] = value[:, :block]
    result[1] = value[:, block:]
    copy = pltpu.make_async_copy(result, out.at[agg, pl.ds(2 * (d + 3), 2)], sem)
    copy.start()
    return copy


def both_sides(run):
    side = pair_side()
    pl.when(side == ABOVE)(lambda: run(ABOVE))
    pl.when(side == BELOW)(lambda: run(BELOW))


def early_kernel(inverse, own, both_0, first_1, out, waiting, results, sems):
    block = inverse.shape[1]
    half = 2 * block

    def run(side):
        shift_0, shift_1 = (1, -1) if side == ABOVE else (-1, 1)
        copies = []
        for agg in range(2):
            inv = split(inverse[agg])
            line = slice(agg * block, (agg + 1) * block)
            for d in range(-3, 4):
                parts, late = [], None
                if -2 <= d <= 2:
                    parts.append(own[line, (d + 2) * half : (d + 3) * half])
                if -2 <= d - shift_0 <= 2:
                    which, c = HELD[d - shift_0 + 2]
                    c = c + 2 * which
                    parts.append(both_0[line, c * half : (c + 1) * half])
                if -2 <= d - shift_1 <= 2:
                    which, c = HELD[d - shift_1 + 2]
                    if which:
                        late = c
                    else:
                        parts.append(first_1[line, c * half : (c + 1) * half])
                total = sum(parts[1:], parts[0]) if parts else jnp.zeros((block, half), F32)
                if late is not None:
                    waiting[agg, late] = total
                else:
                    n = len(copies)
                    copies.append(write_slots(inv, total, results.at[n], agg, d, out, sems.at[n]))
        for copy in copies:
            copy.wait()

    both_sides(run)


def late_kernel(inverse, waiting, second_1, partly, out, results, sems):
    block = inverse.shape[1]
    half = 2 * block

    def run(side):
        shift = -1 if side == ABOVE else 1
        copies = []
        for agg in range(2):
            inv = split(inverse[agg])
            line = slice(agg * block, (agg + 1) * block)
            for c in range(3):
                total = waiting[agg, c] + second_1[line, c * half : (c + 1) * half]
                n = len(copies)
                copies.append(write_slots(inv, total, results.at[n], agg, 2 * c - 2 + shift, out, sems.at[n]))
        for copy in copies:
            copy.wait()

    both_sides(run)


SMEM = pl.BlockSpec(memory_space=pltpu.SMEM)
VMEM = pl.BlockSpec(memory_space=pltpu.VMEM)
HBM = pl.BlockSpec(memory_space=pltpu.HBM)


def call(body, outs, ins, scratch=(), micros=1.0, in_hbm=(), out_hbm=(), aliases={}):
    def specs(values, in_place):
        return [HBM if i in in_place else SMEM if x.dtype == jnp.int32 else VMEM for i, x in enumerate(values)]

    return pl.pallas_call(
        body,
        out_shape=outs,
        in_specs=specs(ins, in_hbm),
        out_specs=specs(outs, out_hbm),
        scratch_shapes=[pltpu.VMEM(*x) if isinstance(x, tuple) else x for x in scratch],
        input_output_aliases=aliases,
        compiler_params=pltpu.CompilerParams(vmem_limit_bytes=24 * 2**20),
        cost_estimate=pl.CostEstimate(flops=int(micros * 1e9), bytes_accessed=2**20, transcendentals=0),
    )(*ins)


def shards(a, a_cols, t_blocks, t_agg, dinv, coarse_inv):
    devices = lax.axis_size(AXES)
    rows, block = t_blocks.shape[:2]
    width, half, deep = rows // 2, 2 * block, rows * block
    shape = jax.ShapeDtypeStruct
    full = lambda *dims: shape(dims, F32)
    pair = lambda *dims: [shape(dims, BF16), shape(dims, BF16)]
    two = lambda *dims: [(dims, BF16)] * 2
    tile = full(width, block, half)
    cols = a_cols.reshape(-1, ROW_CHUNK, 4).transpose(0, 2, 1).reshape(-1)

    tab, t_0, t_1, t = call(
        functools.partial(load_kernel, devices),
        [shape((TAB,), jnp.int32)] + [full(width, block, block)] * 2 + [full(*t_blocks.shape)],
        [pltpu.with_memory_space_constraint(x, pltpu.HBM) for x in (cols, t_agg, t_blocks)],
        [
            pltpu.SMEM((3 * 4 * ROW_CHUNK,), jnp.int32),
            pltpu.SMEM(t_agg.shape, jnp.int32),
            pltpu.SMEM((8 * rows,), jnp.int32),
            pltpu.SemaphoreType.DMA((5,)),
        ],
        micros=3,
        in_hbm=(0, 1, 2),
    )
    t_1 = exchanged(t_1, 1)
    t_0 = exchanged(t_0, 0)
    (near_1,) = call(near_sent_kernel, [tile], [tab, a, t, dinv], micros=2)
    got_near_1 = exchanged(near_1, 1)
    near_0, own, part_own, a01_high, a01_low = call(
        near_rest_kernel,
        [tile] + [full(rows, block, half)] * 2 + pair(rows, block, half),
        [tab, a, t, dinv, near_1],
        two(rows, block, half),
        micros=2,
    )
    near_0, near_1 = exchanged(near_0, 0), got_near_1
    sent = full(width, 2, block, block)
    far_0, far_1, far, a23_high, a23_low = call(
        far_kernel,
        [sent, sent, full(rows, 2, block, block)] + pair(rows, block, half),
        [tab, a, dinv, t_0, t_1, own],
        two(2, width, block, block),
        micros=2,
    )
    far_1 = exchanged(far_1, 1)
    far_0 = exchanged(far_0, 0)
    part, out_high, out_low = call(
        pre_kernel,
        [full(rows, block, 2 * half)] + pair(half, deep),
        [tab, a01_high, a01_low, far],
        two(2, rows, block, half),
        micros=3,
    )
    ap1_high, ap1_low, first_1 = call(
        first_kernel,
        pair(deep, 2 * half) + [full(half, 2 * half)],
        [tab, a23_high, a23_low, part, out_high, out_low, near_0, near_1],
        two(2, width, block, half),
        micros=3,
    )
    first_1 = exchanged(first_1, 1)
    ap2_high, ap2_low, second_1 = call(
        second_kernel,
        pair(deep, 3 * half) + [full(half, 3 * half)],
        [tab, a23_high, a23_low, part_own, out_high, out_low, far_0, far_1, ap1_high],
        two(2, width, block, half),
        micros=3,
    )
    second_1 = exchanged(second_1, 1)
    (both_0,) = call(
        other_kernel,
        [full(half, 5 * half)],
        [tab, far, ap1_high, ap1_low, ap2_high, ap2_low],
        two(half, deep),
        micros=2,
    )
    both_0 = exchanged(both_0, 0)
    (total,) = call(
        own_kernel, [full(half, 5 * half)], [own, ap1_high, ap1_low, ap2_high, ap2_low], two(half, deep), micros=2
    )
    result = full(2, 14, block, block)
    partly, waiting = call(
        early_kernel,
        [result, full(2, 3, block, half)],
        [coarse_inv, total, both_0, first_1],
        [((8, 2, block, block), F32), pltpu.SemaphoreType.DMA((8,))],
        micros=2,
        out_hbm=(0,),
    )
    (out,) = call(
        late_kernel,
        [result],
        [coarse_inv, waiting, second_1, partly],
        [((6, 2, block, block), F32), pltpu.SemaphoreType.DMA((6,))],
        micros=1,
        in_hbm=(3,),
        out_hbm=(0,),
        aliases={3: 0},
    )
    return out


def solution(mesh):
    placed = (
        P(AXES, None, None, None),
        P(),
        P(AXES, None, None),
        P(),
        P(AXES, None, None),
        P(AXES, None, None),
    )
    return jax.shard_map(
        shards,
        mesh=mesh,
        in_specs=placed,
        out_specs=P(AXES, None, None, None),
        check_vma=False,
    )
```

time: 62.5 us -> 63.8 us (1.021)
  waiting for transfers between devices: 13.8 us -> 15.6 us
    ppermute x10 -> x9, waiting for transfers between devices: 13.8 us -> 15.6 us  [exchanged(): return lax.ppermute(value, AXES, pairs)]
    pallas_call x13 -> x11, Pallas kernels: 24.1 us -> 23.5 us  [call(): pl.pallas_call(body, out_shape=outs, in_specs=specs(ins, in_hbm), out_spe...]
    ppermute x10 -> x9, starting transfers between devices: 24.2 us -> 24.3 us  [exchanged(): return lax.ppermute(value, AXES, pairs)]
  transfers between devices with their start and end apart: 10 -> 9, of which waited for: 3 -> 2; matrix products, arithmetic and copies ran while one was open for 0% -> 0% of each run, Pallas kernels for 26% -> 22%
where the time goes in v4:
time: 63.8 us; the launch traced here: 63.7 us
  starting transfers between devices  24.3 us (38%)
  Pallas kernels  23.5 us (37%)
  waiting for transfers between devices  15.6 us (24%)
    ppermute x9, starting transfers between devices, exchanged(): return lax.ppermute(value, AXES, pairs)  24.3 us
    pallas_call x11, Pallas kernels, call(): pl.pallas_call(body, out_shape=outs, in_specs=specs(ins, in_hbm), out_spe...  23.5 us
    ppermute x9, waiting for transfers between devices, exchanged(): return lax.ppermute(value, AXES, pairs)  15.6 us
  transfers between devices with their start and end apart: 9, of which 2 were waited for; matrix products, arithmetic and copies ran while one was open for 0% of the time, Pallas kernels for 22%

profile of v4, /device:TPU:0, one launch (start us, length us, event | category | flops | bytes accessed | tf_op | source)
XLA Modules:
  0.0 63.7 jit_solution(10291533150236415257)
XLA Ops:
  0.0 2.1 %shard_map.64 = (s32[128]{0:T(128)S(1)}, f32[4,128,128]{2,1,0:T(8,128)S(1)}, f32[4,128,128]{2,1,0:T(8,128)S(1)}, f32[8,128,128]{2,1,0:T(8,128)S(1)}) custom-call(s32[4096]{0:T(1024)} %bitcast.5, s32[1024]{0:T(1024)} %agg_hbm.1, f32[8,128,128]{2,1,0:T(8,128)} %t_hbm.1), custom_call_target="tpu_custom_call" | custom-call | flops 3000000000 | bytes 1048576 | tf_op jit(solution)/shard_map/pallas_call | solution.py:400
  2.1 0.1 collective-permute-start
  2.2 8.9 %collective-permute-start.1 = (f32[4,128,128]{2,1,0:T(8,128)S(1)}, f32[4,128,128]{2,1,0:T(8,128)S(1)}, u32[]{:S(2)}, u32[]{:S(2)}) collective-permute-start(f32[4,128,128]{2,1,0:T(8,128)S(1)} %get-tuple-element.34), channel_id=1, source_target_pairs={{1,2},{2,1},{3,4},{4,3},{5,6},{6,5},{7,8},{8,7},{9,10},{10,9},{11,... | collective-permute-start | bytes 786440 | tf_op jit(solution)/shard_map/ppermute | solution.py:26
  11.1 0.0 copy-done.1
  11.1 0.0 copy-done.2
  11.1 1.6 %shard_map.65.near_1 = f32[4,128,256]{2,1,0:T(8,128)S(1)} custom-call(s32[128]{0:T(128)S(1)} %get-tuple-element.30.tab, f32[8,4,128,128]{3,2,1,0:T(8,128)S(1)} %copy-done.1, f32[8,128,128]{2,1,0:T(8,128)S(1)} %get-tuple-element.31.t, f32[8,128,128]{2,1,0:T(8,128)S(1)} %copy-done.2), custom_call_target="tpu_custom_call" | custom-call | flops 2000000000 | bytes 1048576 | tf_op jit(solution)/shard_map/pallas_call | solution.py:400
  12.7 0.1 collective-permute-start.3
  12.8 2.3 %shard_map.66 = (f32[4,128,256]{2,1,0:T(8,128)S(1)}, f32[8,128,256]{2,1,0:T(8,128)S(1)}, f32[8,128,256]{2,1,0:T(8,128)S(1)}, bf16[8,128,256]{2,1,0:T(8,128)(2,1)S(1)}, bf16[8,128,256]{2,1,0:T(8,128)(2,1)S(1)}) custom-call(s32[128]{0:T(128)S(1)} %get-tuple-element.30.tab, f32[8,4,128,128]{3,2,1,0:T(8,128)S(1)} %copy-done.1, ...), custom_call_target="tpu_custom_call" | custom-call | flops 2000000000 | bytes 1048576 | tf_op jit(solution)/shard_map/pallas_call | solution.py:400
  15.1 0.1 collective-permute-start.2
  15.2 0.0 collective-permute-done.t_0
  15.2 0.0 collective-permute-done.1.t_1
  15.2 2.5 %shard_map.67 = (f32[4,2,128,128]{3,2,1,0:T(8,128)S(1)}, f32[4,2,128,128]{3,2,1,0:T(8,128)S(1)}, f32[8,2,128,128]{3,2,1,0:T(8,128)S(1)}, bf16[8,128,256]{2,1,0:T(8,128)(2,1)S(1)}, bf16[8,128,256]{2,1,0:T(8,128)(2,1)S(1)}) custom-call(s32[128]{0:T(128)S(1)} %get-tuple-element.30.tab, f32[8,4,128,128]{3,2,1,0:T(8,128)S(1)} %copy-done.1, ...), custom_call_target="tpu_custom_call" | custom-call | flops 2000000000 | bytes 1048576 | tf_op jit(solution)/shard_map/pallas_call | solution.py:400
  17.8 0.6 collective-permute-start.4
  18.4 7.2 %collective-permute-start.5 = (f32[4,2,128,128]{3,2,1,0:T(8,128)S(1)}, f32[4,2,128,128]{3,2,1,0:T(8,128)S(1)}, u32[]{:S(2)}, u32[]{:S(2)}) collective-permute-start(f32[4,2,128,128]{3,2,1,0:T(8,128)S(1)} %get-tuple-element.48), channel_id=1, source_target_pairs={{1,2},{2,1},{3,4},{4,3},{5,6},{6,5},{7,8},{8,7},{9,10},{10,9},{11,... | collective-permute-start | bytes 1572872 | tf_op jit(solution)/shard_map/ppermute | solution.py:26
  25.5 1.9 %shard_map.68 = (f32[8,128,512]{2,1,0:T(8,128)S(1)}, bf16[256,1024]{1,0:T(8,128)(2,1)S(1)}, bf16[256,1024]{1,0:T(8,128)(2,1)S(1)}) custom-call(s32[128]{0:T(128)S(1)} %get-tuple-element.30.tab, bf16[8,128,256]{2,1,0:T(8,128)(2,1)S(1)} %get-tuple-element.37.a_high, bf16[8,128,256]{2,1,0:T(8,128)(2,1)S(1)} %get-tuple-element.38.a_low, ...), custom_call_target="tpu_custom_call" | custom-call | flops 3000000000 | bytes 1048576 | tf_op jit(solution)/shard_map/pallas_call | solution.py:400
  27.4 0.0 collective-permute-done.3.near_1
  27.4 0.0 collective-permute-done.2.near_0
  27.4 2.3 %shard_map.69 = (bf16[1024,512]{1,0:T(8,128)(2,1)S(1)}, bf16[1024,512]{1,0:T(8,128)(2,1)S(1)}, f32[256,512]{1,0:T(8,128)S(1)}) custom-call(s32[128]{0:T(128)S(1)} %get-tuple-element.30.tab, bf16[8,128,256]{2,1,0:T(8,128)(2,1)S(1)} %get-tuple-element.35.a_high, bf16[8,128,256]{2,1,0:T(8,128)(2,1)S(1)} %get-tuple-element.36.a_low, ...), custom_call_target="tpu_custom_call" | custom-call | flops 3000000000 | bytes 1048576 | tf_op jit(solution)/shard_map/pallas_call | solution.py:400
  29.7 0.0 collective-permute-done.4.far_0
  29.7 2.7 %collective-permute-done.5.far_1 = f32[4,2,128,128]{3,2,1,0:T(8,128)S(1)} collective-permute-done((f32[4,2,128,128]{3,2,1,0:T(8,128)S(1)}, f32[4,2,128,128]{3,2,1,0:T(8,128)S(1)}, u32[]{:S(2)}, u32[]{:S(2)}) %collective-permute-start.5) | collective-permute-done | bytes 524320 | tf_op jit(solution)/shard_map/ppermute | solution.py:26
  32.4 2.9 %shard_map.70 = (bf16[1024,768]{1,0:T(8,128)(2,1)S(1)}, bf16[1024,768]{1,0:T(8,128)(2,1)S(1)}, f32[256,768]{1,0:T(8,128)S(1)}) custom-call(s32[128]{0:T(128)S(1)} %get-tuple-element.30.tab, bf16[8,128,256]{2,1,0:T(8,128)(2,1)S(1)} %get-tuple-element.35.a_high, bf16[8,128,256]{2,1,0:T(8,128)(2,1)S(1)} %get-tuple-element.36.a_low, ...), custom_call_target="tpu_custom_call" | custom-call | flops 3000000000 | bytes 1048576 | tf_op jit(solution)/shard_map/pallas_call | solution.py:400
  35.3 3.1 %shard_map.72 = f32[256,1280]{1,0:T(8,128)S(1)} custom-call(s32[128]{0:T(128)S(1)} %get-tuple-element.30.tab, f32[8,2,128,128]{3,2,1,0:T(8,128)S(1)} %get-tuple-element.39.far, bf16[1024,512]{1,0:T(8,128)(2,1)S(1)} %get-tuple-element.44.after.ap1_high, bf16[1024,512]{1,0:T(8,128)(2,1)S(1)} %get-tuple-element.45.ap1_low, ...), custom_call_target="tpu_custom_call" | custom-call | flops 2000000000 | bytes 1048576 | tf_op jit(solution)/shard_map/pallas_call | solution.py:400
  38.4 0.1 collective-permute-start.6
  38.5 7.2 %collective-permute-start.8 = (f32[256,768]{1,0:T(8,128)S(1)}, f32[256,768]{1,0:T(8,128)S(1)}, u32[]{:S(2)}, u32[]{:S(2)}) collective-permute-start(f32[256,768]{1,0:T(8,128)S(1)} %get-tuple-element.53), channel_id=1, source_target_pairs={{1,2},{2,1},{3,4},{4,3},{5,6},{6,5},{7,8},{8,7},{9,10},{10,9},{11,... | collective-permute-start | bytes 2359304 | tf_op jit(solution)/shard_map/ppermute | solution.py:26
  45.7 0.1 collective-permute-start.7
  45.8 2.4 %shard_map.71.own = f32[256,1280]{1,0:T(8,128)S(1)} custom-call(f32[8,128,256]{2,1,0:T(8,128)S(1)} %get-tuple-element.32.after.own, bf16[1024,512]{1,0:T(8,128)(2,1)S(1)} %get-tuple-element.44.after.ap1_high, bf16[1024,512]{1,0:T(8,128)(2,1)S(1)} %get-tuple-element.45.ap1_low, bf16[1024,768]{1,0:T(8,128)(2,1)S(1)} %get-tuple-element.49.ap2_high, ...), custom_call_target="tpu_custom_call" | custom-call | flops 2000000000 | bytes 1048576 | tf_op jit(solution)/shard_map/pallas_call | solution.py:400
  48.2 12.9 %collective-permute-done.7.first_1 = f32[256,512]{1,0:T(8,128)S(1)} collective-permute-done((f32[256,512]{1,0:T(8,128)S(1)}, f32[256,512]{1,0:T(8,128)S(1)}, u32[]{:S(2)}, u32[]{:S(2)}) %collective-permute-start.7) | collective-permute-done | bytes 524320 | tf_op jit(solution)/shard_map/ppermute | solution.py:26
  61.0 0.0 collective-permute-done.6.both_0
  61.0 0.0 copy-done
  61.0 1.3 %shard_map.73 = (f32[2,14,128,128]{3,2,1,0:T(8,128)}, f32[2,3,128,256]{3,2,1,0:T(8,128)S(1)}) custom-call(f32[2,128,128]{2,1,0:T(8,128)S(1)} %copy-done, f32[256,1280]{1,0:T(8,128)S(1)} %shard_map.71.own, f32[256,1280]{1,0:T(8,128)S(1)} %collective-permute-done.6.both_0, f32[256,512]{1,0:T(8,128)S(1)} %collective-permute-done.7.first_1), custom_call_target="tpu_custom_call" | custom-call | flops 2000000000 | bytes 1048576 | tf_op jit(solution)/shard_map/pallas_call | solution.py:400
  62.3 0.0 collective-permute-done.8.second_1
  62.4 1.2 %shard_map.74 = f32[2,14,128,128]{3,2,1,0:T(8,128)} custom-call(f32[2,128,128]{2,1,0:T(8,128)S(1)} %copy-done, f32[2,3,128,256]{3,2,1,0:T(8,128)S(1)} %get-tuple-element.52.waiting, f32[256,768]{1,0:T(8,128)S(1)} %collective-permute-done.8.second_1, f32[2,14,128,128]{3,2,1,0:T(8,128)} %get-tuple-element.54.partly), custom_call_target="tpu_custom_call", output_to_operand_aliasing={{}: (3, {})} | custom-call | flops 1000000000 | bytes 1048576 | tf_op jit(solution)/shard_map/pallas_call | solution.py:400
  (3 shorter events, 0.0 us)
Async XLA Ops:
  0.0 11.1 %copy-start.1 = (f32[8,4,128,128]{3,2,1,0:T(8,128)S(1)}, f32[8,4,128,128]{3,2,1,0:T(8,128)}, u32[]{:S(2)}) copy-start(f32[8,4,128,128]{3,2,1,0:T(8,128)} %a.5) | copy-start | bytes 6291460
  0.0 11.1 %copy-start.2 = (f32[8,128,128]{2,1,0:T(8,128)S(1)}, f32[8,128,128]{2,1,0:T(8,128)}, u32[]{:S(2)}) copy-start(f32[8,128,128]{2,1,0:T(8,128)} %dinv.5) | copy-start | bytes 1572868
  2.1 13.1 %collective-permute-start = (f32[4,128,128]{2,1,0:T(8,128)S(1)}, f32[4,128,128]{2,1,0:T(8,128)S(1)}, u32[]{:S(2)}, u32[]{:S(2)}) collective-permute-start(f32[4,128,128]{2,1,0:T(8,128)S(1)} %get-tuple-element.33), channel_id=1, source_target_pairs={{0,1},{1,0},{2,3},{3,2},{4,5},{5,4},{6,7},{7,6},{8,9},{9,8},{10,11... | collective-permute-start | bytes 786440 | tf_op jit(solution)/shard_map/ppermute | solution.py:26
  2.2 13.0 %collective-permute-start.1 = (f32[4,128,128]{2,1,0:T(8,128)S(1)}, f32[4,128,128]{2,1,0:T(8,128)S(1)}, u32[]{:S(2)}, u32[]{:S(2)}) collective-permute-start(f32[4,128,128]{2,1,0:T(8,128)S(1)} %get-tuple-element.34), channel_id=1, source_target_pairs={{1,2},{2,1},{3,4},{4,3},{5,6},{6,5},{7,8},{8,7},{9,10},{10,9},{11,... | collective-permute-start | bytes 786440 | tf_op jit(solution)/shard_map/ppermute | solution.py:26
  12.7 14.7 %collective-permute-start.3 = (f32[4,128,256]{2,1,0:T(8,128)S(1)}, f32[4,128,256]{2,1,0:T(8,128)S(1)}, u32[]{:S(2)}, u32[]{:S(2)}) collective-permute-start(f32[4,128,256]{2,1,0:T(8,128)S(1)} %shard_map.65.near_1), channel_id=1, source_target_pairs={{1,2},{2,1},{3,4},{4,3},{5,6},{6,5},{7,8},{8,7},{9,10},{10,9},{11,... | collective-permute-start | bytes 1572872 | tf_op jit(solution)/shard_map/ppermute | solution.py:26
  15.1 12.3 %collective-permute-start.2 = (f32[4,128,256]{2,1,0:T(8,128)S(1)}, f32[4,128,256]{2,1,0:T(8,128)S(1)}, u32[]{:S(2)}, u32[]{:S(2)}) collective-permute-start(f32[4,128,256]{2,1,0:T(8,128)S(1)} %get-tuple-element.43), channel_id=1, source_target_pairs={{0,1},{1,0},{2,3},{3,2},{4,5},{5,4},{6,7},{7,6},{8,9},{9,8},{10,11... | collective-permute-start | bytes 1572872 | tf_op jit(solution)/shard_map/ppermute | solution.py:26
  17.8 12.0 %collective-permute-start.4 = (f32[4,2,128,128]{3,2,1,0:T(8,128)S(1)}, f32[4,2,128,128]{3,2,1,0:T(8,128)S(1)}, u32[]{:S(2)}, u32[]{:S(2)}) collective-permute-start(f32[4,2,128,128]{3,2,1,0:T(8,128)S(1)} %get-tuple-element.47), channel_id=1, source_target_pairs={{0,1},{1,0},{2,3},{3,2},{4,5},{5,4},{6,7},{7,6},{8,9},{9,8},{10,11... | collective-permute-start | bytes 1572872 | tf_op jit(solution)/shard_map/ppermute | solution.py:26
  18.4 14.1 %collective-permute-start.5 = (f32[4,2,128,128]{3,2,1,0:T(8,128)S(1)}, f32[4,2,128,128]{3,2,1,0:T(8,128)S(1)}, u32[]{:S(2)}, u32[]{:S(2)}) collective-permute-start(f32[4,2,128,128]{3,2,1,0:T(8,128)S(1)} %get-tuple-element.48), channel_id=1, source_target_pairs={{1,2},{2,1},{3,4},{4,3},{5,6},{6,5},{7,8},{8,7},{9,10},{10,9},{11,... | collective-permute-start | bytes 1572872 | tf_op jit(solution)/shard_map/ppermute | solution.py:26
  38.4 22.6 %collective-permute-start.6 = (f32[256,1280]{1,0:T(8,128)S(1)}, f32[256,1280]{1,0:T(8,128)S(1)}, u32[]{:S(2)}, u32[]{:S(2)}) collective-permute-start(f32[256,1280]{1,0:T(8,128)S(1)} %shard_map.72), channel_id=1, source_target_pairs={{0,1},{1,0},{2,3},{3,2},{4,5},{5,4},{6,7},{7,6},{8,9},{9,8},{10,11... | collective-permute-start | bytes 3932168 | tf_op jit(solution)/shard_map/ppermute | solution.py:26
  38.5 23.9 %collective-permute-start.8 = (f32[256,768]{1,0:T(8,128)S(1)}, f32[256,768]{1,0:T(8,128)S(1)}, u32[]{:S(2)}, u32[]{:S(2)}) collective-permute-start(f32[256,768]{1,0:T(8,128)S(1)} %get-tuple-element.53), channel_id=1, source_target_pairs={{1,2},{2,1},{3,4},{4,3},{5,6},{6,5},{7,8},{8,7},{9,10},{10,9},{11,... | collective-permute-start | bytes 2359304 | tf_op jit(solution)/shard_map/ppermute | solution.py:26
  45.7 15.4 %copy-start = (f32[2,128,128]{2,1,0:T(8,128)S(1)}, f32[2,128,128]{2,1,0:T(8,128)}, u32[]{:S(2)}) copy-start(f32[2,128,128]{2,1,0:T(8,128)} %inverse.3) | copy-start | bytes 393220
  45.7 15.3 %collective-permute-start.7 = (f32[256,512]{1,0:T(8,128)S(1)}, f32[256,512]{1,0:T(8,128)S(1)}, u32[]{:S(2)}, u32[]{:S(2)}) collective-permute-start(f32[256,512]{1,0:T(8,128)S(1)} %get-tuple-element.51), channel_id=1, source_target_pairs={{1,2},{2,1},{3,4},{4,3},{5,6},{6,5},{7,8},{8,7},{9,10},{10,9},{11,... | collective-permute-start | bytes 1572872 | tf_op jit(solution)/shard_map/ppermute | solution.py:26

commit v5 on v4

--- a/solution.py
+++ b/solution.py
@@ -12,7 +12,8 @@
 AXES = ("gx", "gy")
 F32 = jnp.float32
 BF16 = jnp.bfloat16
-ROW, NEAR, POS2, POS3, LIST_0, OWN_LAB, SIDE_LAB, TAB = 0, 8, 16, 24, 32, 48, 80, 128
+ROW, NEAR, POS2, POS3, LIST_0, OWN_LAB, SIDE_LAB, TAB = 0, 8, 16, 24, 32, 40, 72, 88
+LANES = 128
 BELOW, ABOVE = 0, 1
 ROW_CHUNK = 128
 
@@ -46,6 +47,14 @@
 def dot3k(a_high, a_low, b_high, b_low):
     both = jnp.concatenate([a_high, a_low], axis=1)
     return dot(both, jnp.concatenate([b_high, b_high], axis=0)) + dot(a_high, b_low)
+
+
+def note(tab, i, value):
+    tab[pl.ds(i, 1), :] = jnp.full((1, tab.shape[1]), value, jnp.int32)
+
+
+def entry(tab, i):
+    return tab[pl.ds(i, 1), :][0, 0]
 
 
 def load_kernel(devices, cols_hbm, agg_hbm, t_hbm, tab, t_0, t_1, t, cols, agg, rank, sem):
@@ -102,18 +111,18 @@
     rank_rows(2, 2, 4)
     rank_rows(2, 3, 6)
     for j in range(width):
-        tab[LIST_0 + j] = ranked(sent_1, ranked(sent_0 + 1, j))
+        note(tab, LIST_0 + j, ranked(sent_1, ranked(sent_0 + 1, j)))
         for which in (BELOW, ABOVE):
             for k in range(2):
-                tab[SIDE_LAB + 8 * which + 2 * j + k] = agg[col(which, ranked(5 + 2 * which, j), 2 + k)]
+                note(tab, SIDE_LAB + 8 * which + 2 * j + k, agg[col(which, ranked(5 + 2 * which, j), 2 + k)])
     for u in range(rows):
         row = ranked(sent_1 + 1, u)
-        tab[ROW + u] = row
-        tab[NEAR + u] = ranked(sent_1, col(2, row, 1) & (rows - 1))
-        tab[POS2 + u] = ranked(4, col(2, row, 2) & (rows - 1))
-        tab[POS3 + u] = ranked(6, col(2, row, 3) & (rows - 1))
+        note(tab, ROW + u, row)
+        note(tab, NEAR + u, ranked(sent_1, col(2, row, 1) & (rows - 1)))
+        note(tab, POS2 + u, ranked(4, col(2, row, 2) & (rows - 1)))
+        note(tab, POS3 + u, ranked(6, col(2, row, 3) & (rows - 1)))
         for k in range(4):
-            tab[OWN_LAB + 4 * u + k] = agg[col(2, row, k)]
+            note(tab, OWN_LAB + 4 * u + k, agg[col(2, row, k)])
 
 
 def put(value, label, column):
@@ -126,15 +135,15 @@
 
 def near_tile(tab, a, t, dinv, u):
     block = t.shape[1]
-    row = tab[ROW + u]
-    near = tab[ROW + tab[NEAR + u]]
+    row = entry(tab, ROW + u)
+    near = entry(tab, ROW + entry(tab, NEAR + u))
     prod = jnp.concatenate(
         [dot3k(*split(a[row, 0]), *split(t[row])), dot3k(*split(a[row, 1]), *split(t[near]))], axis=1
     )
     smoothed = dot3k(*split(dinv[row]), *split(prod))
     p0 = t[row] - OMEGA * smoothed[:, :block]
     p1 = -OMEGA * smoothed[:, block:]
-    return two_columns(p0, tab[OWN_LAB + 4 * u]) + two_columns(p1, tab[OWN_LAB + 4 * u + 1])
+    return two_columns(p0, entry(tab, OWN_LAB + 4 * u)) + two_columns(p1, entry(tab, OWN_LAB + 4 * u + 1))
 
 
 def near_sent_kernel(tab, a, t, dinv, near_1):
@@ -152,11 +161,11 @@
         own[u] = near_1[u]
         own[width + u] = near_tile(tab, a, t, dinv, width + u)
     for j in range(width):
-        near_0[j] = own[tab[LIST_0 + j]]
+        near_0[j] = own[entry(tab, LIST_0 + j)]
     for u in range(2 * width):
         own_high[u], own_low[u] = split(own[u])
     for u in range(2 * width):
-        row, near = tab[ROW + u], tab[NEAR + u]
+        row, near = entry(tab, ROW + u), entry(tab, NEAR + u)
         a_high[u], a_low[u] = split(jnp.concatenate([a[row, 0], a[row, 1]], axis=1))
         part[u] = dot3(a_high[u], a_low[u], wide(own_high, u, near), wide(own_low, u, near))
 
@@ -169,8 +178,8 @@
         t_high[side, j], t_low[side, j] = split(t_0[j])
         t_high[1 - side, j], t_low[1 - side, j] = split(t_1[j])
     for u in range(rows):
-        row = tab[ROW + u]
-        below, above = tab[POS2 + u], tab[POS3 + u]
+        row = entry(tab, ROW + u)
+        below, above = entry(tab, POS2 + u), entry(tab, POS3 + u)
         a2, a3 = split(a[row, 2]), split(a[row, 3])
         a_high[u] = jnp.concatenate([a2[0], a3[0]], axis=1)
         a_low[u] = jnp.concatenate([a2[1], a3[1]], axis=1)
@@ -186,7 +195,7 @@
         far[u, ABOVE] = both[:, block:]
     for j in range(width):
         far_1[j] = far[j]
-        far_0[j] = far[tab[LIST_0 + j]]
+        far_0[j] = far[entry(tab, LIST_0 + j)]
 
 
 def store_turned(trans, label, place, value):
@@ -198,7 +207,7 @@
 def turn(tab, far, side, trans_high, trans_low):
     for u in range(far.shape[0]):
         block = far.shape[2]
-        label = tab[OWN_LAB + 4 * u + 2 + side]
+        label = entry(tab, OWN_LAB + 4 * u + 2 + side)
         high, low = split(far[u, side])
         place = slice(u * block, (u + 1) * block)
         store_turned(trans_high, label, place, high)
@@ -214,13 +223,13 @@
     half = 2 * block
     for u in range(rows):
         for side in (BELOW, ABOVE):
-            label = tab[OWN_LAB + 4 * u + 2 + side]
+            label = entry(tab, OWN_LAB + 4 * u + 2 + side)
             high, low = split(far[u, side])
             far_high[side, u] = two_columns(high, label)
             far_low[side, u] = two_columns(low, label)
     turn(tab, far, 1 - pair_side(), trans_high, trans_low)
     for u in range(rows):
-        near = tab[NEAR + u]
+        near = entry(tab, NEAR + u)
         for side in (BELOW, ABOVE):
             part[u, :, side * half : (side + 1) * half] = dot3(
                 a_high[u], a_low[u], wide(far_high.at[side], u, near), wide(far_low.at[side], u, near)
@@ -248,7 +257,7 @@
         p_high[side, j], p_low[side, j] = split(near_0[j])
         p_high[1 - side, j], p_low[1 - side, j] = split(near_1[j])
     for u in range(rows):
-        pos2, pos3 = tab[POS2 + u], tab[POS3 + u]
+        pos2, pos3 = entry(tab, POS2 + u), entry(tab, POS3 + u)
         a2 = a_high[u, :, :block], a_low[u, :, :block]
         a3 = a_high[u, :, block:], a_low[u, :, block:]
         low = part[u, :, :half] + dot3k(*a2, p_high[BELOW, pos2], p_low[BELOW, pos2])
@@ -273,12 +282,12 @@
             p_high[side, j, :, cols], p_low[side, j, :, cols] = split(far_0[j, q])
             p_high[1 - side, j, :, cols], p_low[1 - side, j, :, cols] = split(far_1[j, q])
     for u in range(rows):
-        pos2, pos3 = tab[POS2 + u], tab[POS3 + u]
+        pos2, pos3 = entry(tab, POS2 + u), entry(tab, POS3 + u)
         a2 = a_high[u, :, :block], a_low[u, :, :block]
         a3 = a_high[u, :, block:], a_low[u, :, block:]
         left = dot3k(*a2, p_high[BELOW, pos2], p_low[BELOW, pos2])
         right = dot3k(*a3, p_high[ABOVE, pos3], p_low[ABOVE, pos3])
-        labels = [tab[SIDE_LAB + 8 * which + 2 * pos + k] for which, pos in ((BELOW, pos2), (ABOVE, pos3)) for k in (0, 1)]
+        labels = [entry(tab, SIDE_LAB + 8 * which + 2 * pos + k) for which, pos in ((BELOW, pos2), (ABOVE, pos3)) for k in (0, 1)]
         own = part[u] + two_columns(left[:, block:], labels[1]) + two_columns(right[:, :block], labels[2])
         place = slice(u * block, (u + 1) * block)
         ap_high[place, half : 2 * half], ap_low[place, half : 2 * half] = split(own)
@@ -388,14 +397,13 @@
     both_sides(run)
 
 
-SMEM = pl.BlockSpec(memory_space=pltpu.SMEM)
 VMEM = pl.BlockSpec(memory_space=pltpu.VMEM)
 HBM = pl.BlockSpec(memory_space=pltpu.HBM)
 
 
 def call(body, outs, ins, scratch=(), micros=1.0, in_hbm=(), out_hbm=(), aliases={}):
     def specs(values, in_place):
-        return [HBM if i in in_place else SMEM if x.dtype == jnp.int32 else VMEM for i, x in enumerate(values)]
+        return [HBM if i in in_place else VMEM for i, x in enumerate(values)]
 
     return pl.pallas_call(
         body,
@@ -422,7 +430,7 @@
 
     tab, t_0, t_1, t = call(
         functools.partial(load_kernel, devices),
-        [shape((TAB,), jnp.int32)] + [full(width, block, block)] * 2 + [full(*t_blocks.shape)],
+        [shape((TAB, LANES), jnp.int32)] + [full(width, block, block)] * 2 + [full(*t_blocks.shape)],
         [pltpu.with_memory_space_constraint(x, pltpu.HBM) for x in (cols, t_agg, t_blocks)],
         [
             pltpu.SMEM((3 * 4 * ROW_CHUNK,), jnp.int32),

time: 63.8 us -> 61.7 us (0.967)
  Pallas kernels: 23.5 us -> 19.5 us
  waiting for transfers between devices: 15.6 us -> 17.8 us
    pallas_call x11, Pallas kernels: 23.5 us -> 19.5 us  [call(): pl.pallas_call(body, out_shape=outs, in_specs=specs(ins, in_hbm), out_spe...]
    ppermute x9, waiting for transfers between devices: 15.6 us -> 17.8 us  [exchanged(): return lax.ppermute(value, AXES, pairs)]
  transfers between devices with their start and end apart: 9 -> 9, of which waited for: 2 -> 4; matrix products, arithmetic and copies ran while one was open for 0% -> 0% of each run, Pallas kernels for 22% -> 19%
where the time goes in v5:
time: 61.7 us; the launch traced here: 61.6 us
  starting transfers between devices  24 us (39%)
  Pallas kernels  19.5 us (32%)
  waiting for transfers between devices  17.8 us (29%)
    ppermute x9, starting transfers between devices, exchanged(): return lax.ppermute(value, AXES, pairs)  24 us
    pallas_call x11, Pallas kernels, call(): pl.pallas_call(body, out_shape=outs, in_specs=specs(ins, in_hbm), out_spe...  19.5 us
    ppermute x9, waiting for transfers between devices, exchanged(): return lax.ppermute(value, AXES, pairs)  17.8 us
  transfers between devices with their start and end apart: 9, of which 4 were waited for; matrix products, arithmetic and copies ran while one was open for 0% of the time, Pallas kernels for 19%

profile of v5, /device:TPU:0, one launch (start us, length us, event | category | flops | bytes accessed | tf_op | source)
XLA Modules:
  0.0 61.6 jit_solution(6581061096256392229)
XLA Ops:
  0.0 1.5 %shard_map.64 = (s32[88,128]{1,0:T(8,128)S(1)}, f32[4,128,128]{2,1,0:T(8,128)S(1)}, f32[4,128,128]{2,1,0:T(8,128)S(1)}, f32[8,128,128]{2,1,0:T(8,128)S(1)}) custom-call(s32[4096]{0:T(1024)} %bitcast.5, s32[1024]{0:T(1024)} %agg_hbm.1, f32[8,128,128]{2,1,0:T(8,128)} %t_hbm.1), custom_call_target="tpu_custom_call" | custom-call | flops 3000000000 | bytes 1048576 | tf_op jit(solution)/shard_map/pallas_call | solution.py:408
  1.5 0.1 collective-permute-start
  1.6 8.9 %collective-permute-start.1 = (f32[4,128,128]{2,1,0:T(8,128)S(1)}, f32[4,128,128]{2,1,0:T(8,128)S(1)}, u32[]{:S(2)}, u32[]{:S(2)}) collective-permute-start(f32[4,128,128]{2,1,0:T(8,128)S(1)} %get-tuple-element.34), channel_id=1, source_target_pairs={{1,2},{2,1},{3,4},{4,3},{5,6},{6,5},{7,8},{8,7},{9,10},{10,9},{11,... | collective-permute-start | bytes 786440 | tf_op jit(solution)/shard_map/ppermute | solution.py:27
  10.5 0.0 copy-done.1
  10.5 0.0 copy-done.2
  10.5 1.1 %shard_map.65.near_1 = f32[4,128,256]{2,1,0:T(8,128)S(1)} custom-call(s32[88,128]{1,0:T(8,128)S(1)} %get-tuple-element.30.tab, f32[8,4,128,128]{3,2,1,0:T(8,128)S(1)} %copy-done.1, f32[8,128,128]{2,1,0:T(8,128)S(1)} %get-tuple-element.31.t, f32[8,128,128]{2,1,0:T(8,128)S(1)} %copy-done.2), custom_call_target="tpu_custom_call" | custom-call | flops 2000000000 | bytes 1048576 | tf_op jit(solution)/shard_map/pallas_call | solution.py:408
  11.6 0.1 collective-permute-start.3
  11.7 1.9 %shard_map.66 = (f32[4,128,256]{2,1,0:T(8,128)S(1)}, f32[8,128,256]{2,1,0:T(8,128)S(1)}, f32[8,128,256]{2,1,0:T(8,128)S(1)}, bf16[8,128,256]{2,1,0:T(8,128)(2,1)S(1)}, bf16[8,128,256]{2,1,0:T(8,128)(2,1)S(1)}) custom-call(s32[88,128]{1,0:T(8,128)S(1)} %get-tuple-element.30.tab, f32[8,4,128,128]{3,2,1,0:T(8,128)S(1)} %copy-done.1, ...), custom_call_target="tpu_custom_call" | custom-call | flops 2000000000 | bytes 1048576 | tf_op jit(solution)/shard_map/pallas_call | solution.py:408
  13.6 0.1 collective-permute-start.2
  13.7 0.0 collective-permute-done.t_0
  13.7 0.9 %collective-permute-done.1.t_1 = f32[4,128,128]{2,1,0:T(8,128)S(1)} collective-permute-done((f32[4,128,128]{2,1,0:T(8,128)S(1)}, f32[4,128,128]{2,1,0:T(8,128)S(1)}, u32[]{:S(2)}, u32[]{:S(2)}) %collective-permute-start.1) | collective-permute-done | bytes 262176 | tf_op jit(solution)/shard_map/ppermute | solution.py:27
  14.5 2.1 %shard_map.67 = (f32[4,2,128,128]{3,2,1,0:T(8,128)S(1)}, f32[4,2,128,128]{3,2,1,0:T(8,128)S(1)}, f32[8,2,128,128]{3,2,1,0:T(8,128)S(1)}, bf16[8,128,256]{2,1,0:T(8,128)(2,1)S(1)}, bf16[8,128,256]{2,1,0:T(8,128)(2,1)S(1)}) custom-call(s32[88,128]{1,0:T(8,128)S(1)} %get-tuple-element.30.tab, f32[8,4,128,128]{3,2,1,0:T(8,128)S(1)} %copy-done.1, ...), custom_call_target="tpu_custom_call" | custom-call | flops 2000000000 | bytes 1048576 | tf_op jit(solution)/shard_map/pallas_call | solution.py:408
  16.6 0.1 collective-permute-start.4
  16.7 7.4 %collective-permute-start.5 = (f32[4,2,128,128]{3,2,1,0:T(8,128)S(1)}, f32[4,2,128,128]{3,2,1,0:T(8,128)S(1)}, u32[]{:S(2)}, u32[]{:S(2)}) collective-permute-start(f32[4,2,128,128]{3,2,1,0:T(8,128)S(1)} %get-tuple-element.48), channel_id=1, source_target_pairs={{1,2},{2,1},{3,4},{4,3},{5,6},{6,5},{7,8},{8,7},{9,10},{10,9},{11,... | collective-permute-start | bytes 1572872 | tf_op jit(solution)/shard_map/ppermute | solution.py:27
  24.1 1.4 %shard_map.68 = (f32[8,128,512]{2,1,0:T(8,128)S(1)}, bf16[256,1024]{1,0:T(8,128)(2,1)S(1)}, bf16[256,1024]{1,0:T(8,128)(2,1)S(1)}) custom-call(s32[88,128]{1,0:T(8,128)S(1)} %get-tuple-element.30.tab, bf16[8,128,256]{2,1,0:T(8,128)(2,1)S(1)} %get-tuple-element.37.a_high, bf16[8,128,256]{2,1,0:T(8,128)(2,1)S(1)} %get-tuple-element.38.a_low, ...), custom_call_target="tpu_custom_call" | custom-call | flops 3000000000 | bytes 1048576 | tf_op jit(solution)/shard_map/pallas_call | solution.py:408
  25.6 0.2 collective-permute-done.3.near_1
  25.7 0.0 collective-permute-done.2.near_0
  25.7 1.8 %shard_map.69 = (bf16[1024,512]{1,0:T(8,128)(2,1)S(1)}, bf16[1024,512]{1,0:T(8,128)(2,1)S(1)}, f32[256,512]{1,0:T(8,128)S(1)}) custom-call(s32[88,128]{1,0:T(8,128)S(1)} %get-tuple-element.30.tab, bf16[8,128,256]{2,1,0:T(8,128)(2,1)S(1)} %get-tuple-element.35.a_high, bf16[8,128,256]{2,1,0:T(8,128)(2,1)S(1)} %get-tuple-element.36.a_low, ...), custom_call_target="tpu_custom_call" | custom-call | flops 3000000000 | bytes 1048576 | tf_op jit(solution)/shard_map/pallas_call | solution.py:408
  27.5 0.0 collective-permute-done.4.far_0
  27.6 3.8 %collective-permute-done.5.far_1 = f32[4,2,128,128]{3,2,1,0:T(8,128)S(1)} collective-permute-done((f32[4,2,128,128]{3,2,1,0:T(8,128)S(1)}, f32[4,2,128,128]{3,2,1,0:T(8,128)S(1)}, u32[]{:S(2)}, u32[]{:S(2)}) %collective-permute-start.5) | collective-permute-done | bytes 524320 | tf_op jit(solution)/shard_map/ppermute | solution.py:27
  31.3 2.4 %shard_map.70 = (bf16[1024,768]{1,0:T(8,128)(2,1)S(1)}, bf16[1024,768]{1,0:T(8,128)(2,1)S(1)}, f32[256,768]{1,0:T(8,128)S(1)}) custom-call(s32[88,128]{1,0:T(8,128)S(1)} %get-tuple-element.30.tab, bf16[8,128,256]{2,1,0:T(8,128)(2,1)S(1)} %get-tuple-element.35.a_high, bf16[8,128,256]{2,1,0:T(8,128)(2,1)S(1)} %get-tuple-element.36.a_low, ...), custom_call_target="tpu_custom_call" | custom-call | flops 3000000000 | bytes 1048576 | tf_op jit(solution)/shard_map/pallas_call | solution.py:408
  33.7 2.6 %shard_map.72 = f32[256,1280]{1,0:T(8,128)S(1)} custom-call(s32[88,128]{1,0:T(8,128)S(1)} %get-tuple-element.30.tab, f32[8,2,128,128]{3,2,1,0:T(8,128)S(1)} %get-tuple-element.39.far, bf16[1024,512]{1,0:T(8,128)(2,1)S(1)} %get-tuple-element.44.after.ap1_high, bf16[1024,512]{1,0:T(8,128)(2,1)S(1)} %get-tuple-element.45.ap1_low, ...), custom_call_target="tpu_custom_call" | custom-call | flops 2000000000 | bytes 1048576 | tf_op jit(solution)/shard_map/pallas_call | solution.py:408
  36.3 0.1 collective-permute-start.6
  36.4 6.9 %collective-permute-start.8 = (f32[256,768]{1,0:T(8,128)S(1)}, f32[256,768]{1,0:T(8,128)S(1)}, u32[]{:S(2)}, u32[]{:S(2)}) collective-permute-start(f32[256,768]{1,0:T(8,128)S(1)} %get-tuple-element.53), channel_id=1, source_target_pairs={{1,2},{2,1},{3,4},{4,3},{5,6},{6,5},{7,8},{8,7},{9,10},{10,9},{11,... | collective-permute-start | bytes 2359304 | tf_op jit(solution)/shard_map/ppermute | solution.py:27
  43.3 0.4 collective-permute-start.7
  43.6 2.3 %shard_map.71.own = f32[256,1280]{1,0:T(8,128)S(1)} custom-call(f32[8,128,256]{2,1,0:T(8,128)S(1)} %get-tuple-element.32.after.own, bf16[1024,512]{1,0:T(8,128)(2,1)S(1)} %get-tuple-element.44.after.ap1_high, bf16[1024,512]{1,0:T(8,128)(2,1)S(1)} %get-tuple-element.45.ap1_low, bf16[1024,768]{1,0:T(8,128)(2,1)S(1)} %get-tuple-element.49.ap2_high, ...), custom_call_target="tpu_custom_call" | custom-call | flops 2000000000 | bytes 1048576 | tf_op jit(solution)/shard_map/pallas_call | solution.py:408
  46.0 12.9 %collective-permute-done.7.first_1 = f32[256,512]{1,0:T(8,128)S(1)} collective-permute-done((f32[256,512]{1,0:T(8,128)S(1)}, f32[256,512]{1,0:T(8,128)S(1)}, u32[]{:S(2)}, u32[]{:S(2)}) %collective-permute-start.7) | collective-permute-done | bytes 524320 | tf_op jit(solution)/shard_map/ppermute | solution.py:27
  58.9 0.0 collective-permute-done.6.both_0
  58.9 0.0 copy-done
  58.9 1.3 %shard_map.73 = (f32[2,14,128,128]{3,2,1,0:T(8,128)}, f32[2,3,128,256]{3,2,1,0:T(8,128)S(1)}) custom-call(f32[2,128,128]{2,1,0:T(8,128)S(1)} %copy-done, f32[256,1280]{1,0:T(8,128)S(1)} %shard_map.71.own, f32[256,1280]{1,0:T(8,128)S(1)} %collective-permute-done.6.both_0, f32[256,512]{1,0:T(8,128)S(1)} %collective-permute-done.7.first_1), custom_call_target="tpu_custom_call" | custom-call | flops 2000000000 | bytes 1048576 | tf_op jit(solution)/shard_map/pallas_call | solution.py:408
  60.2 0.0 collective-permute-done.8.second_1
  60.2 1.2 %shard_map.74 = f32[2,14,128,128]{3,2,1,0:T(8,128)} custom-call(f32[2,128,128]{2,1,0:T(8,128)S(1)} %copy-done, f32[2,3,128,256]{3,2,1,0:T(8,128)S(1)} %get-tuple-element.52.waiting, f32[256,768]{1,0:T(8,128)S(1)} %collective-permute-done.8.second_1, f32[2,14,128,128]{3,2,1,0:T(8,128)} %get-tuple-element.54.partly), custom_call_target="tpu_custom_call", output_to_operand_aliasing={{}: (3, {})} | custom-call | flops 1000000000 | bytes 1048576 | tf_op jit(solution)/shard_map/pallas_call | solution.py:408
  (3 shorter events, 0.0 us)
Async XLA Ops:
  0.0 10.5 %copy-start.1 = (f32[8,4,128,128]{3,2,1,0:T(8,128)S(1)}, f32[8,4,128,128]{3,2,1,0:T(8,128)}, u32[]{:S(2)}) copy-start(f32[8,4,128,128]{3,2,1,0:T(8,128)} %a.5) | copy-start | bytes 6291460
  0.0 10.5 %copy-start.2 = (f32[8,128,128]{2,1,0:T(8,128)S(1)}, f32[8,128,128]{2,1,0:T(8,128)}, u32[]{:S(2)}) copy-start(f32[8,128,128]{2,1,0:T(8,128)} %dinv.5) | copy-start | bytes 1572868
  1.5 12.2 %collective-permute-start = (f32[4,128,128]{2,1,0:T(8,128)S(1)}, f32[4,128,128]{2,1,0:T(8,128)S(1)}, u32[]{:S(2)}, u32[]{:S(2)}) collective-permute-start(f32[4,128,128]{2,1,0:T(8,128)S(1)} %get-tuple-element.33), channel_id=1, source_target_pairs={{0,1},{1,0},{2,3},{3,2},{4,5},{5,4},{6,7},{7,6},{8,9},{9,8},{10,11... | collective-permute-start | bytes 786440 | tf_op jit(solution)/shard_map/ppermute | solution.py:27
  1.6 12.9 %collective-permute-start.1 = (f32[4,128,128]{2,1,0:T(8,128)S(1)}, f32[4,128,128]{2,1,0:T(8,128)S(1)}, u32[]{:S(2)}, u32[]{:S(2)}) collective-permute-start(f32[4,128,128]{2,1,0:T(8,128)S(1)} %get-tuple-element.34), channel_id=1, source_target_pairs={{1,2},{2,1},{3,4},{4,3},{5,6},{6,5},{7,8},{8,7},{9,10},{10,9},{11,... | collective-permute-start | bytes 786440 | tf_op jit(solution)/shard_map/ppermute | solution.py:27
  11.6 14.1 %collective-permute-start.3 = (f32[4,128,256]{2,1,0:T(8,128)S(1)}, f32[4,128,256]{2,1,0:T(8,128)S(1)}, u32[]{:S(2)}, u32[]{:S(2)}) collective-permute-start(f32[4,128,256]{2,1,0:T(8,128)S(1)} %shard_map.65.near_1), channel_id=1, source_target_pairs={{1,2},{2,1},{3,4},{4,3},{5,6},{6,5},{7,8},{8,7},{9,10},{10,9},{11,... | collective-permute-start | bytes 1572872 | tf_op jit(solution)/shard_map/ppermute | solution.py:27
  13.6 12.2 %collective-permute-start.2 = (f32[4,128,256]{2,1,0:T(8,128)S(1)}, f32[4,128,256]{2,1,0:T(8,128)S(1)}, u32[]{:S(2)}, u32[]{:S(2)}) collective-permute-start(f32[4,128,256]{2,1,0:T(8,128)S(1)} %get-tuple-element.43), channel_id=1, source_target_pairs={{0,1},{1,0},{2,3},{3,2},{4,5},{5,4},{6,7},{7,6},{8,9},{9,8},{10,11... | collective-permute-start | bytes 1572872 | tf_op jit(solution)/shard_map/ppermute | solution.py:27
  16.6 10.9 %collective-permute-start.4 = (f32[4,2,128,128]{3,2,1,0:T(8,128)S(1)}, f32[4,2,128,128]{3,2,1,0:T(8,128)S(1)}, u32[]{:S(2)}, u32[]{:S(2)}) collective-permute-start(f32[4,2,128,128]{3,2,1,0:T(8,128)S(1)} %get-tuple-element.47), channel_id=1, source_target_pairs={{0,1},{1,0},{2,3},{3,2},{4,5},{5,4},{6,7},{7,6},{8,9},{9,8},{10,11... | collective-permute-start | bytes 1572872 | tf_op jit(solution)/shard_map/ppermute | solution.py:27
  16.7 14.6 %collective-permute-start.5 = (f32[4,2,128,128]{3,2,1,0:T(8,128)S(1)}, f32[4,2,128,128]{3,2,1,0:T(8,128)S(1)}, u32[]{:S(2)}, u32[]{:S(2)}) collective-permute-start(f32[4,2,128,128]{3,2,1,0:T(8,128)S(1)} %get-tuple-element.48), channel_id=1, source_target_pairs={{1,2},{2,1},{3,4},{4,3},{5,6},{6,5},{7,8},{8,7},{9,10},{10,9},{11,... | collective-permute-start | bytes 1572872 | tf_op jit(solution)/shard_map/ppermute | solution.py:27
  36.3 22.6 %collective-permute-start.6 = (f32[256,1280]{1,0:T(8,128)S(1)}, f32[256,1280]{1,0:T(8,128)S(1)}, u32[]{:S(2)}, u32[]{:S(2)}) collective-permute-start(f32[256,1280]{1,0:T(8,128)S(1)} %shard_map.72), channel_id=1, source_target_pairs={{0,1},{1,0},{2,3},{3,2},{4,5},{5,4},{6,7},{7,6},{8,9},{9,8},{10,11... | collective-permute-start | bytes 3932168 | tf_op jit(solution)/shard_map/ppermute | solution.py:27
  36.4 23.9 %collective-permute-start.8 = (f32[256,768]{1,0:T(8,128)S(1)}, f32[256,768]{1,0:T(8,128)S(1)}, u32[]{:S(2)}, u32[]{:S(2)}) collective-permute-start(f32[256,768]{1,0:T(8,128)S(1)} %get-tuple-element.53), channel_id=1, source_target_pairs={{1,2},{2,1},{3,4},{4,3},{5,6},{6,5},{7,8},{8,7},{9,10},{10,9},{11,... | collective-permute-start | bytes 2359304 | tf_op jit(solution)/shard_map/ppermute | solution.py:27
  43.3 15.6 %copy-start = (f32[2,128,128]{2,1,0:T(8,128)S(1)}, f32[2,128,128]{2,1,0:T(8,128)}, u32[]{:S(2)}) copy-start(f32[2,128,128]{2,1,0:T(8,128)} %inverse.3) | copy-start | bytes 393220
  43.3 15.6 %collective-permute-start.7 = (f32[256,512]{1,0:T(8,128)S(1)}, f32[256,512]{1,0:T(8,128)S(1)}, u32[]{:S(2)}, u32[]{:S(2)}) collective-permute-start(f32[256,512]{1,0:T(8,128)S(1)} %get-tuple-element.51), channel_id=1, source_target_pairs={{1,2},{2,1},{3,4},{4,3},{5,6},{6,5},{7,8},{8,7},{9,10},{10,9},{11,... | collective-permute-start | bytes 1572872 | tf_op jit(solution)/shard_map/ppermute | solution.py:27

commit v6 on v5

--- a/solution.py
+++ b/solution.py
@@ -170,32 +170,31 @@
         part[u] = dot3(a_high[u], a_low[u], wide(own_high, u, near), wide(own_low, u, near))
 
 
-def far_kernel(tab, a, dinv, t_0, t_1, after, far_0, far_1, far, a_high, a_low, t_high, t_low):
-    rows, block = dinv.shape[0], dinv.shape[1]
-    width = rows // 2
-    side = pair_side()
-    for j in range(width):
-        t_high[side, j], t_low[side, j] = split(t_0[j])
-        t_high[1 - side, j], t_low[1 - side, j] = split(t_1[j])
-    for u in range(rows):
-        row = entry(tab, ROW + u)
-        below, above = entry(tab, POS2 + u), entry(tab, POS3 + u)
-        a2, a3 = split(a[row, 2]), split(a[row, 3])
-        a_high[u] = jnp.concatenate([a2[0], a3[0]], axis=1)
-        a_low[u] = jnp.concatenate([a2[1], a3[1]], axis=1)
-        prod = jnp.concatenate(
-            [
-                dot3k(*a2, t_high[BELOW, below], t_low[BELOW, below]),
-                dot3k(*a3, t_high[ABOVE, above], t_low[ABOVE, above]),
-            ],
-            axis=1,
-        )
-        both = -OMEGA * dot3k(*split(dinv[row]), *split(prod))
-        far[u, BELOW] = both[:, :block]
-        far[u, ABOVE] = both[:, block:]
-    for j in range(width):
-        far_1[j] = far[j]
-        far_0[j] = far[entry(tab, LIST_0 + j)]
+def far_blocks(tab, a, dinv, t_high, t_low, u):
+    row = entry(tab, ROW + u)
+    prod = jnp.concatenate(
+        [
+            dot3k(*split(a[row, 2 + which]), t_high[which, pos], t_low[which, pos])
+            for which, pos in ((BELOW, entry(tab, POS2 + u)), (ABOVE, entry(tab, POS3 + u)))
+        ],
+        axis=1,
+    )
+    return -OMEGA * dot3k(*split(dinv[row]), *split(prod))
+
+
+def split_both(side, value_0, value_1, high, low):
+    for j in range(value_0.shape[0]):
+        high[side, j], low[side, j] = split(value_0[j])
+        high[1 - side, j], low[1 - side, j] = split(value_1[j])
+
+
+def far_sent_kernel(tab, a, dinv, t_0, t_1, after, far_1, t_high, t_low):
+    block = dinv.shape[1]
+    split_both(pair_side(), t_0, t_1, t_high, t_low)
+    for u in range(far_1.shape[0]):
+        both = far_blocks(tab, a, dinv, t_high, t_low, u)
+        far_1[u, BELOW] = both[:, :block]
+        far_1[u, ABOVE] = both[:, block:]
 
 
 def store_turned(trans, label, place, value):
@@ -214,115 +213,140 @@
         store_turned(trans_low, label, place, low)
 
 
-def pre_kernel(
-    tab, a_high, a_low, far,
-    part, trans_high, trans_low,
-    far_high, far_low,
+def coarse_group(trans_high, trans_low, ap_high, ap_low):
+    return dot3(trans_high[...], trans_low[...], ap_high[...], ap_low[...])
+
+
+def mid_kernel(
+    tab, a, dinv, t_0, t_1, far_1, a01_high, a01_low, near_0,
+    far_0, far, a_high, a_low, trans_high, trans_low, part, ap_high, ap_low, group,
+    t_high, t_low, far_high, far_low, p_high, p_low,
 ):
     rows, block = far.shape[0], far.shape[2]
-    half = 2 * block
-    for u in range(rows):
-        for side in (BELOW, ABOVE):
-            label = entry(tab, OWN_LAB + 4 * u + 2 + side)
-            high, low = split(far[u, side])
-            far_high[side, u] = two_columns(high, label)
-            far_low[side, u] = two_columns(low, label)
-    turn(tab, far, 1 - pair_side(), trans_high, trans_low)
-    for u in range(rows):
-        near = entry(tab, NEAR + u)
-        for side in (BELOW, ABOVE):
-            part[u, :, side * half : (side + 1) * half] = dot3(
-                a_high[u], a_low[u], wide(far_high.at[side], u, near), wide(far_low.at[side], u, near)
-            )
-
-
-def coarse_rows(trans_high, trans_low, ap_high, ap_low, out, start=0):
-    half = trans_high.shape[0]
-    for c in range(ap_high.shape[1] // half):
-        cols = slice(c * half, (c + 1) * half)
-        out[:, start + c * half : start + (c + 1) * half] = dot3(
-            trans_high[...], trans_low[...], ap_high[:, cols], ap_low[:, cols]
-        )
+    width = rows // 2
+    side = pair_side()
+    split_both(side, t_0, t_1, t_high, t_low)
+    for u in range(width):
+        far[u] = far_1[u]
+        both = far_blocks(tab, a, dinv, t_high, t_low, width + u)
+        far[width + u, BELOW] = both[:, :block]
+        far[width + u, ABOVE] = both[:, block:]
+    for j in range(width):
+        far_0[j] = far[entry(tab, LIST_0 + j)]
+        p_high[j], p_low[j] = split(near_0[j])
+    for u in range(rows):
+        row = entry(tab, ROW + u)
+        for which in (BELOW, ABOVE):
+            a_high[which, u], a_low[which, u] = split(a[row, 2 + which])
+            label = entry(tab, OWN_LAB + 4 * u + 2 + which)
+            high, low = split(far[u, which])
+            far_high[which, u] = two_columns(high, label)
+            far_low[which, u] = two_columns(low, label)
+    turn(tab, far, 1 - side, trans_high, trans_low)
+    for u in range(rows):
+        near, pos = entry(tab, NEAR + u), entry(tab, POS2 + 8 * side + u)
+        place = slice(u * block, (u + 1) * block)
+        mine = [
+            dot3(a01_high[u], a01_low[u], wide(far_high.at[which], u, near), wide(far_low.at[which], u, near))
+            for which in (side, 1 - side)
+        ]
+        part[u] = mine[1]
+        total = mine[0] + dot3k(a_high[side, u], a_low[side, u], p_high[pos], p_low[pos])
+        ap_high[place], ap_low[place] = split(total)
+    group[...] = coarse_group(trans_high, trans_low, ap_high, ap_low)
 
 
 def first_kernel(
-    tab, a_high, a_low, part, trans_high, trans_low, near_0, near_1,
+    tab, a_high, a_low, part, trans_high, trans_low, near_1, group,
     ap_high, ap_low, out_1,
     p_high, p_low,
 ):
-    rows, block = a_high.shape[0], a_high.shape[1]
+    rows, block = part.shape[0], part.shape[1]
     half = 2 * block
-    side = pair_side()
+    side = 1 - pair_side()
+    out_1[:, :half] = group[...]
     for j in range(rows // 2):
-        p_high[side, j], p_low[side, j] = split(near_0[j])
-        p_high[1 - side, j], p_low[1 - side, j] = split(near_1[j])
-    for u in range(rows):
-        pos2, pos3 = entry(tab, POS2 + u), entry(tab, POS3 + u)
-        a2 = a_high[u, :, :block], a_low[u, :, :block]
-        a3 = a_high[u, :, block:], a_low[u, :, block:]
-        low = part[u, :, :half] + dot3k(*a2, p_high[BELOW, pos2], p_low[BELOW, pos2])
-        upp = part[u, :, half:] + dot3k(*a3, p_high[ABOVE, pos3], p_low[ABOVE, pos3])
+        p_high[j], p_low[j] = split(near_1[j])
+    for u in range(rows):
+        pos = entry(tab, POS2 + 8 * side + u)
         place = slice(u * block, (u + 1) * block)
-        ap_high[place, :half], ap_low[place, :half] = split(low)
-        ap_high[place, half:], ap_low[place, half:] = split(upp)
-    coarse_rows(trans_high, trans_low, ap_high, ap_low, out_1)
-
-
-def second_kernel(
-    tab, a_high, a_low, part, trans_high, trans_low, far_0, far_1, after,
-    ap_high, ap_low, out_1,
+        total = part[u] + dot3k(a_high[side, u], a_low[side, u], p_high[pos], p_low[pos])
+        ap_high[place], ap_low[place] = split(total)
+    out_1[:, half:] = coarse_group(trans_high, trans_low, ap_high, ap_low)
+
+
+def take_far(side, far_in, p_high, p_low):
+    block = far_in.shape[2]
+    for j in range(far_in.shape[0]):
+        p_high[j, :, :block], p_low[j, :, :block] = split(far_in[j, 1 - side])
+        p_high[j, :, block:], p_low[j, :, block:] = split(far_in[j, side])
+
+
+def far_columns(tab, side, u, a_high, a_low, p_high, p_low):
+    block = a_high.shape[3]
+    pos = entry(tab, POS2 + 8 * side + u)
+    value = dot3k(a_high[side, u], a_low[side, u], p_high[pos], p_low[pos])
+    labels = SIDE_LAB + 8 * side + 2 * pos
+    here = two_columns(value[:, :block], entry(tab, labels + 1 - side))
+    high, low = split(value[:, block:])
+    label = entry(tab, labels + side)
+    return here, two_columns(high, label), two_columns(low, label)
+
+
+def second_pre_kernel(
+    tab, a_high, a_low, part, trans_high, trans_low, far_0, after,
+    own_part, ap_high, ap_low, group,
     p_high, p_low,
 ):
-    rows, block = a_high.shape[0], a_high.shape[1]
+    rows, block = part.shape[0], part.shape[1]
+    side = pair_side()
+    take_far(side, far_0, p_high, p_low)
+    for u in range(rows):
+        place = slice(u * block, (u + 1) * block)
+        here, ap_high[place], ap_low[place] = far_columns(tab, side, u, a_high, a_low, p_high, p_low)
+        own_part[u] = part[u] + here
+    group[...] = coarse_group(trans_high, trans_low, ap_high, ap_low)
+
+
+def second_kernel(
+    tab, a_high, a_low, own_part, trans_high, trans_low, far_1, group,
+    own_high, own_low, ap_high, ap_low, out_1,
+    p_high, p_low,
+):
+    rows, block = own_part.shape[0], own_part.shape[1]
     half = 2 * block
-    side = pair_side()
-    for j in range(rows // 2):
-        for q in range(2):
-            cols = slice(q * block, (q + 1) * block)
-            p_high[side, j, :, cols], p_low[side, j, :, cols] = split(far_0[j, q])
-            p_high[1 - side, j, :, cols], p_low[1 - side, j, :, cols] = split(far_1[j, q])
-    for u in range(rows):
-        pos2, pos3 = entry(tab, POS2 + u), entry(tab, POS3 + u)
-        a2 = a_high[u, :, :block], a_low[u, :, :block]
-        a3 = a_high[u, :, block:], a_low[u, :, block:]
-        left = dot3k(*a2, p_high[BELOW, pos2], p_low[BELOW, pos2])
-        right = dot3k(*a3, p_high[ABOVE, pos3], p_low[ABOVE, pos3])
-        labels = [entry(tab, SIDE_LAB + 8 * which + 2 * pos + k) for which, pos in ((BELOW, pos2), (ABOVE, pos3)) for k in (0, 1)]
-        own = part[u] + two_columns(left[:, block:], labels[1]) + two_columns(right[:, :block], labels[2])
+    side = 1 - pair_side()
+    out_1[:, :half] = group[...]
+    take_far(side, far_1, p_high, p_low)
+    for u in range(rows):
         place = slice(u * block, (u + 1) * block)
-        ap_high[place, half : 2 * half], ap_low[place, half : 2 * half] = split(own)
-        for cols, value, label in (
-            (slice(0, half), left[:, :block], labels[0]),
-            (slice(2 * half, 3 * half), right[:, block:], labels[3]),
-        ):
-            high, low = split(value)
-            ap_high[place, cols] = two_columns(high, label)
-            ap_low[place, cols] = two_columns(low, label)
-    coarse_rows(trans_high, trans_low, ap_high, ap_low, out_1)
-
-
-def other_kernel(tab, far, ap1_high, ap1_low, ap2_high, ap2_low, out_0, trans_high, trans_low):
+        here, ap_high[place], ap_low[place] = far_columns(tab, side, u, a_high, a_low, p_high, p_low)
+        own_high[place], own_low[place] = split(own_part[u] + here)
+    out_1[:, half : 2 * half] = coarse_group(trans_high, trans_low, own_high, own_low)
+    out_1[:, 2 * half :] = coarse_group(trans_high, trans_low, ap_high, ap_low)
+
+
+def every_group(trans_high, trans_low, aps, out):
+    half = trans_high.shape[0]
+    for i in range(len(aps) // 2):
+        out[:, i * half : (i + 1) * half] = coarse_group(trans_high, trans_low, aps[2 * i], aps[2 * i + 1])
+
+
+def other_kernel(tab, far, *refs):
+    aps, (out_0, trans_high, trans_low) = refs[:10], refs[10:]
     turn(tab, far, pair_side(), trans_high, trans_low)
-    coarse_rows(trans_high, trans_low, ap1_high, ap1_low, out_0)
-    coarse_rows(trans_high, trans_low, ap2_high, ap2_low, out_0, ap1_high.shape[1])
-
-
-HELD = ((1, 0), (0, 0), (1, 1), (0, 1), (1, 2))
-
-
-def own_kernel(own, ap1_high, ap1_low, ap2_high, ap2_low, out, trans_high, trans_low):
+    every_group(trans_high, trans_low, aps, out_0)
+
+
+def own_kernel(own, *refs):
+    aps, (out, trans_high, trans_low) = refs[:10], refs[10:]
     rows, block = own.shape[0], own.shape[1]
-    half = 2 * block
     for u in range(rows):
         place = slice(u * block, (u + 1) * block)
         high, low = split(own[u])
         trans_high[:, place] = high.T
         trans_low[:, place] = low.T
-    aps = (ap1_high, ap1_low), (ap2_high, ap2_low)
-    for d, (which, c) in enumerate(HELD):
-        cols = slice(c * half, (c + 1) * half)
-        high, low = aps[which]
-        out[:, d * half : (d + 1) * half] = dot3(trans_high[...], trans_low[...], high[:, cols], low[:, cols])
+    every_group(trans_high, trans_low, aps, out)
 
 
 def write_slots(inv, total, result, agg, d, out, sem):
@@ -335,66 +359,56 @@
     return copy
 
 
-def both_sides(run):
+OWN_AT, SAME_AT, OTHER_AT = (1, -1, 2, 0, -2), (0, 2, -1, 1, 3), (-2, 0, -3, -1, 1)
+
+
+def both_ways(run):
     side = pair_side()
-    pl.when(side == ABOVE)(lambda: run(ABOVE))
-    pl.when(side == BELOW)(lambda: run(BELOW))
+    pl.when(side == ABOVE)(lambda: run(1))
+    pl.when(side == BELOW)(lambda: run(-1))
 
 
 def early_kernel(inverse, own, both_0, first_1, out, waiting, results, sems):
     block = inverse.shape[1]
     half = 2 * block
 
-    def run(side):
-        shift_0, shift_1 = (1, -1) if side == ABOVE else (-1, 1)
+    def run(way):
         copies = []
         for agg in range(2):
             inv = split(inverse[agg])
             line = slice(agg * block, (agg + 1) * block)
             for d in range(-3, 4):
-                parts, late = [], None
-                if -2 <= d <= 2:
-                    parts.append(own[line, (d + 2) * half : (d + 3) * half])
-                if -2 <= d - shift_0 <= 2:
-                    which, c = HELD[d - shift_0 + 2]
-                    c = c + 2 * which
-                    parts.append(both_0[line, c * half : (c + 1) * half])
-                if -2 <= d - shift_1 <= 2:
-                    which, c = HELD[d - shift_1 + 2]
-                    if which:
-                        late = c
-                    else:
-                        parts.append(first_1[line, c * half : (c + 1) * half])
+                places = [(ref, at.index(d)) for ref, at in ((own, OWN_AT), (both_0, SAME_AT), (first_1, OTHER_AT[:2])) if d in at]
+                parts = [ref[line, i * half : (i + 1) * half] for ref, i in places]
                 total = sum(parts[1:], parts[0]) if parts else jnp.zeros((block, half), F32)
-                if late is not None:
-                    waiting[agg, late] = total
+                if d in OTHER_AT[2:]:
+                    waiting[agg, OTHER_AT.index(d) - 2] = total
                 else:
                     n = len(copies)
-                    copies.append(write_slots(inv, total, results.at[n], agg, d, out, sems.at[n]))
+                    copies.append(write_slots(inv, total, results.at[n], agg, way * d, out, sems.at[n]))
         for copy in copies:
             copy.wait()
 
-    both_sides(run)
+    both_ways(run)
 
 
 def late_kernel(inverse, waiting, second_1, partly, out, results, sems):
     block = inverse.shape[1]
     half = 2 * block
 
-    def run(side):
-        shift = -1 if side == ABOVE else 1
+    def run(way):
         copies = []
         for agg in range(2):
             inv = split(inverse[agg])
             line = slice(agg * block, (agg + 1) * block)
-            for c in range(3):
-                total = waiting[agg, c] + second_1[line, c * half : (c + 1) * half]
+            for i in range(3):
+                total = waiting[agg, i] + second_1[line, i * half : (i + 1) * half]
                 n = len(copies)
-                copies.append(write_slots(inv, total, results.at[n], agg, 2 * c - 2 + shift, out, sems.at[n]))
+                copies.append(write_slots(inv, total, results.at[n], agg, way * OTHER_AT[2 + i], out, sems.at[n]))
         for copy in copies:
             copy.wait()
 
-    both_sides(run)
+    both_ways(run)
 
 
 VMEM = pl.BlockSpec(memory_space=pltpu.VMEM)
@@ -454,49 +468,51 @@
     )
     near_0, near_1 = exchanged(near_0, 0), got_near_1
     sent = full(width, 2, block, block)
-    far_0, far_1, far, a23_high, a23_low = call(
-        far_kernel,
-        [sent, sent, full(rows, 2, block, block)] + pair(rows, block, half),
-        [tab, a, dinv, t_0, t_1, own],
-        two(2, width, block, block),
+    (far_1,) = call(far_sent_kernel, [sent], [tab, a, dinv, t_0, t_1, own], two(2, width, block, block), micros=2)
+    got_far_1 = exchanged(far_1, 1)
+    far_0, far, a23_high, a23_low, out_high, out_low, part, ap_e1_high, ap_e1_low, group = call(
+        mid_kernel,
+        [sent, full(rows, 2, block, block)]
+        + pair(2, rows, block, block)
+        + pair(half, deep)
+        + [full(rows, block, half)]
+        + pair(deep, half)
+        + [full(half, half)],
+        [tab, a, dinv, t_0, t_1, far_1, a01_high, a01_low, near_0],
+        two(2, width, block, block) + two(2, rows, block, half) + two(width, block, half),
+        micros=3,
+    )
+    far_0, far_1 = exchanged(far_0, 0), got_far_1
+    ap_o1_high, ap_o1_low, first_1 = call(
+        first_kernel,
+        pair(deep, half) + [full(half, 2 * half)],
+        [tab, a23_high, a23_low, part, out_high, out_low, near_1, group],
+        two(width, block, half),
         micros=2,
     )
-    far_1 = exchanged(far_1, 1)
-    far_0 = exchanged(far_0, 0)
-    part, out_high, out_low = call(
-        pre_kernel,
-        [full(rows, block, 2 * half)] + pair(half, deep),
-        [tab, a01_high, a01_low, far],
-        two(2, rows, block, half),
-        micros=3,
-    )
-    ap1_high, ap1_low, first_1 = call(
-        first_kernel,
-        pair(deep, 2 * half) + [full(half, 2 * half)],
-        [tab, a23_high, a23_low, part, out_high, out_low, near_0, near_1],
-        two(2, width, block, half),
-        micros=3,
-    )
     first_1 = exchanged(first_1, 1)
-    ap2_high, ap2_low, second_1 = call(
+    part_own, ap_e2_high, ap_e2_low, group = call(
+        second_pre_kernel,
+        [full(rows, block, half)] + pair(deep, half) + [full(half, half)],
+        [tab, a23_high, a23_low, part_own, out_high, out_low, far_0, ap_o1_high],
+        two(width, block, half),
+        micros=2,
+    )
+    ap_own_high, ap_own_low, ap_o2_high, ap_o2_low, second_1 = call(
         second_kernel,
-        pair(deep, 3 * half) + [full(half, 3 * half)],
-        [tab, a23_high, a23_low, part_own, out_high, out_low, far_0, far_1, ap1_high],
-        two(2, width, block, half),
-        micros=3,
+        pair(deep, half) * 2 + [full(half, 3 * half)],
+        [tab, a23_high, a23_low, part_own, out_high, out_low, far_1, group],
+        two(width, block, half),
+        micros=2,
     )
     second_1 = exchanged(second_1, 1)
-    (both_0,) = call(
-        other_kernel,
-        [full(half, 5 * half)],
-        [tab, far, ap1_high, ap1_low, ap2_high, ap2_low],
-        two(half, deep),
-        micros=2,
-    )
+    aps = [
+        ap_e1_high, ap_e1_low, ap_o1_high, ap_o1_low, ap_e2_high, ap_e2_low,
+        ap_own_high, ap_own_low, ap_o2_high, ap_o2_low,
+    ]
+    (both_0,) = call(other_kernel, [full(half, 5 * half)], [tab, far] + aps, two(half, deep), micros=2)
     both_0 = exchanged(both_0, 0)
-    (total,) = call(
-        own_kernel, [full(half, 5 * half)], [own, ap1_high, ap1_low, ap2_high, ap2_low], two(half, deep), micros=2
-    )
+    (total,) = call(own_kernel, [full(half, 5 * half)], [own] + aps, two(half, deep), micros=2)
     result = full(2, 14, block, block)
     partly, waiting = call(
         early_kernel,

time: 61.7 us -> 66.6 us (1.079)
  waiting for transfers between devices: 17.8 us -> 21.6 us
    ppermute x9, waiting for transfers between devices: 17.8 us -> 21.6 us  [exchanged(): return lax.ppermute(value, AXES, pairs)]
    pallas_call x11 -> x12, Pallas kernels: 19.5 us -> 20.1 us  [call(): pl.pallas_call(body, out_shape=outs, in_specs=specs(ins, in_hbm), out_spe...]
  transfers between devices with their start and end apart: 9 -> 9, of which waited for: 4 -> 3; matrix products, arithmetic and copies ran while one was open for 0% -> 0% of each run, Pallas kernels for 19% -> 16%
where the time goes in v6:
time: 66.6 us; the launch traced here: 66.5 us
  starting transfers between devices  24.1 us (36%)
  waiting for transfers between devices  21.6 us (32%)
  Pallas kernels  20.1 us (30%)
    ppermute x9, starting transfers between devices, exchanged(): return lax.ppermute(value, AXES, pairs)  24.1 us
    ppermute x9, waiting for transfers between devices, exchanged(): return lax.ppermute(value, AXES, pairs)  21.6 us
    pallas_call x12, Pallas kernels, call(): pl.pallas_call(body, out_shape=outs, in_specs=specs(ins, in_hbm), out_spe...  20.1 us
  transfers between devices with their start and end apart: 9, of which 3 were waited for; matrix products, arithmetic and copies ran while one was open for 0% of the time, Pallas kernels for 16%

profile of v6, /device:TPU:0, one launch (start us, length us, event | category | flops | bytes accessed | tf_op | source)
XLA Modules:
  0.0 66.5 jit_solution(13151074134548567653)
XLA Ops:
  0.0 1.5 %shard_map.64 = (s32[88,128]{1,0:T(8,128)S(1)}, f32[4,128,128]{2,1,0:T(8,128)S(1)}, f32[4,128,128]{2,1,0:T(8,128)S(1)}, f32[8,128,128]{2,1,0:T(8,128)S(1)}) custom-call(s32[4096]{0:T(1024)} %bitcast.5, s32[1024]{0:T(1024)} %agg_hbm.1, f32[8,128,128]{2,1,0:T(8,128)} %t_hbm.1), custom_call_target="tpu_custom_call" | custom-call | flops 3000000000 | bytes 1048576 | tf_op jit(solution)/shard_map/pallas_call | solution.py:422
  1.5 0.3 copy-done.1
  1.7 0.1 copy-done.2
  1.8 1.1 %shard_map.65.near_1 = f32[4,128,256]{2,1,0:T(8,128)S(1)} custom-call(s32[88,128]{1,0:T(8,128)S(1)} %get-tuple-element.38.tab, f32[8,4,128,128]{3,2,1,0:T(8,128)S(1)} %copy-done.1, f32[8,128,128]{2,1,0:T(8,128)S(1)} %get-tuple-element.39.t, f32[8,128,128]{2,1,0:T(8,128)S(1)} %copy-done.2), custom_call_target="tpu_custom_call" | custom-call | flops 2000000000 | bytes 1048576 | tf_op jit(solution)/shard_map/pallas_call | solution.py:422
  3.0 1.9 %shard_map.66 = (f32[4,128,256]{2,1,0:T(8,128)S(1)}, f32[8,128,256]{2,1,0:T(8,128)S(1)}, f32[8,128,256]{2,1,0:T(8,128)S(1)}, bf16[8,128,256]{2,1,0:T(8,128)(2,1)S(1)}, bf16[8,128,256]{2,1,0:T(8,128)(2,1)S(1)}) custom-call(s32[88,128]{1,0:T(8,128)S(1)} %get-tuple-element.38.tab, f32[8,4,128,128]{3,2,1,0:T(8,128)S(1)} %copy-done.1, ...), custom_call_target="tpu_custom_call" | custom-call | flops 2000000000 | bytes 1048576 | tf_op jit(solution)/shard_map/pallas_call | solution.py:422
  4.9 0.1 collective-permute-start.2
  4.9 0.5 collective-permute-start
  5.4 8.5 %collective-permute-start.1 = (f32[4,128,128]{2,1,0:T(8,128)S(1)}, f32[4,128,128]{2,1,0:T(8,128)S(1)}, u32[]{:S(2)}, u32[]{:S(2)}) collective-permute-start(f32[4,128,128]{2,1,0:T(8,128)S(1)} %get-tuple-element.42), channel_id=1, source_target_pairs={{1,2},{2,1},{3,4},{4,3},{5,6},{6,5},{7,8},{8,7},{9,10},{10,9},{11,... | collective-permute-start | bytes 786440 | tf_op jit(solution)/shard_map/ppermute | solution.py:27
  13.9 0.0 collective-permute-start.3
  14.0 0.0 collective-permute-done.t_0
  14.0 4.0 %collective-permute-done.1.t_1 = f32[4,128,128]{2,1,0:T(8,128)S(1)} collective-permute-done((f32[4,128,128]{2,1,0:T(8,128)S(1)}, f32[4,128,128]{2,1,0:T(8,128)S(1)}, u32[]{:S(2)}, u32[]{:S(2)}) %collective-permute-start.1) | collective-permute-done | bytes 262176 | tf_op jit(solution)/shard_map/ppermute | solution.py:27
  18.0 1.1 %shard_map.67.far_1 = f32[4,2,128,128]{3,2,1,0:T(8,128)S(1)} custom-call(s32[88,128]{1,0:T(8,128)S(1)} %get-tuple-element.38.tab, f32[8,4,128,128]{3,2,1,0:T(8,128)S(1)} %copy-done.1, f32[8,128,128]{2,1,0:T(8,128)S(1)} %copy-done.2, f32[4,128,128]{2,1,0:T(8,128)S(1)} %collective-permute-done.t_0, f32[4,128,128]{2,1,0:T(8,128)S(1)} %collective-permute-done.1.t_1, ...), custom_call_target="tpu_custom_call" | custom-call | flops 2000000000 | bytes 1048576 | tf_op jit(solution)/shard_map/pallas_call | solution.py:422
  19.1 0.0 collective-permute-done.2.near_0
  19.2 3.4 %shard_map.68 = (f32[4,2,128,128]{3,2,1,0:T(8,128)S(1)}, f32[8,2,128,128]{3,2,1,0:T(8,128)S(1)}, bf16[2,8,128,128]{3,2,1,0:T(8,128)(2,1)S(1)}, bf16[2,8,128,128]...) custom-call(s32[88,128]{1,0:T(8,128)S(1)} %get-tuple-element.38.tab,, ...), custom_call_target="tpu_custom_call" | custom-call | flops 3000000000 | bytes 1048576 | tf_op jit(solution)/shard_map/pallas_call | solution.py:422
  22.6 0.1 collective-permute-start.4
  22.7 7.4 %collective-permute-start.5 = (f32[4,2,128,128]{3,2,1,0:T(8,128)S(1)}, f32[4,2,128,128]{3,2,1,0:T(8,128)S(1)}, u32[]{:S(2)}, u32[]{:S(2)}) collective-permute-start(f32[4,2,128,128]{3,2,1,0:T(8,128)S(1)} %shard_map.67.far_1), channel_id=1, source_target_pairs={{1,2},{2,1},{3,4},{4,3},{5,6},{6,5},{7,8},{8,7},{9,10},{10,9},{11,... | collective-permute-start | bytes 1572872 | tf_op jit(solution)/shard_map/ppermute | solution.py:27
  30.1 0.0 collective-permute-done.3.near_1
  30.1 1.0 %shard_map.69 = (bf16[1024,256]{1,0:T(8,128)(2,1)S(1)}, bf16[1024,256]{1,0:T(8,128)(2,1)S(1)}, f32[256,512]{1,0:T(8,128)S(1)}) custom-call(s32[88,128]{1,0:T(8,128)S(1)} %get-tuple-element.38.tab, bf16[2,8,128,128]{3,2,1,0:T(8,128)(2,1)S(1)} %get-tuple-element.48.a_high, bf16[2,8,128,128]{3,2,1,0:T(8,128)(2,1)S(1)} %get-tuple-element.49.a_low, ...), custom_call_target="tpu_custom_call" | custom-call | flops 2000000000 | bytes 1048576 | tf_op jit(solution)/shard_map/pallas_call | solution.py:422
  31.2 0.0 collective-permute-done.4.far_0
  31.2 1.1 %shard_map.70 = (f32[8,128,256]{2,1,0:T(8,128)S(1)}, bf16[1024,256]{1,0:T(8,128)(2,1)S(1)}, bf16[1024,256]{1,0:T(8,128)(2,1)S(1)}, f32[256,256]{1,0:T(8,128)S(1)}) custom-call(s32[88,128]{1,0:T(8,128)S(1)} %get-tuple-element.38.tab, bf16[2,8,128,128]{3,2,1,0:T(8,128)(2,1)S(1)} %get-tuple-element.48.a_high, ...), custom_call_target="tpu_custom_call" | custom-call | flops 2000000000 | bytes 1048576 | tf_op jit(solution)/shard_map/pallas_call | solution.py:422
  32.2 4.7 %collective-permute-done.5.far_1 = f32[4,2,128,128]{3,2,1,0:T(8,128)S(1)} collective-permute-done((f32[4,2,128,128]{3,2,1,0:T(8,128)S(1)}, f32[4,2,128,128]{3,2,1,0:T(8,128)S(1)}, u32[]{:S(2)}, u32[]{:S(2)}) %collective-permute-start.5) | collective-permute-done | bytes 524320 | tf_op jit(solution)/shard_map/ppermute | solution.py:27
  37.0 1.5 %shard_map.71 = (bf16[1024,256]{1,0:T(8,128)(2,1)S(1)}, bf16[1024,256]{1,0:T(8,128)(2,1)S(1)}, bf16[1024,256]{1,0:T(8,128)(2,1)S(1)}, bf16[1024,256]{1,0:T(8,128)(2,1)S(1)}, f32[256,768]{1,0:T(8,128)S(1)}) custom-call(s32[88,128]{1,0:T(8,128)S(1)} %get-tuple-element.38.tab, bf16[2,8,128,128]{3,2,1,0:T(8,128)(2,1)S(1)} %get-tuple-element.48.a_high, ...), custom_call_target="tpu_custom_call" | custom-call | flops 2000000000 | bytes 1048576 | tf_op jit(solution)/shard_map/pallas_call | solution.py:422
  38.5 2.5 %shard_map.73 = f32[256,1280]{1,0:T(8,128)S(1)} custom-call(s32[88,128]{1,0:T(8,128)S(1)} %get-tuple-element.38.tab, f32[8,2,128,128]{3,2,1,0:T(8,128)S(1)} %get-tuple-element.66.far, bf16[1024,256]{1,0:T(8,128)(2,1)S(1)} %get-tuple-element.46.refs_0_, bf16[1024,256]{1,0:T(8,128)(2,1)S(1)} %get-tuple-element.47.refs_1_, ...), custom_call_target="tpu_custom_call" | custom-call | flops 2000000000 | bytes 1048576 | tf_op jit(solution)/shard_map/pallas_call | solution.py:422
  41.1 0.1 collective-permute-start.6
  41.2 7.3 %collective-permute-start.8 = (f32[256,768]{1,0:T(8,128)S(1)}, f32[256,768]{1,0:T(8,128)S(1)}, u32[]{:S(2)}, u32[]{:S(2)}) collective-permute-start(f32[256,768]{1,0:T(8,128)S(1)} %get-tuple-element.69), channel_id=1, source_target_pairs={{1,2},{2,1},{3,4},{4,3},{5,6},{6,5},{7,8},{8,7},{9,10},{10,9},{11,... | collective-permute-start | bytes 2359304 | tf_op jit(solution)/shard_map/ppermute | solution.py:27
  48.4 0.1 collective-permute-start.7
  48.5 2.3 %shard_map.72.own = f32[256,1280]{1,0:T(8,128)S(1)} custom-call(f32[8,128,256]{2,1,0:T(8,128)S(1)} %get-tuple-element.40.after.own, bf16[1024,256]{1,0:T(8,128)(2,1)S(1)} %get-tuple-element.46.refs_0_, bf16[1024,256]{1,0:T(8,128)(2,1)S(1)} %get-tuple-element.47.refs_1_, bf16[1024,256]{1,0:T(8,128)(2,1)S(1)} %get-tuple-element.54.after.refs_2_, ...), custom_call_target="tpu_custom_call" | custom-call | flops 2000000000 | bytes 1048576 | tf_op jit(solution)/shard_map/pallas_call | solution.py:422
  50.9 12.8 %collective-permute-done.7.first_1 = f32[256,512]{1,0:T(8,128)S(1)} collective-permute-done((f32[256,512]{1,0:T(8,128)S(1)}, f32[256,512]{1,0:T(8,128)S(1)}, u32[]{:S(2)}, u32[]{:S(2)}) %collective-permute-start.7) | collective-permute-done | bytes 524320 | tf_op jit(solution)/shard_map/ppermute | solution.py:27
  63.7 0.0 collective-permute-done.6.both_0
  63.7 1.4 %shard_map.74 = (f32[2,14,128,128]{3,2,1,0:T(8,128)}, f32[2,3,128,256]{3,2,1,0:T(8,128)S(1)}) custom-call(f32[2,128,128]{2,1,0:T(8,128)S(1)} %copy-done, f32[256,1280]{1,0:T(8,128)S(1)} %shard_map.72.own, f32[256,1280]{1,0:T(8,128)S(1)} %collective-permute-done.6.both_0, f32[256,512]{1,0:T(8,128)S(1)} %collective-permute-done.7.first_1), custom_call_target="tpu_custom_call" | custom-call | flops 2000000000 | bytes 1048576 | tf_op jit(solution)/shard_map/pallas_call | solution.py:422
  65.1 0.0 collective-permute-done.8.second_1
  65.1 1.2 %shard_map.75 = f32[2,14,128,128]{3,2,1,0:T(8,128)} custom-call(f32[2,128,128]{2,1,0:T(8,128)S(1)} %copy-done, f32[2,3,128,256]{3,2,1,0:T(8,128)S(1)} %get-tuple-element.68.waiting, f32[256,768]{1,0:T(8,128)S(1)} %collective-permute-done.8.second_1, f32[2,14,128,128]{3,2,1,0:T(8,128)} %get-tuple-element.70.partly), custom_call_target="tpu_custom_call", output_to_operand_aliasing={{}: (3, {})} | custom-call | flops 1000000000 | bytes 1048576 | tf_op jit(solution)/shard_map/pallas_call | solution.py:422
  (4 shorter events, 0.0 us)
Async XLA Ops:
  0.0 1.7 %copy-start.1 = (f32[8,4,128,128]{3,2,1,0:T(8,128)S(1)}, f32[8,4,128,128]{3,2,1,0:T(8,128)}, u32[]{:S(2)}) copy-start(f32[8,4,128,128]{3,2,1,0:T(8,128)} %a.7) | copy-start | bytes 6291460
  0.0 1.8 %copy-start.2 = (f32[8,128,128]{2,1,0:T(8,128)S(1)}, f32[8,128,128]{2,1,0:T(8,128)}, u32[]{:S(2)}) copy-start(f32[8,128,128]{2,1,0:T(8,128)} %dinv.7) | copy-start | bytes 1572868
  4.9 14.3 %collective-permute-start.2 = (f32[4,128,256]{2,1,0:T(8,128)S(1)}, f32[4,128,256]{2,1,0:T(8,128)S(1)}, u32[]{:S(2)}, u32[]{:S(2)}) collective-permute-start(f32[4,128,256]{2,1,0:T(8,128)S(1)} %get-tuple-element.45), channel_id=1, source_target_pairs={{0,1},{1,0},{2,3},{3,2},{4,5},{5,4},{6,7},{7,6},{8,9},{9,8},{10,11... | collective-permute-start | bytes 1572872 | tf_op jit(solution)/shard_map/ppermute | solution.py:27
  4.9 9.0 %collective-permute-start = (f32[4,128,128]{2,1,0:T(8,128)S(1)}, f32[4,128,128]{2,1,0:T(8,128)S(1)}, u32[]{:S(2)}, u32[]{:S(2)}) collective-permute-start(f32[4,128,128]{2,1,0:T(8,128)S(1)} %get-tuple-element.41), channel_id=1, source_target_pairs={{0,1},{1,0},{2,3},{3,2},{4,5},{5,4},{6,7},{7,6},{8,9},{9,8},{10,11... | collective-permute-start | bytes 786440 | tf_op jit(solution)/shard_map/ppermute | solution.py:27
  5.4 12.5 %collective-permute-start.1 = (f32[4,128,128]{2,1,0:T(8,128)S(1)}, f32[4,128,128]{2,1,0:T(8,128)S(1)}, u32[]{:S(2)}, u32[]{:S(2)}) collective-permute-start(f32[4,128,128]{2,1,0:T(8,128)S(1)} %get-tuple-element.42), channel_id=1, source_target_pairs={{1,2},{2,1},{3,4},{4,3},{5,6},{6,5},{7,8},{8,7},{9,10},{10,9},{11,... | collective-permute-start | bytes 786440 | tf_op jit(solution)/shard_map/ppermute | solution.py:27
  13.9 16.2 %collective-permute-start.3 = (f32[4,128,256]{2,1,0:T(8,128)S(1)}, f32[4,128,256]{2,1,0:T(8,128)S(1)}, u32[]{:S(2)}, u32[]{:S(2)}) collective-permute-start(f32[4,128,256]{2,1,0:T(8,128)S(1)} %shard_map.65.near_1), channel_id=1, source_target_pairs={{1,2},{2,1},{3,4},{4,3},{5,6},{6,5},{7,8},{8,7},{9,10},{10,9},{11,... | collective-permute-start | bytes 1572872 | tf_op jit(solution)/shard_map/ppermute | solution.py:27
  22.6 8.6 %collective-permute-start.4 = (f32[4,2,128,128]{3,2,1,0:T(8,128)S(1)}, f32[4,2,128,128]{3,2,1,0:T(8,128)S(1)}, u32[]{:S(2)}, u32[]{:S(2)}) collective-permute-start(f32[4,2,128,128]{3,2,1,0:T(8,128)S(1)} %get-tuple-element.57), channel_id=1, source_target_pairs={{0,1},{1,0},{2,3},{3,2},{4,5},{5,4},{6,7},{7,6},{8,9},{9,8},{10,11... | collective-permute-start | bytes 1572872 | tf_op jit(solution)/shard_map/ppermute | solution.py:27
  22.7 14.3 %collective-permute-start.5 = (f32[4,2,128,128]{3,2,1,0:T(8,128)S(1)}, f32[4,2,128,128]{3,2,1,0:T(8,128)S(1)}, u32[]{:S(2)}, u32[]{:S(2)}) collective-permute-start(f32[4,2,128,128]{3,2,1,0:T(8,128)S(1)} %shard_map.67.far_1), channel_id=1, source_target_pairs={{1,2},{2,1},{3,4},{4,3},{5,6},{6,5},{7,8},{8,7},{9,10},{10,9},{11,... | collective-permute-start | bytes 1572872 | tf_op jit(solution)/shard_map/ppermute | solution.py:27
  41.1 22.6 %collective-permute-start.6 = (f32[256,1280]{1,0:T(8,128)S(1)}, f32[256,1280]{1,0:T(8,128)S(1)}, u32[]{:S(2)}, u32[]{:S(2)}) collective-permute-start(f32[256,1280]{1,0:T(8,128)S(1)} %shard_map.73), channel_id=1, source_target_pairs={{0,1},{1,0},{2,3},{3,2},{4,5},{5,4},{6,7},{7,6},{8,9},{9,8},{10,11... | collective-permute-start | bytes 3932168 | tf_op jit(solution)/shard_map/ppermute | solution.py:27
  41.2 23.9 %collective-permute-start.8 = (f32[256,768]{1,0:T(8,128)S(1)}, f32[256,768]{1,0:T(8,128)S(1)}, u32[]{:S(2)}, u32[]{:S(2)}) collective-permute-start(f32[256,768]{1,0:T(8,128)S(1)} %get-tuple-element.69), channel_id=1, source_target_pairs={{1,2},{2,1},{3,4},{4,3},{5,6},{6,5},{7,8},{8,7},{9,10},{10,9},{11,... | collective-permute-start | bytes 2359304 | tf_op jit(solution)/shard_map/ppermute | solution.py:27
  48.4 15.3 %copy-start = (f32[2,128,128]{2,1,0:T(8,128)S(1)}, f32[2,128,128]{2,1,0:T(8,128)}, u32[]{:S(2)}) copy-start(f32[2,128,128]{2,1,0:T(8,128)} %inverse.3) | copy-start | bytes 393220
  48.4 15.3 %collective-permute-start.7 = (f32[256,512]{1,0:T(8,128)S(1)}, f32[256,512]{1,0:T(8,128)S(1)}, u32[]{:S(2)}, u32[]{:S(2)}) collective-permute-start(f32[256,512]{1,0:T(8,128)S(1)} %get-tuple-element.67), channel_id=1, source_target_pairs={{1,2},{2,1},{3,4},{4,3},{5,6},{6,5},{7,8},{8,7},{9,10},{10,9},{11,... | collective-permute-start | bytes 1572872 | tf_op jit(solution)/shard_map/ppermute | solution.py:27

commit v7 on v6

--- a/solution.py
+++ b/solution.py
@@ -133,53 +133,61 @@
     return jnp.concatenate([put(value, label, 0), put(value, label, 1)], axis=1)
 
 
-def near_tile(tab, a, t, dinv, u):
+def near_tiles(tab, a, t, dinv, order):
     block = t.shape[1]
-    row = entry(tab, ROW + u)
-    near = entry(tab, ROW + entry(tab, NEAR + u))
-    prod = jnp.concatenate(
-        [dot3k(*split(a[row, 0]), *split(t[row])), dot3k(*split(a[row, 1]), *split(t[near]))], axis=1
-    )
-    smoothed = dot3k(*split(dinv[row]), *split(prod))
-    p0 = t[row] - OMEGA * smoothed[:, :block]
-    p1 = -OMEGA * smoothed[:, block:]
-    return two_columns(p0, entry(tab, OWN_LAB + 4 * u)) + two_columns(p1, entry(tab, OWN_LAB + 4 * u + 1))
+    rows = [entry(tab, ROW + u) for u in order]
+    prods = []
+    for u, row in zip(order, rows):
+        near = entry(tab, ROW + entry(tab, NEAR + u))
+        prods.append(
+            jnp.concatenate(
+                [dot3k(*split(a[row, 0]), *split(t[row])), dot3k(*split(a[row, 1]), *split(t[near]))], axis=1
+            )
+        )
+    tiles = []
+    for u, row, prod in zip(order, rows, prods):
+        smoothed = dot3k(*split(dinv[row]), *split(prod))
+        p0 = t[row] - OMEGA * smoothed[:, :block]
+        p1 = -OMEGA * smoothed[:, block:]
+        tiles.append(two_columns(p0, entry(tab, OWN_LAB + 4 * u)) + two_columns(p1, entry(tab, OWN_LAB + 4 * u + 1)))
+    return tiles
 
 
 def near_sent_kernel(tab, a, t, dinv, near_1):
-    for u in range(near_1.shape[0]):
-        near_1[u] = near_tile(tab, a, t, dinv, u)
+    for u, value in enumerate(near_tiles(tab, a, t, dinv, range(near_1.shape[0]))):
+        near_1[u] = value
 
 
 def wide(ref, *places):
     return jnp.concatenate([ref[place] for place in places], axis=0)
 
 
-def near_rest_kernel(tab, a, t, dinv, near_1, near_0, own, part, a_high, a_low, own_high, own_low):
+def near_rest_kernel(tab, a, t, dinv, near_1, near_0, own, a_high, a_low, a01_high, a01_low):
     width = near_1.shape[0]
-    for u in range(width):
+    for u, value in enumerate(near_tiles(tab, a, t, dinv, range(width, 2 * width))):
         own[u] = near_1[u]
-        own[width + u] = near_tile(tab, a, t, dinv, width + u)
+        own[width + u] = value
     for j in range(width):
         near_0[j] = own[entry(tab, LIST_0 + j)]
     for u in range(2 * width):
-        own_high[u], own_low[u] = split(own[u])
-    for u in range(2 * width):
-        row, near = entry(tab, ROW + u), entry(tab, NEAR + u)
-        a_high[u], a_low[u] = split(jnp.concatenate([a[row, 0], a[row, 1]], axis=1))
-        part[u] = dot3(a_high[u], a_low[u], wide(own_high, u, near), wide(own_low, u, near))
-
-
-def far_blocks(tab, a, dinv, t_high, t_low, u):
-    row = entry(tab, ROW + u)
-    prod = jnp.concatenate(
-        [
-            dot3k(*split(a[row, 2 + which]), t_high[which, pos], t_low[which, pos])
-            for which, pos in ((BELOW, entry(tab, POS2 + u)), (ABOVE, entry(tab, POS3 + u)))
-        ],
-        axis=1,
-    )
-    return -OMEGA * dot3k(*split(dinv[row]), *split(prod))
+        row = entry(tab, ROW + u)
+        a01_high[u], a01_low[u] = split(jnp.concatenate([a[row, 0], a[row, 1]], axis=1))
+        for which in (BELOW, ABOVE):
+            a_high[which, u], a_low[which, u] = split(a[row, 2 + which])
+
+
+def far_blocks(tab, a_high, a_low, dinv, t_high, t_low, order):
+    prods = [
+        jnp.concatenate(
+            [
+                dot3k(a_high[which, u], a_low[which, u], t_high[which, pos], t_low[which, pos])
+                for which, pos in ((BELOW, entry(tab, POS2 + u)), (ABOVE, entry(tab, POS3 + u)))
+            ],
+            axis=1,
+        )
+        for u in order
+    ]
+    return [-OMEGA * dot3k(*split(dinv[entry(tab, ROW + u)]), *split(prod)) for u, prod in zip(order, prods)]
 
 
 def split_both(side, value_0, value_1, high, low):
@@ -188,11 +196,10 @@
         high[1 - side, j], low[1 - side, j] = split(value_1[j])
 
 
-def far_sent_kernel(tab, a, dinv, t_0, t_1, after, far_1, t_high, t_low):
+def far_sent_kernel(tab, a_high, a_low, dinv, t_0, t_1, far_1, t_high, t_low):
     block = dinv.shape[1]
     split_both(pair_side(), t_0, t_1, t_high, t_low)
-    for u in range(far_1.shape[0]):
-        both = far_blocks(tab, a, dinv, t_high, t_low, u)
+    for u, both in enumerate(far_blocks(tab, a_high, a_low, dinv, t_high, t_low, range(far_1.shape[0]))):
         far_1[u, BELOW] = both[:, :block]
         far_1[u, ABOVE] = both[:, block:]
 
@@ -218,41 +225,41 @@
 
 
 def mid_kernel(
-    tab, a, dinv, t_0, t_1, far_1, a01_high, a01_low, near_0,
-    far_0, far, a_high, a_low, trans_high, trans_low, part, ap_high, ap_low, group,
-    t_high, t_low, far_high, far_low, p_high, p_low,
+    tab, a01_high, a01_low, a_high, a_low, dinv, t_high, t_low, far_1, near_0,
+    far_0, far, trans_high, trans_low, part, ap_high, ap_low, group,
+    far_high, far_low, p_high, p_low,
 ):
     rows, block = far.shape[0], far.shape[2]
     width = rows // 2
     side = pair_side()
-    split_both(side, t_0, t_1, t_high, t_low)
-    for u in range(width):
+    for u, both in enumerate(far_blocks(tab, a_high, a_low, dinv, t_high, t_low, range(width, rows))):
         far[u] = far_1[u]
-        both = far_blocks(tab, a, dinv, t_high, t_low, width + u)
         far[width + u, BELOW] = both[:, :block]
         far[width + u, ABOVE] = both[:, block:]
     for j in range(width):
         far_0[j] = far[entry(tab, LIST_0 + j)]
         p_high[j], p_low[j] = split(near_0[j])
     for u in range(rows):
-        row = entry(tab, ROW + u)
         for which in (BELOW, ABOVE):
-            a_high[which, u], a_low[which, u] = split(a[row, 2 + which])
             label = entry(tab, OWN_LAB + 4 * u + 2 + which)
             high, low = split(far[u, which])
             far_high[which, u] = two_columns(high, label)
             far_low[which, u] = two_columns(low, label)
+
+    def mine(u, which):
+        near = entry(tab, NEAR + u)
+        return dot3(a01_high[u], a01_low[u], wide(far_high.at[which], u, near), wide(far_low.at[which], u, near))
+
+    totals = []
+    for u in range(rows):
+        pos = entry(tab, POS2 + 8 * side + u)
+        totals.append(mine(u, side) + dot3k(a_high[side, u], a_low[side, u], p_high[pos], p_low[pos]))
+    for u in range(rows):
+        place = slice(u * block, (u + 1) * block)
+        ap_high[place], ap_low[place] = split(totals[u])
     turn(tab, far, 1 - side, trans_high, trans_low)
     for u in range(rows):
-        near, pos = entry(tab, NEAR + u), entry(tab, POS2 + 8 * side + u)
-        place = slice(u * block, (u + 1) * block)
-        mine = [
-            dot3(a01_high[u], a01_low[u], wide(far_high.at[which], u, near), wide(far_low.at[which], u, near))
-            for which in (side, 1 - side)
-        ]
-        part[u] = mine[1]
-        total = mine[0] + dot3k(a_high[side, u], a_low[side, u], p_high[pos], p_low[pos])
-        ap_high[place], ap_low[place] = split(total)
+        part[u] = mine(u, 1 - side)
     group[...] = coarse_group(trans_high, trans_low, ap_high, ap_low)
 
 
@@ -267,11 +274,13 @@
     out_1[:, :half] = group[...]
     for j in range(rows // 2):
         p_high[j], p_low[j] = split(near_1[j])
+    totals = []
     for u in range(rows):
         pos = entry(tab, POS2 + 8 * side + u)
+        totals.append(part[u] + dot3k(a_high[side, u], a_low[side, u], p_high[pos], p_low[pos]))
+    for u in range(rows):
         place = slice(u * block, (u + 1) * block)
-        total = part[u] + dot3k(a_high[side, u], a_low[side, u], p_high[pos], p_low[pos])
-        ap_high[place], ap_low[place] = split(total)
+        ap_high[place], ap_low[place] = split(totals[u])
     out_1[:, half:] = coarse_group(trans_high, trans_low, ap_high, ap_low)
 
 
@@ -282,29 +291,37 @@
         p_high[j, :, block:], p_low[j, :, block:] = split(far_in[j, side])
 
 
-def far_columns(tab, side, u, a_high, a_low, p_high, p_low):
-    block = a_high.shape[3]
-    pos = entry(tab, POS2 + 8 * side + u)
-    value = dot3k(a_high[side, u], a_low[side, u], p_high[pos], p_low[pos])
-    labels = SIDE_LAB + 8 * side + 2 * pos
-    here = two_columns(value[:, :block], entry(tab, labels + 1 - side))
-    high, low = split(value[:, block:])
-    label = entry(tab, labels + side)
-    return here, two_columns(high, label), two_columns(low, label)
+def far_columns(tab, side, a_high, a_low, p_high, p_low, ap_high, ap_low):
+    rows, block = a_high.shape[1], a_high.shape[3]
+    values, here = [], []
+    for u in range(rows):
+        pos = entry(tab, POS2 + 8 * side + u)
+        values.append(dot3k(a_high[side, u], a_low[side, u], p_high[pos], p_low[pos]))
+    for u in range(rows):
+        labels = SIDE_LAB + 8 * side + 2 * entry(tab, POS2 + 8 * side + u)
+        here.append(two_columns(values[u][:, :block], entry(tab, labels + 1 - side)))
+        high, low = split(values[u][:, block:])
+        label = entry(tab, labels + side)
+        place = slice(u * block, (u + 1) * block)
+        ap_high[place] = two_columns(high, label)
+        ap_low[place] = two_columns(low, label)
+    return here
 
 
 def second_pre_kernel(
-    tab, a_high, a_low, part, trans_high, trans_low, far_0, after,
+    tab, a01_high, a01_low, a_high, a_low, own, trans_high, trans_low, far_0, after,
     own_part, ap_high, ap_low, group,
-    p_high, p_low,
+    p_high, p_low, own_high, own_low,
 ):
-    rows, block = part.shape[0], part.shape[1]
+    rows = own.shape[0]
     side = pair_side()
     take_far(side, far_0, p_high, p_low)
     for u in range(rows):
-        place = slice(u * block, (u + 1) * block)
-        here, ap_high[place], ap_low[place] = far_columns(tab, side, u, a_high, a_low, p_high, p_low)
-        own_part[u] = part[u] + here
+        own_high[u], own_low[u] = split(own[u])
+    here = far_columns(tab, side, a_high, a_low, p_high, p_low, ap_high, ap_low)
+    for u in range(rows):
+        near = entry(tab, NEAR + u)
+        own_part[u] = here[u] + dot3(a01_high[u], a01_low[u], wide(own_high, u, near), wide(own_low, u, near))
     group[...] = coarse_group(trans_high, trans_low, ap_high, ap_low)
 
 
@@ -318,10 +335,10 @@
     side = 1 - pair_side()
     out_1[:, :half] = group[...]
     take_far(side, far_1, p_high, p_low)
+    here = far_columns(tab, side, a_high, a_low, p_high, p_low, ap_high, ap_low)
     for u in range(rows):
         place = slice(u * block, (u + 1) * block)
-        here, ap_high[place], ap_low[place] = far_columns(tab, side, u, a_high, a_low, p_high, p_low)
-        own_high[place], own_low[place] = split(own_part[u] + here)
+        own_high[place], own_low[place] = split(own_part[u] + here[u])
     out_1[:, half : 2 * half] = coarse_group(trans_high, trans_low, own_high, own_low)
     out_1[:, 2 * half :] = coarse_group(trans_high, trans_low, ap_high, ap_low)
 
@@ -349,14 +366,18 @@
     every_group(trans_high, trans_low, aps, out)
 
 
-def write_slots(inv, total, result, agg, d, out, sem):
-    block = total.shape[0]
-    value = dot3k(*inv, *split(total))
-    result[0] = value[:, :block]
-    result[1] = value[:, block:]
-    copy = pltpu.make_async_copy(result, out.at[agg, pl.ds(2 * (d + 3), 2)], sem)
-    copy.start()
-    return copy
+def write_slots(inverse, totals, results, out, sems):
+    block = inverse.shape[1]
+    inv = [split(inverse[agg]) for agg in range(2)]
+    values = [dot3k(*inv[agg], *split(total)) for agg, _, total in totals]
+    copies = []
+    for n, ((agg, d, _), value) in enumerate(zip(totals, values)):
+        results[n, 0] = value[:, :block]
+        results[n, 1] = value[:, block:]
+        copies.append(pltpu.make_async_copy(results.at[n], out.at[agg, pl.ds(2 * (d + 3), 2)], sems.at[n]))
+        copies[-1].start()
+    for copy in copies:
+        copy.wait()
 
 
 OWN_AT, SAME_AT, OTHER_AT = (1, -1, 2, 0, -2), (0, 2, -1, 1, 3), (-2, 0, -3, -1, 1)
@@ -373,9 +394,8 @@
     half = 2 * block
 
     def run(way):
-        copies = []
+        done = []
         for agg in range(2):
-            inv = split(inverse[agg])
             line = slice(agg * block, (agg + 1) * block)
             for d in range(-3, 4):
                 places = [(ref, at.index(d)) for ref, at in ((own, OWN_AT), (both_0, SAME_AT), (first_1, OTHER_AT[:2])) if d in at]
@@ -384,10 +404,8 @@
                 if d in OTHER_AT[2:]:
                     waiting[agg, OTHER_AT.index(d) - 2] = total
                 else:
-                    n = len(copies)
-                    copies.append(write_slots(inv, total, results.at[n], agg, way * d, out, sems.at[n]))
-        for copy in copies:
-            copy.wait()
+                    done.append((agg, way * d, total))
+        write_slots(inverse, done, results, out, sems)
 
     both_ways(run)
 
@@ -397,16 +415,13 @@
     half = 2 * block
 
     def run(way):
-        copies = []
+        done = []
         for agg in range(2):
-            inv = split(inverse[agg])
             line = slice(agg * block, (agg + 1) * block)
             for i in range(3):
                 total = waiting[agg, i] + second_1[line, i * half : (i + 1) * half]
-                n = len(copies)
-                copies.append(write_slots(inv, total, results.at[n], agg, way * OTHER_AT[2 + i], out, sems.at[n]))
-        for copy in copies:
-            copy.wait()
+                done.append((agg, way * OTHER_AT[2 + i], total))
+        write_slots(inverse, done, results, out, sems)
 
     both_ways(run)
 
@@ -459,27 +474,27 @@
     t_0 = exchanged(t_0, 0)
     (near_1,) = call(near_sent_kernel, [tile], [tab, a, t, dinv], micros=2)
     got_near_1 = exchanged(near_1, 1)
-    near_0, own, part_own, a01_high, a01_low = call(
+    near_0, own, a23_high, a23_low, a01_high, a01_low = call(
         near_rest_kernel,
-        [tile] + [full(rows, block, half)] * 2 + pair(rows, block, half),
+        [tile, full(rows, block, half)] + pair(2, rows, block, block) + pair(rows, block, half),
         [tab, a, t, dinv, near_1],
-        two(rows, block, half),
         micros=2,
     )
     near_0, near_1 = exchanged(near_0, 0), got_near_1
     sent = full(width, 2, block, block)
-    (far_1,) = call(far_sent_kernel, [sent], [tab, a, dinv, t_0, t_1, own], two(2, width, block, block), micros=2)
+    far_1, t_high, t_low = call(
+        far_sent_kernel, [sent] + pair(2, width, block, block), [tab, a23_high, a23_low, dinv, t_0, t_1], micros=2
+    )
     got_far_1 = exchanged(far_1, 1)
-    far_0, far, a23_high, a23_low, out_high, out_low, part, ap_e1_high, ap_e1_low, group = call(
+    far_0, far, out_high, out_low, part, ap_e1_high, ap_e1_low, group = call(
         mid_kernel,
         [sent, full(rows, 2, block, block)]
-        + pair(2, rows, block, block)
         + pair(half, deep)
         + [full(rows, block, half)]
         + pair(deep, half)
         + [full(half, half)],
-        [tab, a, dinv, t_0, t_1, far_1, a01_high, a01_low, near_0],
-        two(2, width, block, block) + two(2, rows, block, half) + two(width, block, half),
+        [tab, a01_high, a01_low, a23_high, a23_low, dinv, t_high, t_low, far_1, near_0],
+        two(2, rows, block, half) + two(width, block, half),
         micros=3,
     )
     far_0, far_1 = exchanged(far_0, 0), got_far_1
@@ -494,8 +509,8 @@
     part_own, ap_e2_high, ap_e2_low, group = call(
         second_pre_kernel,
         [full(rows, block, half)] + pair(deep, half) + [full(half, half)],
-        [tab, a23_high, a23_low, part_own, out_high, out_low, far_0, ap_o1_high],
-        two(width, block, half),
+        [tab, a01_high, a01_low, a23_high, a23_low, own, out_high, out_low, far_0, ap_o1_high],
+        two(width, block, half) + two(rows, block, half),
         micros=2,
     )
     ap_own_high, ap_own_low, ap_o2_high, ap_o2_low, second_1 = call(

time: 66.6 us -> 64.1 us (0.962)
  Pallas kernels: 20.1 us -> 18.2 us
    pallas_call x12, Pallas kernels: 20.1 us -> 18.2 us  [call(): pl.pallas_call(body, out_shape=outs, in_specs=specs(ins, in_hbm), out_spe...]
where the time goes in v7:
time: 64.1 us; the launch traced here: 64 us
  starting transfers between devices  24.1 us (38%)
  waiting for transfers between devices  21.1 us (33%)
  Pallas kernels  18.2 us (28%)
    ppermute x9, starting transfers between devices, exchanged(): return lax.ppermute(value, AXES, pairs)  24.1 us
    ppermute x9, waiting for transfers between devices, exchanged(): return lax.ppermute(value, AXES, pairs)  21.1 us
    pallas_call x12, Pallas kernels, call(): pl.pallas_call(body, out_shape=outs, in_specs=specs(ins, in_hbm), out_spe...  18.2 us
  transfers between devices with their start and end apart: 9, of which 3 were waited for; matrix products, arithmetic and copies ran while one was open for 0% of the time, Pallas kernels for 16%

profile of v7, /device:TPU:0, one launch (start us, length us, event | category | flops | bytes accessed | tf_op | source)
XLA Modules:
  0.0 64.0 jit_solution(4802859744362555209)
XLA Ops:
  0.0 1.5 %shard_map.64 = (s32[88,128]{1,0:T(8,128)S(1)}, f32[4,128,128]{2,1,0:T(8,128)S(1)}, f32[4,128,128]{2,1,0:T(8,128)S(1)}, f32[8,128,128]{2,1,0:T(8,128)S(1)}) custom-call(s32[4096]{0:T(1024)} %bitcast.5, s32[1024]{0:T(1024)} %agg_hbm.1, f32[8,128,128]{2,1,0:T(8,128)} %t_hbm.1), custom_call_target="tpu_custom_call" | custom-call | flops 3000000000 | bytes 1048576 | tf_op jit(solution)/shard_map/pallas_call | solution.py:437
  1.5 0.3 copy-done.1
  1.7 0.1 copy-done.2
  1.8 0.6 %shard_map.65.near_1 = f32[4,128,256]{2,1,0:T(8,128)S(1)} custom-call(s32[88,128]{1,0:T(8,128)S(1)} %get-tuple-element.40.tab, f32[8,4,128,128]{3,2,1,0:T(8,128)S(1)} %copy-done.1, f32[8,128,128]{2,1,0:T(8,128)S(1)} %get-tuple-element.41.t, f32[8,128,128]{2,1,0:T(8,128)S(1)} %copy-done.2), custom_call_target="tpu_custom_call" | custom-call | flops 2000000000 | bytes 1048576 | tf_op jit(solution)/shard_map/pallas_call | solution.py:437
  2.5 0.9 %shard_map.66 = (f32[4,128,256]{2,1,0:T(8,128)S(1)}, f32[8,128,256]{2,1,0:T(8,128)S(1)}, bf16[2,8,128,128]{3,2,1,0:T(8,128)(2,1)S(1)}, bf16[2,8,128,128]{3,2,1,0...) custom-call(s32[88,128]{1,0:T(8,128)S(1)} %get-tuple-element.40.tab, ...), custom_call_target="tpu_custom_call" | custom-call | flops 2000000000 | bytes 1048576 | tf_op jit(solution)/shard_map/pallas_call | solution.py:437
  3.4 0.1 collective-permute-start.2
  3.5 0.5 collective-permute-start
  4.0 8.5 %collective-permute-start.1 = (f32[4,128,128]{2,1,0:T(8,128)S(1)}, f32[4,128,128]{2,1,0:T(8,128)S(1)}, u32[]{:S(2)}, u32[]{:S(2)}) collective-permute-start(f32[4,128,128]{2,1,0:T(8,128)S(1)} %get-tuple-element.48), channel_id=1, source_target_pairs={{1,2},{2,1},{3,4},{4,3},{5,6},{6,5},{7,8},{8,7},{9,10},{10,9},{11,... | collective-permute-start | bytes 786440 | tf_op jit(solution)/shard_map/ppermute | solution.py:27
  12.5 0.0 collective-permute-start.3
  12.5 0.0 collective-permute-done.t_0
  12.5 4.0 %collective-permute-done.1.t_1 = f32[4,128,128]{2,1,0:T(8,128)S(1)} collective-permute-done((f32[4,128,128]{2,1,0:T(8,128)S(1)}, f32[4,128,128]{2,1,0:T(8,128)S(1)}, u32[]{:S(2)}, u32[]{:S(2)}) %collective-permute-start.1) | collective-permute-done | bytes 262176 | tf_op jit(solution)/shard_map/ppermute | solution.py:27
  16.5 0.6 shard_map.67
  17.2 0.0 collective-permute-done.2.near_0
  17.2 2.9 %shard_map.68 = (f32[4,2,128,128]{3,2,1,0:T(8,128)S(1)}, f32[8,2,128,128]{3,2,1,0:T(8,128)S(1)}, bf16[256,1024]{1,0:T(8,128)(2,1)S(1)}, bf16[256,1024]{1,0:T(8,1...) custom-call(s32[88,128]{1,0:T(8,128)S(1)} %get-tuple-element.40.tab,, ...), custom_call_target="tpu_custom_call" | custom-call | flops 3000000000 | bytes 1048576 | tf_op jit(solution)/shard_map/pallas_call | solution.py:437
  20.1 0.1 collective-permute-start.4
  20.2 7.3 %collective-permute-start.5 = (f32[4,2,128,128]{3,2,1,0:T(8,128)S(1)}, f32[4,2,128,128]{3,2,1,0:T(8,128)S(1)}, u32[]{:S(2)}, u32[]{:S(2)}) collective-permute-start(f32[4,2,128,128]{3,2,1,0:T(8,128)S(1)} %get-tuple-element.51.far_1), channel_id=1, source_target_pairs={{1,2},{2,1},{3,4},{4,3},{5,6},{6,5},{7,8},{8,7},{9,10},{10,9},{11,... | collective-permute-start | bytes 1572872 | tf_op jit(solution)/shard_map/ppermute | solution.py:27
  27.5 0.0 collective-permute-done.3.near_1
  27.5 1.0 %shard_map.69 = (bf16[1024,256]{1,0:T(8,128)(2,1)S(1)}, bf16[1024,256]{1,0:T(8,128)(2,1)S(1)}, f32[256,512]{1,0:T(8,128)S(1)}) custom-call(s32[88,128]{1,0:T(8,128)S(1)} %get-tuple-element.40.tab, bf16[2,8,128,128]{3,2,1,0:T(8,128)(2,1)S(1)} %get-tuple-element.45.a_high, bf16[2,8,128,128]{3,2,1,0:T(8,128)(2,1)S(1)} %get-tuple-element.46.a_low, ...), custom_call_target="tpu_custom_call" | custom-call | flops 2000000000 | bytes 1048576 | tf_op jit(solution)/shard_map/pallas_call | solution.py:437
  28.5 0.0 collective-permute-done.4.far_0
  28.5 1.6 %shard_map.70 = (f32[8,128,256]{2,1,0:T(8,128)S(1)}, bf16[1024,256]{1,0:T(8,128)(2,1)S(1)}, bf16[1024,256]{1,0:T(8,128)(2,1)S(1)}, f32[256,256]{1,0:T(8,128)S(1)}) custom-call(s32[88,128]{1,0:T(8,128)S(1)} %get-tuple-element.40.tab, bf16[8,128,256]{2,1,0:T(8,128)(2,1)S(1)} %get-tuple-element.43.a01_high, bf16[8,128,256]{2,1,0:T(8,128)(2,1)S(1)} %get-tuple-element.44.a01_low, ...), custom_call_target="tpu_custom_call" | custom-call | flops 2000000000 | bytes 1048576 | tf_op jit(solution)/shard_map/pallas_call | solution.py:437
  30.2 4.2 %collective-permute-done.5.far_1 = f32[4,2,128,128]{3,2,1,0:T(8,128)S(1)} collective-permute-done((f32[4,2,128,128]{3,2,1,0:T(8,128)S(1)}, f32[4,2,128,128]{3,2,1,0:T(8,128)S(1)}, u32[]{:S(2)}, u32[]{:S(2)}) %collective-permute-start.5) | collective-permute-done | bytes 524320 | tf_op jit(solution)/shard_map/ppermute | solution.py:27
  34.4 1.5 %shard_map.71 = (bf16[1024,256]{1,0:T(8,128)(2,1)S(1)}, bf16[1024,256]{1,0:T(8,128)(2,1)S(1)}, bf16[1024,256]{1,0:T(8,128)(2,1)S(1)}, bf16[1024,256]{1,0:T(8,128)(2,1)S(1)}, f32[256,768]{1,0:T(8,128)S(1)}) custom-call(s32[88,128]{1,0:T(8,128)S(1)} %get-tuple-element.40.tab, bf16[2,8,128,128]{3,2,1,0:T(8,128)(2,1)S(1)} %get-tuple-element.45.a_high, ...), custom_call_target="tpu_custom_call" | custom-call | flops 2000000000 | bytes 1048576 | tf_op jit(solution)/shard_map/pallas_call | solution.py:437
  35.9 2.5 %shard_map.73 = f32[256,1280]{1,0:T(8,128)S(1)} custom-call(s32[88,128]{1,0:T(8,128)S(1)} %get-tuple-element.40.tab, f32[8,2,128,128]{3,2,1,0:T(8,128)S(1)} %get-tuple-element.70.far, bf16[1024,256]{1,0:T(8,128)(2,1)S(1)} %get-tuple-element.53.refs_0_, bf16[1024,256]{1,0:T(8,128)(2,1)S(1)} %get-tuple-element.54.refs_1_, ...), custom_call_target="tpu_custom_call" | custom-call | flops 2000000000 | bytes 1048576 | tf_op jit(solution)/shard_map/pallas_call | solution.py:437
  38.4 0.3 collective-permute-start.6
  38.7 7.2 %collective-permute-start.8 = (f32[256,768]{1,0:T(8,128)S(1)}, f32[256,768]{1,0:T(8,128)S(1)}, u32[]{:S(2)}, u32[]{:S(2)}) collective-permute-start(f32[256,768]{1,0:T(8,128)S(1)} %get-tuple-element.73), channel_id=1, source_target_pairs={{1,2},{2,1},{3,4},{4,3},{5,6},{6,5},{7,8},{8,7},{9,10},{10,9},{11,... | collective-permute-start | bytes 2359304 | tf_op jit(solution)/shard_map/ppermute | solution.py:27
  46.0 0.1 collective-permute-start.7
  46.1 2.3 %shard_map.72.own = f32[256,1280]{1,0:T(8,128)S(1)} custom-call(f32[8,128,256]{2,1,0:T(8,128)S(1)} %get-tuple-element.42.own, bf16[1024,256]{1,0:T(8,128)(2,1)S(1)} %get-tuple-element.53.refs_0_, bf16[1024,256]{1,0:T(8,128)(2,1)S(1)} %get-tuple-element.54.refs_1_, bf16[1024,256]{1,0:T(8,128)(2,1)S(1)} %get-tuple-element.59.after.refs_2_, ...), custom_call_target="tpu_custom_call" | custom-call | flops 2000000000 | bytes 1048576 | tf_op jit(solution)/shard_map/pallas_call | solution.py:437
  48.4 12.8 %collective-permute-done.7.first_1 = f32[256,512]{1,0:T(8,128)S(1)} collective-permute-done((f32[256,512]{1,0:T(8,128)S(1)}, f32[256,512]{1,0:T(8,128)S(1)}, u32[]{:S(2)}, u32[]{:S(2)}) %collective-permute-start.7) | collective-permute-done | bytes 524320 | tf_op jit(solution)/shard_map/ppermute | solution.py:27
  61.2 0.0 collective-permute-done.6.both_0
  61.3 1.4 %shard_map.74 = (f32[2,14,128,128]{3,2,1,0:T(8,128)}, f32[2,3,128,256]{3,2,1,0:T(8,128)S(1)}) custom-call(f32[2,128,128]{2,1,0:T(8,128)S(1)} %copy-done, f32[256,1280]{1,0:T(8,128)S(1)} %shard_map.72.own, f32[256,1280]{1,0:T(8,128)S(1)} %collective-permute-done.6.both_0, f32[256,512]{1,0:T(8,128)S(1)} %collective-permute-done.7.first_1), custom_call_target="tpu_custom_call" | custom-call | flops 2000000000 | bytes 1048576 | tf_op jit(solution)/shard_map/pallas_call | solution.py:437
  62.6 0.0 collective-permute-done.8.second_1
  62.6 1.2 %shard_map.75 = f32[2,14,128,128]{3,2,1,0:T(8,128)} custom-call(f32[2,128,128]{2,1,0:T(8,128)S(1)} %copy-done, f32[2,3,128,256]{3,2,1,0:T(8,128)S(1)} %get-tuple-element.72.waiting, f32[256,768]{1,0:T(8,128)S(1)} %collective-permute-done.8.second_1, f32[2,14,128,128]{3,2,1,0:T(8,128)} %get-tuple-element.74.partly), custom_call_target="tpu_custom_call", output_to_operand_aliasing={{}: (3, {})} | custom-call | flops 1000000000 | bytes 1048576 | tf_op jit(solution)/shard_map/pallas_call | solution.py:437
  (4 shorter events, 0.0 us)
Async XLA Ops:
  0.0 1.7 %copy-start.1 = (f32[8,4,128,128]{3,2,1,0:T(8,128)S(1)}, f32[8,4,128,128]{3,2,1,0:T(8,128)}, u32[]{:S(2)}) copy-start(f32[8,4,128,128]{3,2,1,0:T(8,128)} %a.3) | copy-start | bytes 6291460
  0.0 1.8 %copy-start.2 = (f32[8,128,128]{2,1,0:T(8,128)S(1)}, f32[8,128,128]{2,1,0:T(8,128)}, u32[]{:S(2)}) copy-start(f32[8,128,128]{2,1,0:T(8,128)} %dinv.7) | copy-start | bytes 1572868
  3.4 13.8 %collective-permute-start.2 = (f32[4,128,256]{2,1,0:T(8,128)S(1)}, f32[4,128,256]{2,1,0:T(8,128)S(1)}, u32[]{:S(2)}, u32[]{:S(2)}) collective-permute-start(f32[4,128,256]{2,1,0:T(8,128)S(1)} %get-tuple-element.52), channel_id=1, source_target_pairs={{0,1},{1,0},{2,3},{3,2},{4,5},{5,4},{6,7},{7,6},{8,9},{9,8},{10,11... | collective-permute-start | bytes 1572872 | tf_op jit(solution)/shard_map/ppermute | solution.py:27
  3.5 9.0 %collective-permute-start = (f32[4,128,128]{2,1,0:T(8,128)S(1)}, f32[4,128,128]{2,1,0:T(8,128)S(1)}, u32[]{:S(2)}, u32[]{:S(2)}) collective-permute-start(f32[4,128,128]{2,1,0:T(8,128)S(1)} %get-tuple-element.47), channel_id=1, source_target_pairs={{0,1},{1,0},{2,3},{3,2},{4,5},{5,4},{6,7},{7,6},{8,9},{9,8},{10,11... | collective-permute-start | bytes 786440 | tf_op jit(solution)/shard_map/ppermute | solution.py:27
  4.0 12.5 %collective-permute-start.1 = (f32[4,128,128]{2,1,0:T(8,128)S(1)}, f32[4,128,128]{2,1,0:T(8,128)S(1)}, u32[]{:S(2)}, u32[]{:S(2)}) collective-permute-start(f32[4,128,128]{2,1,0:T(8,128)S(1)} %get-tuple-element.48), channel_id=1, source_target_pairs={{1,2},{2,1},{3,4},{4,3},{5,6},{6,5},{7,8},{8,7},{9,10},{10,9},{11,... | collective-permute-start | bytes 786440 | tf_op jit(solution)/shard_map/ppermute | solution.py:27
  12.5 15.0 %collective-permute-start.3 = (f32[4,128,256]{2,1,0:T(8,128)S(1)}, f32[4,128,256]{2,1,0:T(8,128)S(1)}, u32[]{:S(2)}, u32[]{:S(2)}) collective-permute-start(f32[4,128,256]{2,1,0:T(8,128)S(1)} %shard_map.65.near_1), channel_id=1, source_target_pairs={{1,2},{2,1},{3,4},{4,3},{5,6},{6,5},{7,8},{8,7},{9,10},{10,9},{11,... | collective-permute-start | bytes 1572872 | tf_op jit(solution)/shard_map/ppermute | solution.py:27
  20.1 8.4 %collective-permute-start.4 = (f32[4,2,128,128]{3,2,1,0:T(8,128)S(1)}, f32[4,2,128,128]{3,2,1,0:T(8,128)S(1)}, u32[]{:S(2)}, u32[]{:S(2)}) collective-permute-start(f32[4,2,128,128]{3,2,1,0:T(8,128)S(1)} %get-tuple-element.61), channel_id=1, source_target_pairs={{0,1},{1,0},{2,3},{3,2},{4,5},{5,4},{6,7},{7,6},{8,9},{9,8},{10,11... | collective-permute-start | bytes 1572872 | tf_op jit(solution)/shard_map/ppermute | solution.py:27
  20.2 14.1 %collective-permute-start.5 = (f32[4,2,128,128]{3,2,1,0:T(8,128)S(1)}, f32[4,2,128,128]{3,2,1,0:T(8,128)S(1)}, u32[]{:S(2)}, u32[]{:S(2)}) collective-permute-start(f32[4,2,128,128]{3,2,1,0:T(8,128)S(1)} %get-tuple-element.51.far_1), channel_id=1, source_target_pairs={{1,2},{2,1},{3,4},{4,3},{5,6},{6,5},{7,8},{8,7},{9,10},{10,9},{11,... | collective-permute-start | bytes 1572872 | tf_op jit(solution)/shard_map/ppermute | solution.py:27
  38.4 22.8 %collective-permute-start.6 = (f32[256,1280]{1,0:T(8,128)S(1)}, f32[256,1280]{1,0:T(8,128)S(1)}, u32[]{:S(2)}, u32[]{:S(2)}) collective-permute-start(f32[256,1280]{1,0:T(8,128)S(1)} %shard_map.73), channel_id=1, source_target_pairs={{0,1},{1,0},{2,3},{3,2},{4,5},{5,4},{6,7},{7,6},{8,9},{9,8},{10,11... | collective-permute-start | bytes 3932168 | tf_op jit(solution)/shard_map/ppermute | solution.py:27
  38.7 23.9 %collective-permute-start.8 = (f32[256,768]{1,0:T(8,128)S(1)}, f32[256,768]{1,0:T(8,128)S(1)}, u32[]{:S(2)}, u32[]{:S(2)}) collective-permute-start(f32[256,768]{1,0:T(8,128)S(1)} %get-tuple-element.73), channel_id=1, source_target_pairs={{1,2},{2,1},{3,4},{4,3},{5,6},{6,5},{7,8},{8,7},{9,10},{10,9},{11,... | collective-permute-start | bytes 2359304 | tf_op jit(solution)/shard_map/ppermute | solution.py:27
  46.0 15.3 %copy-start = (f32[2,128,128]{2,1,0:T(8,128)S(1)}, f32[2,128,128]{2,1,0:T(8,128)}, u32[]{:S(2)}) copy-start(f32[2,128,128]{2,1,0:T(8,128)} %inverse.3) | copy-start | bytes 393220
  46.0 15.3 %collective-permute-start.7 = (f32[256,512]{1,0:T(8,128)S(1)}, f32[256,512]{1,0:T(8,128)S(1)}, u32[]{:S(2)}, u32[]{:S(2)}) collective-permute-start(f32[256,512]{1,0:T(8,128)S(1)} %get-tuple-element.71), channel_id=1, source_target_pairs={{1,2},{2,1},{3,4},{4,3},{5,6},{6,5},{7,8},{8,7},{9,10},{10,9},{11,... | collective-permute-start | bytes 1572872 | tf_op jit(solution)/shard_map/ppermute | solution.py:27
